TPU v7x, 32 devices: a whole 2x2x4 slice. The times are simulated.
32 devices in a mesh: shard: 4 (over x, core), rep: 8 (over z, y).
Axes of the slice: x: 2, y: 2, z: 4, core: 2. Of those that a mesh axis runs over, the one named last changes fastest.
Arguments:
- block_input: bfloat16 [1536, 49, 512], P(('shard', 'rep')), may hold values from -6 to 6
- out_grad: bfloat16 [1536, 49, 512], P(('shard', 'rep')), may hold values from -6 to 6
- qkv_weight: bfloat16 [512, 1536], P('shard'), may hold values from -0.25 to 0.25
- query_bias: float32 [512], replicated, may hold values from -3 to 3
- value_bias: float32 [512], replicated, may hold values from -3 to 3
- proj_weight: bfloat16 [512, 512], P('shard'), may hold values from -0.75 to 0.75
- proj_bias: float32 [512], replicated, may hold values from -3 to 3
- hidden_weight: bfloat16 [512, 2048], P('shard'), may hold values from -0.25 to 0.25
- hidden_bias: float32 [2048], replicated, may hold values from -3 to 3
- output_weight: bfloat16 [2048, 512], P('shard'), may hold values from -0.125 to 0.125
- output_bias: float32 [512], replicated, may hold values from -3 to 3
- first_gain: float32 [512], replicated, may hold values from 0.25 to 1.75
- first_shift: float32 [512], replicated, may hold values from -3 to 3
- second_gain: float32 [512], replicated, may hold values from 0.25 to 1.75
- second_shift: float32 [512], replicated, may hold values from -3 to 3
- bias_table: float32 [169, 16], replicated, may hold values from -2.5 to 303
- table_index: int32 [49, 49], replicated, may hold values from 0 to 168, as said below
Outputs:
- block_output: bfloat16 [1536, 49, 512], P(('shard', 'rep'))
- input_grad: float32 [1536, 49, 512], P(('shard', 'rep'))
- qkv_weight_grad: float32 [512, 1536], P('shard')
- query_bias_grad: float32 [512], replicated
- value_bias_grad: float32 [512], replicated
- proj_weight_grad: float32 [512, 512], P('shard')
- proj_bias_grad: float32 [512], replicated
- hidden_weight_grad: float32 [512, 2048], P('shard')
- hidden_bias_grad: float32 [2048], replicated
- output_weight_grad: float32 [2048, 512], P('shard')
- output_bias_grad: float32 [512], replicated
- first_gain_grad: float32 [512], replicated
- first_shift_grad: float32 [512], replicated
- second_gain_grad: float32 [512], replicated
- second_shift_grad: float32 [512], replicated
- bias_table_grad: float32 [169, 16], replicated
Inputs may be any that keep to these rules, and one draw needn't show every extreme that they name: `table_index`: every one of the 169 table rows is named by some pair.
All inputs are finite; a program needn't handle non-finite values.
Results may differ from a plain program's by a relative error of at most 0.017.
Values may be sent and summed in bfloat16 or wider, within the bound.
A program may use at most 320 MiB of HBM per device.

v0:
```python
import jax
import jax.numpy as jnp
from jax import lax
from jax.sharding import PartitionSpec as P

epsilon = 1e-05


def layer_norm(values, gain, shift):
    center = values - jnp.mean(values, axis=-1, keepdims=True)
    inverse = lax.rsqrt(jnp.mean(center * center, axis=-1, keepdims=True) + epsilon)
    normal = center * inverse
    return (normal * gain + shift, normal, inverse)


def norm_back(grad, normal, inverse, gain):
    scaled = grad * gain
    back = inverse * (
        scaled
        - jnp.mean(scaled, axis=-1, keepdims=True)
        - normal * jnp.mean(scaled * normal, axis=-1, keepdims=True)
    )
    return (back, jnp.sum(grad * normal, axis=0), jnp.sum(grad, axis=0))


def gelu_value(upper):
    return 0.5 * upper * (1.0 + lax.erf(upper * 0.7071067811865476))


def gelu_slope(upper):
    return (
        0.5 * (1.0 + lax.erf(upper * 0.7071067811865476))
        + upper * jnp.exp(-0.5 * upper * upper) * 0.3989422804014327
    )


def window_scores(query, keys, table_bias):
    return (
        jnp.einsum("wqhd,wkhd->whqk", query, keys, preferred_element_type=jnp.float32)
        + table_bias[None]
    )


def on_device(
    block_input,
    out_grad,
    qkv_weight,
    query_bias,
    value_bias,
    proj_weight,
    proj_bias,
    hidden_weight,
    hidden_bias,
    output_weight,
    output_bias,
    first_gain,
    first_shift,
    second_gain,
    second_shift,
    bias_table,
    table_index,
):
    windows, tokens, width = block_input.shape
    heads = bias_table.shape[1]
    head_size = width // heads
    scale = head_size ** (-0.5)
    table_rows = bias_table.shape[0]
    pairs = tokens * tokens
    one_hot = (
        table_index.reshape(pairs, 1) == lax.broadcasted_iota(jnp.int32, (pairs, table_rows), 1)
    ).astype(jnp.float32)
    table_bias = jnp.dot(one_hot, bias_table, precision=lax.Precision.HIGHEST).T.reshape(
        heads, tokens, tokens
    )
    split_shape = (windows, tokens, heads, head_size)
    qkv_full, proj_full = (
        lax.all_gather(qkv_weight, "shard", axis=0, tiled=True),
        lax.all_gather(proj_weight, "shard", axis=0, tiled=True),
    )
    flat_input = block_input.reshape(-1, width).astype(jnp.float32)
    normed1, normal1, inverse1 = layer_norm(flat_input, first_gain, first_shift)
    first_act = normed1.astype(jnp.bfloat16)
    projected = jnp.dot(first_act, qkv_full, preferred_element_type=jnp.float32)
    query = ((projected[:, :width] + query_bias) * scale).astype(jnp.bfloat16).reshape(split_shape)
    keys = projected[:, width : 2 * width].astype(jnp.bfloat16).reshape(split_shape)
    values = (projected[:, 2 * width :] + value_bias).astype(jnp.bfloat16).reshape(split_shape)
    scores = window_scores(query, keys, table_bias)
    top = jnp.max(scores, axis=-1, keepdims=True)
    logsum = top + jnp.log(jnp.sum(jnp.exp(scores - top), axis=-1, keepdims=True))
    prob_half = jnp.exp(scores - logsum).astype(jnp.bfloat16)
    mixed = (
        jnp.einsum("whqk,wkhd->wqhd", prob_half, values, preferred_element_type=jnp.float32)
        .astype(jnp.bfloat16)
        .reshape(-1, width)
    )
    residual = (
        flat_input + jnp.dot(mixed, proj_full, preferred_element_type=jnp.float32) + proj_bias
    )
    hidden_full, output_full = (
        lax.all_gather(hidden_weight, "shard", axis=0, tiled=True),
        lax.all_gather(output_weight, "shard", axis=0, tiled=True),
    )
    normed2, normal2, inverse2 = layer_norm(residual, second_gain, second_shift)
    second_act = normed2.astype(jnp.bfloat16)
    upper = jnp.dot(second_act, hidden_full, preferred_element_type=jnp.float32) + hidden_bias
    activated = gelu_value(upper).astype(jnp.bfloat16)
    block_output = (
        residual + jnp.dot(activated, output_full, preferred_element_type=jnp.float32) + output_bias
    ).astype(jnp.bfloat16)
    hidden_back, output_back = (
        lax.all_gather(hidden_weight, "shard", axis=0, tiled=True),
        lax.all_gather(output_weight, "shard", axis=0, tiled=True),
    )
    flat_cot = out_grad.reshape(-1, width)
    cot_wide = flat_cot.astype(jnp.float32)
    output_weight_grad = jnp.dot(activated.T, flat_cot, preferred_element_type=jnp.float32)
    output_bias_grad = jnp.sum(cot_wide, axis=0)
    upper_grad = (
        jnp.dot(flat_cot, output_back.T, preferred_element_type=jnp.float32) * gelu_slope(upper)
    ).astype(jnp.bfloat16)
    hidden_weight_grad = jnp.dot(second_act.T, upper_grad, preferred_element_type=jnp.float32)
    hidden_bias_grad = jnp.sum(upper_grad.astype(jnp.float32), axis=0)
    second_grad = jnp.dot(upper_grad, hidden_back.T, preferred_element_type=jnp.float32)
    second_back, second_gain_grad, second_shift_grad = norm_back(
        second_grad, normal2, inverse2, second_gain
    )
    residual_grad = cot_wide + second_back
    residual_half = residual_grad.astype(jnp.bfloat16)
    qkv_back, proj_back = (
        lax.all_gather(qkv_weight, "shard", axis=0, tiled=True),
        lax.all_gather(proj_weight, "shard", axis=0, tiled=True),
    )
    proj_weight_grad = jnp.dot(mixed.T, residual_half, preferred_element_type=jnp.float32)
    proj_bias_grad = jnp.sum(residual_grad, axis=0)
    mixed_grad = (
        jnp.dot(residual_half, proj_back.T, preferred_element_type=jnp.float32)
        .astype(jnp.bfloat16)
        .reshape(split_shape)
    )
    probs = jnp.exp(window_scores(query, keys, table_bias) - logsum)
    prob_again = probs.astype(jnp.bfloat16)
    prob_grad = jnp.einsum(
        "wqhd,wkhd->whqk", mixed_grad, values, preferred_element_type=jnp.float32
    )
    value_grad = jnp.einsum(
        "whqk,wqhd->wkhd", prob_again, mixed_grad, preferred_element_type=jnp.float32
    )
    score_grad = probs * (prob_grad - jnp.sum(probs * prob_grad, axis=-1, keepdims=True))
    bias_sum = jnp.sum(score_grad, axis=0).reshape(heads, pairs)
    bias_table_grad = jnp.dot(bias_sum, one_hot, precision=lax.Precision.HIGHEST).T
    score_half = score_grad.astype(jnp.bfloat16)
    query_grad = (
        jnp.einsum("whqk,wkhd->wqhd", score_half, keys, preferred_element_type=jnp.float32) * scale
    )
    key_grad = jnp.einsum("whqk,wqhd->wkhd", score_half, query, preferred_element_type=jnp.float32)
    query_flat = query_grad.reshape(-1, width)
    value_flat = value_grad.reshape(-1, width)
    merged_grad = jnp.concatenate(
        [query_flat, key_grad.reshape(-1, width), value_flat], axis=1
    ).astype(jnp.bfloat16)
    query_bias_grad = jnp.sum(query_flat, axis=0)
    value_bias_grad = jnp.sum(value_flat, axis=0)
    qkv_weight_grad = jnp.dot(first_act.T, merged_grad, preferred_element_type=jnp.float32)
    first_grad = jnp.dot(merged_grad, qkv_back.T, preferred_element_type=jnp.float32)
    first_back, first_gain_grad, first_shift_grad = norm_back(
        first_grad, normal1, inverse1, first_gain
    )
    input_grad = (residual_grad + first_back).reshape(windows, tokens, width)
    shares = (
        lax.psum_scatter(
            qkv_weight_grad.astype(jnp.bfloat16), "shard", scatter_dimension=0, tiled=True
        ).astype(jnp.float32),
        lax.psum_scatter(
            proj_weight_grad.astype(jnp.bfloat16), "shard", scatter_dimension=0, tiled=True
        ).astype(jnp.float32),
        lax.psum_scatter(
            hidden_weight_grad.astype(jnp.bfloat16), "shard", scatter_dimension=0, tiled=True
        ).astype(jnp.float32),
        lax.psum_scatter(
            output_weight_grad.astype(jnp.bfloat16), "shard", scatter_dimension=0, tiled=True
        ).astype(jnp.float32),
    )
    qkv_share, proj_share, hidden_share, output_share = (
        lax.psum(shares[0].astype(jnp.bfloat16), "rep").astype(jnp.float32),
        lax.psum(shares[1].astype(jnp.bfloat16), "rep").astype(jnp.float32),
        lax.psum(shares[2].astype(jnp.bfloat16), "rep").astype(jnp.float32),
        lax.psum(shares[3].astype(jnp.bfloat16), "rep").astype(jnp.float32),
    )
    small_total = lax.psum(
        (
            query_bias_grad,
            value_bias_grad,
            proj_bias_grad,
            hidden_bias_grad,
            output_bias_grad,
            first_gain_grad,
            first_shift_grad,
            second_gain_grad,
            second_shift_grad,
            bias_table_grad,
        ),
        ("shard", "rep"),
    )
    return (
        block_output.reshape(windows, tokens, width),
        input_grad,
        qkv_share,
        small_total[0],
        small_total[1],
        proj_share,
        small_total[2],
        hidden_share,
        small_total[3],
        output_share,
        small_total[4],
        small_total[5],
        small_total[6],
        small_total[7],
        small_total[8],
        small_total[9],
    )


def solution(mesh):
    return jax.shard_map(
        on_device,
        mesh=mesh,
        in_specs=(
            P(("shard", "rep"), None, None),
            P(("shard", "rep"), None, None),
            P("shard", None),
            P(),
            P(),
            P("shard", None),
            P(),
            P("shard", None),
            P(),
            P("shard", None),
            P(),
            P(),
            P(),
            P(),
            P(),
            P(),
            P(),
        ),
        out_specs=(
            P(("shard", "rep"), None, None),
            P(("shard", "rep"), None, None),
            P("shard", None),
            P(),
            P(),
            P("shard", None),
            P(),
            P("shard", None),
            P(),
            P("shard", None),
            P(),
            P(),
            P(),
            P(),
            P(),
            P(),
        ),
        check_vma=False,
    )
```

profile of v0, /device:TPU:0, one launch (start us, length us, event | category | flops | bytes accessed | tf_op | source)
XLA Modules:
  0.0 625.3 jit_solution(6641242391102229124)
XLA Ops:
  9.5 2.1 convert_reduce_fusion.2
  12.7 3.9 copy.76
  17.1 1.2 convolution_bitcast_fusion
  18.9 12.1 %all_gather.17 = bf16[512,512]{1,0:T(8,128)(2,1)} all-gather(bf16[128,512]{1,0:T(8,128)(2,1)S(1)} %copy-done.16), channel_id=1, replica_groups=mesh['shard'=4,'rep'=8] {'shard'}, dimensions={0}, use_global_device_ids=true | all-gather | bytes 655360 | tf_op jit(solution)/shard_map/all_gather | solution.py:78
  30.9 3.0 copy.88
  34.0 2.5 reshape.163
  36.5 5.9 reshape.170
  42.4 7.3 %fusion.25 = f32[2352,1536]{1,0:T(8,128)S(1)} fusion(bf16[512,1536]{1,0:T(8,128)(2,1)} %all-gather.4.cloned.1.call-done, f32[2352,512]{1,0:T(8,128)} %reshape.170, f32[512]{0:T(512)S(1)} %copy-done.43, f32[512]{0:T(512)S(1)} %copy-done.35, f32[2352]{0:T(1024)S(1)} %rsqrt.20, f32[2352]{0:T(1024)S(1)} %div.27), kind=kOutput, calls=%fused_computation.76 | convolution fusion | flops 3705397248 | bytes 20863360 | tf_op jit(solution)/shard_map/dot_general | solution.py:83
  50.4 3.7 fusion.12
  54.1 11.5 %reshape.172 = bf16[48,49,16,32]{3,2,1,0:T(8,128)(2,1)} reshape(bf16[2352,512]{1,0:T(8,128)(2,1)} %get-tuple-element.90) | data formatting | bytes 4816896 | tf_op jit(solution)/shard_map/reshape | solution.py:84
  65.6 13.6 %copy.82 = bf16[48,49,16,32]{1,3,2,0:T(8,128)(2,1)} copy(bf16[48,49,16,32]{3,2,1,0:T(8,128)(2,1)} %reshape.172) | data formatting | bytes 4816896 | tf_op jit(solution)/shard_map/reshape | solution.py:84
  79.2 7.5 %reshape.173 = bf16[48,49,16,32]{3,2,1,0:T(8,128)(2,1)} reshape(bf16[2352,512]{1,0:T(8,128)(2,1)S(1)} %slice.25) | data formatting | bytes 4816896 | tf_op jit(solution)/shard_map/reshape | solution.py:85
  86.7 13.7 %copy.83 = bf16[48,49,16,32]{1,3,2,0:T(8,128)(2,1)} copy(bf16[48,49,16,32]{3,2,1,0:T(8,128)(2,1)} %reshape.173) | data formatting | bytes 4816896 | tf_op jit(solution)/shard_map/reshape | solution.py:85
  100.4 7.5 %reshape.171 = bf16[48,49,16,32]{3,2,1,0:T(8,128)(2,1)} reshape(bf16[2352,512]{1,0:T(8,128)(2,1)S(1)} %copy-done.11) | data formatting | bytes 4816896 | tf_op jit(solution)/shard_map/reshape | solution.py:86
  107.9 13.5 %copy.85 = bf16[48,49,16,32]{1,3,2,0:T(8,128)(2,1)} copy(bf16[48,49,16,32]{3,2,1,0:T(8,128)(2,1)} %reshape.171) | data formatting | bytes 4816896 | tf_op jit(solution)/shard_map/reshape | solution.py:86
  121.4 13.3 %add_reduce_fusion = (f32[48,16,49]{2,1,0:T(8,128)S(1)}, f32[48,16,49,49]{2,3,1,0:T(8,128)}) fusion(f32[16,49,49]{1,2,0:T(8,128)S(1)} %copy.84, bf16[48,49,16,32]{1,3,2,0:T(8,128)(2,1)} %copy.82, bf16[48,49,16,32]{1,3,2,0:T(8,128)(2,1)} %copy.83), kind=kOutput, calls=%fused_computation.5 | convolution fusion | flops 121664256 | bytes 12496960 | tf_op jit(solution)/shard_map/wqhd,wkhd->whqk/dot_general | solution.py:39
  135.5 12.9 %exponential_reduce_fusion = f32[48,16,49]{2,1,0:T(8,128)S(1)} fusion(f32[48,16,49,49]{2,3,1,0:T(8,128)} %get-tuple-element.93, f32[48,16,49]{2,1,0:T(8,128)S(1)} %get-tuple-element.92, f32[16,49,49]{1,2,0:T(8,128)} %copy-done.5), kind=kLoop, calls=%fused_computation.4 | loop fusion | flops 5494272 | bytes 7830592 | tf_op jit(solution)/shard_map/reduce_sum | solution.py:89
  149.5 11.5 %convert_bitcast_fusion.1 = bf16[48,49,16,32]{1,3,2,0:T(8,128)(2,1)} fusion(bf16[48,49,16,32]{1,3,2,0:T(8,128)(2,1)S(1)} %copy-done.2, f32[48,16,49,49]{2,3,1,0:T(8,128)} %get-tuple-element.93, f32[48,16,49]{2,1,0:T(8,128)S(1)} %log_add_fusion, f32[16,49,49]{1,2,0:T(8,128)} %copy-done.5), kind=kOutput, calls=%fused_computation.21 | convolution fusion | flops 124750080 | bytes 12496960 | tf_op jit(solution)/shard_map/whqk,wkhd->wqhd/dot_general | solution.py:92
  161.0 9.5 %copy.87 = bf16[48,49,16,32]{1,0,3,2:T(8,128)(2,1)} copy(bf16[48,49,16,32]{1,3,2,0:T(8,128)(2,1)} %convert_bitcast_fusion.1) | data formatting | bytes 4816896 | tf_op jit(solution)/shard_map/convert_element_type | solution.py:93
  170.4 8.1 %reshape.161 = bf16[2352,512]{0,1:T(8,128)(2,1)S(1)} reshape(bf16[48,49,16,32]{1,0,3,2:T(8,128)(2,1)} %copy.87) | data formatting | bytes 4816896 | tf_op jit(solution)/shard_map/reshape | solution.py:94
  178.6 4.0 fusion.29
  182.6 2.2 copy-done.4
  185.8 14.9 %multiply_convert_fusion = (bf16[2352,2048]{1,0:T(8,128)(2,1)}, f32[2352,2048]{1,0:T(8,128)}) fusion(f32[2048]{0:T(1024)S(1)} %copy-done.42, bf16[512,2048]{1,0:T(8,128)(2,1)} %all-gather.6.cloned.1.call-done, f32[2352,512]{1,0:T(8,128)} %copy-done.4, f32[512]{0:T(512)S(1)} %copy-done.45, f32[512]{0:T(512)S(1)} %copy-done.33, ...), kind=kOutput, calls=%fused_computation.13 | convolution fusion | flops 4967424000 | bytes 35846528 | tf_op jit(solution)/shard_map/dot_general | solution.py:105
  200.7 18.4 %convert_reduce_fusion = (f32[2048]{0:T(1024)}, bf16[2352,2048]{1,0:T(8,128)(2,1)}) fusion(f32[2352,2048]{1,0:T(8,128)} %get-tuple-element.97, f32[2048]{0:T(1024)S(1)} %copy-done.42, bf16[2352,512]{1,0:T(8,128)(2,1)} %reshape.163, bf16[2048,512]{1,0:T(8,128)(2,1)} %all-gather.8.cloned.1.call-done), kind=kOutput, calls=%fused_computation.12 | convolution fusion | flops 4995119104 | bytes 33423360 | tf_op jit(solution)/shard_map/dot_general | solution.py:119
  219.2 11.8 %multiply_reduce_fusion.1 = (f32[512]{0:T(512)}, f32[2352]{0:T(1024)S(1)}, f32[2352]{0:T(1024)S(1)}, f32[512]{0:T(512)}, f32[2352,512]{1,0:T(8,128)S(1)}) fusion(f32[2352,512]{1,0:T(8,128)S(1)} %bitcast.63, f32[2352]{0:T(1024)S(1)} %add_rsqrt_fusion.1, f32[2352]{0:T(1024)S(1)} %broadcast_multiply_fusion.5, f32[512]{0:T(512)S(1)} %copy-done.33, ...), kind=kOutput, calls=%fused_computation.33 | convolution fusion | flops 4943333376 | bytes 21408512 | tf_op jit(solution)/shard_map/dot_general | solution.py:123
  230.9 2.8 fusion.28
  233.7 2.2 copy-done.3
  235.9 2.4 convolution_convert_fusion.4
  238.3 3.9 convolution_convert_fusion
  242.3 7.5 %reshape.174 = bf16[48,49,16,32]{3,2,1,0:T(8,128)(2,1)} reshape(bf16[2352,512]{1,0:T(8,128)(2,1)S(1)} %convolution_convert_fusion) | data formatting | bytes 4816896 | tf_op jit(solution)/shard_map/reshape | solution.py:138
  249.8 13.7 %copy.90 = bf16[48,49,16,32]{1,3,2,0:T(8,128)(2,1)} copy(bf16[48,49,16,32]{3,2,1,0:T(8,128)(2,1)} %reshape.174) | data formatting | bytes 4816896 | tf_op jit(solution)/shard_map/reshape | solution.py:138
  263.4 22.6 %multiply_reduce_fusion = (f32[48,16,49]{2,1,0:T(8,128)S(1)}, f32[48,16,49,49]{2,3,1,0:T(8,128)}) fusion(f32[48,16,49,49]{2,3,1,0:T(8,128)} %get-tuple-element.93, f32[48,16,49]{2,1,0:T(8,128)S(1)} %log_add_fusion, f32[16,49,49]{1,2,0:T(8,128)S(1)} %copy-done.6, bf16[48,49,16,32]{1,3,2,0:T(8,128)(2,1)} %copy.90, bf16[48,49,16,32]{1,3,2,0:T(8,128)(2,1)} %copy.85), kind=kOutput, calls=%fused_computation.2 | convolution fusion | flops 125352192 | bytes 20023360 | tf_op jit(solution)/shard_map/wqhd,wkhd->whqk/dot_general | solution.py:142
  286.0 18.8 %bitcast_convert_fusion = (bf16[48,49,16,32]{1,3,2,0:T(8,128)(2,1)}, f32[48,16,32,49]{3,2,1,0:T(8,128)}) fusion(bf16[48,49,16,32]{1,3,2,0:T(8,128)(2,1)} %copy.90, f32[48,16,49,49]{2,3,1,0:T(8,128)} %get-tuple-element.93, f32[48,16,49]{2,1,0:T(8,128)S(1)} %log_add_fusion, f32[16,49,49]{1,2,0:T(8,128)S(1)} %copy-done.6), kind=kOutput, calls=%fused_computation.17 | convolution fusion | flops 124750080 | bytes 17313856 | tf_op jit(solution)/shard_map/whqk,wqhd->wkhd/dot_general | solution.py:145
  304.9 20.8 %fusion.27 = (f32[16,49,49]{1,2,0:T(8,128)}, bf16[48,16,49,49]{2,3,1,0:T(8,128)(2,1)}) fusion(f32[48,16,49,49]{2,3,1,0:T(8,128)} %get-tuple-element.100, f32[48,16,49]{2,1,0:T(8,128)S(1)} %get-tuple-element.99, f32[48,16,49]{2,1,0:T(8,128)S(1)} %log_add_fusion, f32[48,16,49,49]{2,3,1,0:T(8,128)} %get-tuple-element.93, f32[16,49,49]{1,2,0:T(8,128)S(1)} %copy-done.6), kind=kLoop, calls=%fused_computation.78 | loop fusion | flops 11025392 | bytes 19048064 | tf_op jit(solution)/shard_map/reduce_sum | solution.py:149
  325.7 10.3 %convert_bitcast_fusion = bf16[48,49,16,32]{1,3,2,0:T(8,128)(2,1)} fusion(bf16[48,49,16,32]{1,3,2,0:T(8,128)(2,1)S(1)} %bitcast.59, bf16[48,16,49,49]{2,3,1,0:T(8,128)(2,1)} %get-tuple-element.87), kind=kOutput, calls=%fused_computation.20 | convolution fusion | flops 119218176 | bytes 8504832 | tf_op jit(solution)/shard_map/whqk,wqhd->wkhd/dot_general | solution.py:155
  336.0 15.7 %bitcast_convert_fusion.1 = (bf16[48,49,16,32]{1,3,2,0:T(8,128)(2,1)}, f32[48,16,32,49]{3,2,1,0:T(8,128)}) fusion(bf16[48,49,16,32]{1,3,2,0:T(8,128)(2,1)} %copy.83, bf16[48,16,49,49]{2,3,1,0:T(8,128)(2,1)} %get-tuple-element.87), kind=kOutput, calls=%fused_computation.19 | convolution fusion | flops 120422400 | bytes 13321728 | tf_op jit(solution)/shard_map/whqk,wkhd->wqhd/dot_general | solution.py:153
  351.8 9.5 %copy.97 = bf16[48,49,16,32]{1,0,3,2:T(8,128)(2,1)} copy(bf16[48,49,16,32]{1,3,2,0:T(8,128)(2,1)} %convert_bitcast_fusion) | data formatting | bytes 4816896 | tf_op jit(solution)/shard_map/whqk,wqhd->wkhd/transpose | solution.py:155
  361.3 8.5 %reshape.166 = bf16[2352,512]{0,1:T(8,128)(2,1)S(1)} reshape(bf16[48,49,16,32]{1,0,3,2:T(8,128)(2,1)} %copy.97) | data formatting | bytes 4816896 | tf_op jit(solution)/shard_map/reshape | solution.py:159
  369.8 9.5 %copy.100 = bf16[48,49,16,32]{1,0,3,2:T(8,128)(2,1)} copy(bf16[48,49,16,32]{1,3,2,0:T(8,128)(2,1)} %get-tuple-element.103) | data formatting | bytes 4816896 | tf_op jit(solution)/shard_map/convert.4
  379.3 9.2 %reshape.167 = bf16[2352,512]{0,1:T(8,128)(2,1)} reshape(bf16[48,49,16,32]{1,0,3,2:T(8,128)(2,1)} %copy.100) | data formatting | bytes 4816896 | tf_op jit(solution)/shard_map/reshape | solution.py:157
  388.5 9.5 %copy.94 = bf16[48,49,16,32]{1,0,3,2:T(8,128)(2,1)} copy(bf16[48,49,16,32]{1,3,2,0:T(8,128)(2,1)} %get-tuple-element.101) | data formatting | bytes 4816896 | tf_op jit(solution)/shard_map/convert.7
  398.0 9.3 %reshape.165 = bf16[2352,512]{0,1:T(8,128)(2,1)} reshape(bf16[48,49,16,32]{1,0,3,2:T(8,128)(2,1)} %copy.94) | data formatting | bytes 4816896 | tf_op jit(solution)/shard_map/reshape | solution.py:156
  407.4 2.0 constant_dynamic-update-slice_fusion.2
  410.2 3.0 copy-done.15
  413.3 6.4 %convolution_convert_fusion.2 = bf16[512,1536]{1,0:T(8,128)(2,1)} fusion(bf16[2352,1536]{0,1:T(8,128)(2,1)S(1)} %constant_dynamic-update-slice_fusion, f32[2352,512]{1,0:T(8,128)S(1)} %bitcast.61, f32[512]{0:T(512)S(1)} %copy-done.44, f32[512]{0:T(512)S(1)} %copy-done.36, f32[2352]{0:T(1024)S(1)} %copy-done.24, f32[2352]{0:T(1024)S(1)} %copy-done.22), kind=kOutput, calls=%fused_computation.53 | convolution fusion | flops 3706183680 | bytes 13638016 | tf_op jit(solution)/shard_map/dot_general | solution.py:163
  419.8 10.1 %convolution_convert_fusion.1 = bf16[2048,512]{1,0:T(8,128)(2,1)} fusion(bf16[2352,2048]{1,0:T(8,128)(2,1)} %get-tuple-element.96, bf16[2352,512]{1,0:T(8,128)(2,1)} %reshape.163), kind=kOutput, calls=%fused_computation.52 | convolution fusion | flops 4933550080 | bytes 14139392 | tf_op jit(solution)/shard_map/dot_general | solution.py:116
  430.4 12.5 %convolution_convert_fusion.3 = bf16[512,2048]{1,0:T(8,128)(2,1)} fusion(bf16[2352,2048]{1,0:T(8,128)(2,1)} %get-tuple-element.107, f32[2352,512]{1,0:T(8,128)} %copy-done.4, f32[512]{0:T(512)S(1)} %copy-done.46, f32[512]{0:T(512)S(1)} %copy-done.34, f32[2352]{0:T(1024)S(1)} %copy-done.20, f32[2352]{0:T(1024)S(1)} %copy-done.18), kind=kOutput, calls=%fused_computation.54 | convolution fusion | flops 4939571200 | bytes 16570752 | tf_op jit(solution)/shard_map/dot_general | solution.py:121
  443.3 12.8 %multiply_reduce_fusion.2 = (f32[512]{0:T(512)S(1)}, f32[2352]{0:T(1024)S(1)}, f32[2352]{0:T(1024)S(1)}, f32[512]{0:T(512)S(1)}, f32[2352,512]{1,0:T(8,128)}) fusion(f32[2352,512]{1,0:T(8,128)} %reshape.170, f32[2352]{0:T(1024)S(1)} %copy-done.24, f32[2352]{0:T(1024)S(1)} %copy-done.22, f32[512]{0:T(512)S(1)} %copy-done.36, ...), kind=kOutput, calls=%fused_computation.34 | convolution fusion | flops 3710208512 | bytes 18475776 | tf_op jit(solution)/shard_map/dot_general | solution.py:164
  456.1 6.9 %bitcast_reduce_fusion = f32[16,32]{1,0:T(8,128)S(1)} fusion(f32[48,16,32,49]{3,2,1,0:T(8,128)} %get-tuple-element.104), kind=kLoop, calls=%fused_computation.16 | loop fusion | flops 1203712 | bytes 4818944 | tf_op jit(solution)/shard_map/reduce_sum | solution.py:162
  463.0 6.8 %bitcast_reduce_fusion.1 = f32[16,32]{1,0:T(8,128)S(1)} fusion(f32[48,16,32,49]{3,2,1,0:T(8,128)} %get-tuple-element.102), kind=kLoop, calls=%fused_computation.18 | loop fusion | flops 2407936 | bytes 4818944 | tf_op jit(solution)/shard_map/reduce_sum | solution.py:161
  470.7 6.9 %add_convert_fusion = bf16[2352,512]{1,0:T(8,128)(2,1)} fusion(f32[2352,512]{1,0:T(8,128)S(1)} %bitcast.65, bf16[2352,2048]{1,0:T(8,128)(2,1)S(1)} %bitcast.67, bf16[2048,512]{1,0:T(8,128)(2,1)S(1)} %copy-done.39, f32[512]{0:T(512)S(1)} %copy-done.47), kind=kOutput, calls=%fused_computation.40 | convolution fusion | flops 4936114176 | bytes 18958336 | tf_op jit(solution)/shard_map/dot_general | solution.py:108
  477.5 5.6 reduce-scatter.11.cloned.1.call-done
  483.1 33.7 %reduce-scatter.9.cloned.1.call-done = bf16[128,2048]{1,0:T(8,128)(2,1)} async-done(((bf16[512,2048]{1,0:T(8,128)(2,1)}), bf16[128,2048]{1,0:T(8,128)(2,1)}) %reduce-scatter.9.cloned.1.call-update) | async-done | bytes 524304 | tf_op jit(solution)/shard_map/reduce_scatter | solution.py:176
  516.8 2.9 reshape.162
  519.7 2.2 copy.102
  522.5 8.8 %multiply_add_fusion = f32[2352,512]{1,0:T(8,128)} fusion(f32[2352,512]{1,0:T(8,128)} %copy-done.3, f32[2352,512]{1,0:T(8,128)} %get-tuple-element.105, f32[2352,512]{1,0:T(8,128)} %reshape.170, f32[2352]{0:T(1024)S(1)} %broadcast_multiply_fusion.1, f32[2352]{0:T(1024)S(1)} %broadcast_multiply_fusion.2, f32[512]{0:T(512)S(1)} %copy-done.36, ...), kind=kLoop, calls=%fused_computation.36 | loop fusion | flops 9633792 | bytes 19307264 | tf_op jit(solution)/shard_map/add | solution.py:168
  531.3 5.8 reshape.168
  537.1 7.7 %copy.103 = f32[48,49,512]{2,0,1:T(8,128)} copy(f32[48,49,512]{2,1,0:T(8,128)} %reshape.168) | data formatting | bytes 9633792
  545.8 40.7 %all-reduce = (f32[512]{0:T(512)}, f32[512]{0:T(512)}, f32[512]{0:T(512)}, f32[2048]{0:T(1024)}, f32[512]{0:T(512)}, /*index=5*/f32[512]{0:T(512)}, f32[512]{0:T...) all-reduce(f32[512]{0:T(512)S(1)} %reduce_sum.195, ...), channel_id=1, replica_groups=mesh['shard'=4,'rep'=8] {'shard','rep'}, use_global_device_ids=true, to_apply=%region_14.0 | all-reduce | flops 8848 | bytes 70784 | tf_op jit(solution)/shard_map/psum | solution.py:189
  586.4 23.8 %all-reduce.4.cloned.1.call-done = (bf16[128,1536]{1,0:T(8,128)(2,1)}, bf16[128,512]{1,0:T(8,128)(2,1)}, bf16[128,2048]{1,0:T(8,128)(2,1)}, bf16[512,512]{1,0:T(8,128)(2,1)}) async-done(((bf16[128,1536]{1,0:T(8,128)(2,1)}, bf16[128,512]{1,0:T(8,128)(2,1)}, bf16[128,2048]{1,0:T(8,128)(2,1)}, bf16[512,512]{1,0:T(8,128)(2,1)}), (bf16[128,1536]{1,0:T(8,128)(2,1)}, bf16[128,512]{1,0:T(8,128)(2,1)}, ...) | async-done | bytes 1572880 | tf_op jit(solution)/shard_map/psum | solution.py:184
  610.2 1.6 convert_element_type.114
  611.8 2.0 convert_element_type.112
  613.8 2.1 convert_element_type.116
  615.9 2.1 convert_element_type.119
  (167 shorter events, 11.8 us)
Async XLA Ops:
  7.2 9.9 %copy-start = (f32[169,16]{0,1:T(8,128)S(1)}, f32[169,16]{0,1:T(8,128)}, u32[]{:S(2)}) copy-start(f32[169,16]{0,1:T(8,128)} %param.32) | copy-start | bytes 32452
  7.2 4.4 copy-start.7
  7.2 35.2 %all-gather.4.cloned.1.call-start = ((), (), s32[]{:S(2)}) async-start(), calls=%async_computation.4 | async-start | bytes 1966080 | tf_op jit(solution)/shard_map/all_gather | solution.py:77
  7.9 177.8 %all-gather.6.cloned.1.call-start = ((), (), s32[]{:S(2)}) async-start(), calls=%async_computation.5 | async-start | bytes 2621440 | tf_op jit(solution)/shard_map/all_gather | solution.py:100
  8.7 192.0 %all-gather.8.cloned.1.call-start = ((), (), s32[]{:S(2)}) async-start(), calls=%async_computation.6 | async-start | bytes 2621440 | tf_op jit(solution)/shard_map/all_gather | solution.py:101
  9.4 468.1 %reduce-scatter.7.cloned.1.call-start = ((), (), s32[]{:S(2)}) async-start(), calls=%async_computation.8 | async-start | bytes 655360 | tf_op jit(solution)/shard_map/reduce_scatter | solution.py:173
  11.6 5.0 copy-start.25
  12.7 6.1 copy-start.16
  16.7 2.1 copy-start.26
  16.9 25.5 %copy-start.21 = (f32[2352]{0:T(1024)}, f32[2352]{0:T(1024)S(1)}, u32[]{:S(2)}) copy-start(f32[2352]{0:T(1024)S(1)} %div.27) | copy-start | bytes 28228
  17.1 25.3 %copy-start.23 = (f32[2352]{0:T(1024)}, f32[2352]{0:T(1024)S(1)}, u32[]{:S(2)}) copy-start(f32[2352]{0:T(1024)S(1)} %rsqrt.20) | copy-start | bytes 28228
  18.9 102.6 %copy-start.5 = (f32[16,49,49]{1,2,0:T(8,128)}, f32[16,49,49]{1,2,0:T(8,128)S(1)}, u32[]{:S(2)}) copy-start(f32[16,49,49]{1,2,0:T(8,128)S(1)} %copy.84) | copy-start | bytes 460996
  36.4 6.0 copy-start.35
  36.5 6.0 copy-start.43
  86.7 13.7 %copy-start.11 = (bf16[2352,512]{1,0:T(8,128)(2,1)S(1)}, bf16[2352,512]{1,0:T(8,128)(2,1)}, u32[]{:S(2)}) copy-start(bf16[2352,512]{1,0:T(8,128)(2,1)} %get-tuple-element.91) | copy-start | bytes 7225348
  135.5 14.0 %copy-start.2 = (bf16[48,49,16,32]{1,3,2,0:T(8,128)(2,1)S(1)}, bf16[48,49,16,32]{1,3,2,0:T(8,128)(2,1)}, u32[]{:S(2)}) copy-start(bf16[48,49,16,32]{1,3,2,0:T(8,128)(2,1)} %copy.85) | copy-start | bytes 7225348
  170.4 8.2 %copy-start.12 = (bf16[512,512]{1,0:T(8,128)(2,1)S(1)}, bf16[512,512]{1,0:T(8,128)(2,1)}, u32[]{:S(2)}) copy-start(bf16[512,512]{1,0:T(8,128)(2,1)} %all_gather.17) | copy-start | bytes 1572868
  170.4 8.2 %copy-start.28 = (f32[512]{0:T(512)S(1)}, f32[512]{0:T(512)}, u32[]{:S(2)}) copy-start(f32[512]{0:T(512)} %param.23) | copy-start | bytes 6148
  182.6 2.2 copy-start.4
  182.6 3.2 copy-start.33
  182.6 3.2 copy-start.42
  182.6 3.2 copy-start.45
  182.6 48.3 %copy-start.17 = (f32[2352]{0:T(1024)}, f32[2352]{0:T(1024)S(1)}, u32[]{:S(2)}) copy-start(f32[2352]{0:T(1024)S(1)} %broadcast_multiply_fusion.5) | copy-start | bytes 28228
  185.7 45.2 %copy-start.19 = (f32[2352]{0:T(1024)}, f32[2352]{0:T(1024)S(1)}, u32[]{:S(2)}) copy-start(f32[2352]{0:T(1024)S(1)} %add_rsqrt_fusion.1) | copy-start | bytes 28228
  185.8 33.3 %slice-start.4 = ((s8[4816896]{0:T(1024)(128)(4,1)}), s8[622592]{0:T(1024)(128)(4,1)S(1)}, s32[]{:S(2)}) async-start(s8[4816896]{0:T(1024)(128)(4,1)} %bitcast.62), calls=%async_computation.16 | async-start | bytes 1245184
  200.7 18.4 %slice-start.5 = ((s8[4816896]{0:T(1024)(128)(4,1)}), s8[4194304]{0:T(1024)(128)(4,1)S(1)}, s32[]{:S(2)}) async-start(s8[4816896]{0:T(1024)(128)(4,1)} %bitcast.62), calls=%async_computation.17 | async-start | bytes 8388608
  200.7 18.4 %copy-start.40 = (bf16[512,2048]{1,0:T(8,128)(2,1)S(1)}, bf16[512,2048]{1,0:T(8,128)(2,1)}, u32[]{:S(2)}) copy-start(bf16[512,2048]{1,0:T(8,128)(2,1)} %all-gather.6.cloned.1.call-done) | copy-start | bytes 6291460
  219.1 11.8 %copy-start.10 = (bf16[2352,512]{1,0:T(8,128)(2,1)S(1)}, bf16[2352,512]{1,0:T(8,128)(2,1)}, u32[]{:S(2)}) copy-start(bf16[2352,512]{1,0:T(8,128)(2,1)} %reshape.163) | copy-start | bytes 7225348
  233.7 2.2 copy-start.3
  249.8 13.7 %copy-start.6 = (f32[16,49,49]{1,2,0:T(8,128)S(1)}, f32[16,49,49]{1,2,0:T(8,128)}, u32[]{:S(2)}) copy-start(f32[16,49,49]{1,2,0:T(8,128)} %copy-done.5) | copy-start | bytes 460996
  263.4 62.2 %slice-start = ((s8[6291456]{0:T(1024)(128)(4,1)}), s8[2097152]{0:T(1024)(128)(4,1)S(1)}, s32[]{:S(2)}) async-start(s8[6291456]{0:T(1024)(128)(4,1)} %bitcast.58), calls=%async_computation.12 | async-start | bytes 4194304
  286.0 39.7 %slice-start.1 = ((s8[6291456]{0:T(1024)(128)(4,1)}), s8[4194304]{0:T(1024)(128)(4,1)S(1)}, s32[]{:S(2)}) async-start(s8[6291456]{0:T(1024)(128)(4,1)} %bitcast.58), calls=%async_computation.13 | async-start | bytes 8388608
  351.7 125.8 %reduce-scatter.5.cloned.1.call-start = ((), (), s32[]{:S(2)}) async-start(), calls=%async_computation.7 | async-start | bytes 1966080 | tf_op jit(solution)/shard_map/reduce_scatter | solution.py:170
  407.3 2.5 copy-start.8
  407.4 5.9 slice-start.2
  409.4 3.8 slice-start.3
  409.4 3.8 copy-start.22
  409.4 3.8 copy-start.24
  409.4 3.8 copy-start.36
  409.4 3.8 copy-start.44
  410.2 3.1 copy-start.15
  419.7 63.3 %reduce-scatter.11.cloned.1.call-start = ((), (), s32[]{:S(2)}) async-start(), calls=%async_computation.10 | async-start | bytes 2621440 | tf_op jit(solution)/shard_map/reduce_scatter | solution.py:179
  419.8 10.2 %copy-start.9 = (bf16[48,49,512]{2,0,1:T(8,128)(2,1)S(1)}, bf16[48,49,512]{2,0,1:T(8,128)(2,1)}, u32[]{:S(2)}) copy-start(bf16[48,49,512]{2,0,1:T(8,128)(2,1)} %param.18) | copy-start | bytes 7225348
  419.8 10.6 %copy-start.18 = (f32[2352]{0:T(1024)S(1)}, f32[2352]{0:T(1024)}, u32[]{:S(2)}) copy-start(f32[2352]{0:T(1024)} %copy-done.17) | copy-start | bytes 28228
  419.8 10.6 %copy-start.20 = (f32[2352]{0:T(1024)S(1)}, f32[2352]{0:T(1024)}, u32[]{:S(2)}) copy-start(f32[2352]{0:T(1024)} %copy-done.19) | copy-start | bytes 28228
  419.8 10.6 %copy-start.34 = (f32[512]{0:T(512)S(1)}, f32[512]{0:T(512)}, u32[]{:S(2)}) copy-start(f32[512]{0:T(512)} %param.30) | copy-start | bytes 6148
  419.8 10.6 %copy-start.46 = (f32[512]{0:T(512)S(1)}, f32[512]{0:T(512)}, u32[]{:S(2)}) copy-start(f32[512]{0:T(512)} %param.31) | copy-start | bytes 6148
  429.9 86.8 %reduce-scatter.9.cloned.1.call-start = ((), (), s32[]{:S(2)}) async-start(), calls=%async_computation.9 | async-start | bytes 2621440 | tf_op jit(solution)/shard_map/reduce_scatter | solution.py:176
  430.4 12.8 %copy-start.41 = (bf16[512,1536]{1,0:T(8,128)(2,1)S(1)}, bf16[512,1536]{1,0:T(8,128)(2,1)}, u32[]{:S(2)}) copy-start(bf16[512,1536]{1,0:T(8,128)(2,1)} %all-gather.4.cloned.1.call-done) | copy-start | bytes 4718596
  443.0 167.2 %all-reduce.4.cloned.1.call-start = ((), (), s32[]{:S(2)}) async-start(), calls=%async_computation.11 | async-start | bytes 3145728 | tf_op jit(solution)/shard_map/psum | solution.py:184
  456.1 13.8 %slice-start.6 = ((s8[4816896]{0:T(1024)(128)(4,1)}), s8[4194304]{0:T(1024)(128)(4,1)S(1)}, s32[]{:S(2)}) async-start(s8[4816896]{0:T(1024)(128)(4,1)} %bitcast.64), calls=%async_computation.18 | async-start | bytes 8388608
  456.1 13.8 %slice-start.8 = ((s8[9633792]{0:T(1024)(128)(4,1)}), s8[4194304]{0:T(1024)(128)(4,1)S(1)}, s32[]{:S(2)}) async-start(s8[9633792]{0:T(1024)(128)(4,1)} %bitcast.66), calls=%async_computation.20 | async-start | bytes 8388608
  456.1 13.8 %slice-start.9 = ((s8[9633792]{0:T(1024)(128)(4,1)}), s8[4194304]{0:T(1024)(128)(4,1)S(1)}, s32[]{:S(2)}) async-start(s8[9633792]{0:T(1024)(128)(4,1)} %bitcast.66), calls=%async_computation.21 | async-start | bytes 8388608
  463.0 6.9 %slice-start.7 = ((s8[4816896]{0:T(1024)(128)(4,1)}), s8[622592]{0:T(1024)(128)(4,1)S(1)}, s32[]{:S(2)}) async-start(s8[4816896]{0:T(1024)(128)(4,1)} %bitcast.64), calls=%async_computation.19 | async-start | bytes 1245184
  463.0 7.3 %copy-start.39 = (bf16[2048,512]{1,0:T(8,128)(2,1)S(1)}, bf16[2048,512]{1,0:T(8,128)(2,1)}, u32[]{:S(2)}) copy-start(bf16[2048,512]{1,0:T(8,128)(2,1)} %all-gather.8.cloned.1.call-done) | copy-start | bytes 6291460
  463.0 7.3 %copy-start.47 = (f32[512]{0:T(512)S(1)}, f32[512]{0:T(512)}, u32[]{:S(2)}) copy-start(f32[512]{0:T(512)} %param.27) | copy-start | bytes 6148
  463.0 7.6 %slice-start.10 = ((s8[9633792]{0:T(1024)(128)(4,1)}), s8[1245184]{0:T(1024)(128)(4,1)S(1)}, s32[]{:S(2)}) async-start(s8[9633792]{0:T(1024)(128)(4,1)} %bitcast.66), calls=%async_computation.22 | async-start | bytes 2490368
  516.8 5.1 copy-start.14
  537.1 7.7 %copy-start.27 = (s32[2401]{0:T(1024)S(1)}, s32[2401]{0:T(1024)}, u32[]{:S(2)}) copy-start(s32[2401]{0:T(1024)} %copy-done.26) | copy-start | bytes 28816
  537.1 8.6 %copy-start.29 = (f32[512]{0:T(512)S(1)}, f32[512]{0:T(512)}, u32[]{:S(2)}) copy-start(f32[512]{0:T(512)} %get-tuple-element.88) | copy-start | bytes 6148
  537.1 8.7 %copy-start.30 = (f32[2048]{0:T(1024)S(1)}, f32[2048]{0:T(1024)}, u32[]{:S(2)}) copy-start(f32[2048]{0:T(1024)} %get-tuple-element.106) | copy-start | bytes 24580
  537.1 8.7 %copy-start.37 = (f32[512]{0:T(512)S(1)}, f32[512]{0:T(512)}, u32[]{:S(2)}) copy-start(f32[512]{0:T(512)} %get-tuple-element.64) | copy-start | bytes 6148
  537.1 8.7 %copy-start.38 = (f32[512]{0:T(512)S(1)}, f32[512]{0:T(512)}, u32[]{:S(2)}) copy-start(f32[512]{0:T(512)} %get-tuple-element.70) | copy-start | bytes 6148
  537.1 80.9 %copy-start.1 = (f32[169,16]{0,1:T(8,128)S(1)}, f32[169,16]{0,1:T(8,128)}, u32[]{:S(2)}) copy-start(f32[169,16]{0,1:T(8,128)} %param.32) | copy-start | bytes 32452
  (3 other events, 2.1 us)
Sparse Core Ops, SparseCore 0:
  9.6 25.1 all-gather.3
  36.3 22.5 all-gather.5
  60.5 22.5 all-gather.7
  351.9 23.2 reduce-scatter.6
  419.9 29.6 reduce-scatter.4
  451.9 31.1 reduce-scatter.10
  485.6 31.1 reduce-scatter.8
  520.6 89.5 all-reduce.3
where the time goes:
time: 633 us; the launch traced here: 625 us
  local copies, waits for them, and re-layouts  210 us (33%)
  matrix products  206 us (33%)
  other arithmetic  76.1 us (12%)
  waiting for transfers between devices  65.2 us (10%)
  blocking collectives  52.7 us (8%)
  between operations  15.3 us (2%)
    psum x1, blocking collectives, on_device(): lax.psum((query_bias_grad, value_bias_grad, proj_bias_grad, hidden_bias_g...  40.7 us
    reduce_scatter x1, waiting for transfers between devices, on_device(): lax.psum_scatter(hidden_weight_grad.astype(jnp.bfloat16), 'shard', scatte...  33.7 us
    reshape x2, local copies, waits for them, and re-layouts, on_device(): ((projected[:, :width] + query_bias) * scale).astype(jnp.bfloat16)  25.1 us
    unnamed x123, local copies, waits for them, and re-layouts  24.9 us
    psum x1, waiting for transfers between devices, on_device(): lax.psum(shares[0].astype(jnp.bfloat16), 'rep').astype(jnp.float32)  23.8 us
    dot_general x1, matrix products, on_device(): jnp.einsum('wqhd,wkhd->whqk', mixed_grad, values, preferred_element_type=...  22.6 us
    reshape x2, local copies, waits for them, and re-layouts, on_device(): projected[:, width:2 * width].astype(jnp.bfloat16).reshape(split_shape)  21.2 us
    reshape x2, local copies, waits for them, and re-layouts, on_device(): mixed_grad = jnp.dot(residual_half, proj_back.T, preferred_element_type=j...  21.2 us
  transfers between devices with their start and end apart: 8, of which 3 were waited for; matrix products, arithmetic and copies ran while one was open for 52% of the time, Pallas kernels for 0%

commit v1 on v0

v1 whole, which is shorter than its diff:
```python
import functools

import jax
import jax.numpy as jnp
from jax import lax
from jax.experimental import pallas as pl
from jax.experimental.pallas import tpu as pltpu
from jax.sharding import PartitionSpec as P

epsilon = 1e-05
f32 = jnp.float32
bf16 = jnp.bfloat16


def dot_nn(a, b):
    return lax.dot_general(a, b, (((1,), (0,)), ((), ())), preferred_element_type=f32)


def dot_nt(a, b):
    return lax.dot_general(a, b, (((1,), (1,)), ((), ())), preferred_element_type=f32)


def dot_tn(a, b):
    return lax.dot_general(a, b, (((0,), (0,)), ((), ())), preferred_element_type=f32)


def norm_parts(values):
    center = values - jnp.mean(values, axis=-1, keepdims=True)
    inverse = lax.rsqrt(jnp.mean(center * center, axis=-1, keepdims=True) + epsilon)
    return center * inverse, inverse


def fold_rows(values):
    rows, cols = values.shape
    return jnp.sum(values.reshape(rows // 8, 8, cols), axis=0)


def gelu_pair(upper):
    bell = jnp.exp(upper * upper * -0.5)
    t = 1.0 / (1.0 + 0.23164189 * jnp.abs(upper))
    poly = t * (
        0.127414796
        + t * (-0.142248368 + t * (0.7107068705 + t * (-0.7265760135 + t * 0.5307027145)))
    )
    tail = poly * bell
    phi = jnp.where(upper >= 0.0, 1.0 - tail, tail)
    return upper * phi, phi + upper * bell * 0.3989422804014327


def compute_kernel(
    dims,
    x_ref,
    dy_ref,
    wqkv_ref,
    wproj_ref,
    w1_ref,
    w2_ref,
    qkv_bias_ref,
    qkv_scale_ref,
    proj_bias_ref,
    hidden_bias_ref,
    output_bias_ref,
    gain1_ref,
    shift1_ref,
    gain2_ref,
    shift2_ref,
    bias_ref,
    y_ref,
    dx_ref,
    dwqkv_ref,
    dwproj_ref,
    dw1_ref,
    dw2t_ref,
    small_ref,
    dbias_ref,
    perm_ref,
    back_ref,
    act_w_ref,
    qkv_ref,
    mixed_w_ref,
    mixed_ref,
    lse_ref,
    wide_ref,
    sa_ref,
    sat_ref,
    dyt_ref,
    u_ref,
    da_ref,
    act_ref,
    dup_ref,
    acc_ref,
):
    tokens, windows, width, heads, hidden = dims
    head_size = width // heads
    scale = head_size ** (-0.5)
    pad = 64
    key_rows = 56
    sub = 8
    group = 2 * sub
    groups = windows // group
    quad = 128 // head_size
    quads = heads // quad
    rows8 = tokens * sub
    rows = tokens * group
    rows_w = sub * pad
    chunk = 256
    step = 7
    lane_head = lax.broadcasted_iota(jnp.int32, (pad, 128), 1) // head_size
    head_masks = [(lane_head == h).astype(f32) for h in range(quad)]
    head_masks_half = [m.astype(bf16) for m in head_masks]

    base = {}
    at = 0
    for name, size in (
        ("qb", width),
        ("vb", width),
        ("pb", width),
        ("hb", hidden),
        ("ob", width),
        ("g1", width),
        ("s1", width),
        ("g2", width),
        ("s2", width),
    ):
        base[name] = (at, size)
        at += size

    def add_small(name, value, offset=0):
        start = base[name][0] + offset
        cols = pl.ds(start, value.shape[1])
        small_ref[:, cols] = small_ref[:, cols] + value

    small_ref[...] = jnp.zeros(small_ref.shape, f32)
    dbias_ref[...] = jnp.zeros(dbias_ref.shape, f32)

    @pl.loop(0, rows_w // 64)
    def _(n):
        start = pl.multiple_of(n * 64, 64)
        to = lax.broadcasted_iota(jnp.int32, (64, rows8), 0) + start
        source = lax.broadcasted_iota(jnp.int32, (64, rows8), 1)
        hit = (to // pad == source % sub) & (to % pad == source // sub)
        perm_ref[pl.ds(start, 64), :] = hit.astype(f32).astype(bf16)

    @pl.loop(0, rows8 // 56)
    def _(n):
        start = pl.multiple_of(n * 56, 8)
        to = lax.broadcasted_iota(jnp.int32, (56, rows_w), 0) + start
        source = lax.broadcasted_iota(jnp.int32, (56, rows_w), 1)
        hit = (source // pad == to % sub) & (source % pad == to // sub)
        back_ref[pl.ds(start, 56), :] = hit.astype(f32).astype(bf16)

    def stacked(tile):
        return jnp.concatenate([tile * m for m in head_masks_half], axis=0)

    def diagonal(tall):
        total = tall[0:pad] * head_masks[0]
        for h in range(1, quad):
            total = total + tall[h * pad : (h + 1) * pad] * head_masks[h]
        return total

    def grow(values):
        return jnp.concatenate([values, jnp.zeros((pad - key_rows, values.shape[1]), f32)], axis=0)

    @pl.loop(0, groups)
    def _(g):
        win0 = pl.multiple_of(g * group, group)

        @pl.loop(0, tokens // step)
        def _(n):
            part = x_ref[pl.ds(n * step, step), pl.ds(win0, group), :].astype(f32)
            flat = part.reshape(step * group, width)
            normal, _ = norm_parts(flat)
            wide_ref[pl.ds(n * step, step)] = (normal * gain1_ref[...] + shift1_ref[...]).reshape(
                step, group, width
            )

        for s in range(2):
            g2 = g * 2 + s
            act8 = wide_ref[:, sub * s : sub * (s + 1), :].reshape(rows8, width).astype(bf16)
            act_w_ref[g2] = dot_nn(perm_ref[...], act8).astype(bf16)

            @pl.loop(0, 3 * width // chunk)
            def _(n):
                cols = pl.ds(pl.multiple_of(n * chunk, chunk), chunk)
                out = dot_nn(act_w_ref[g2], wqkv_ref[:, cols])
                qkv_ref[g2, :, cols] = (
                    (out + qkv_bias_ref[:, cols]) * qkv_scale_ref[:, cols]
                ).astype(bf16)

            @pl.loop(0, sub)
            def _(w):
                line = pl.ds(pl.multiple_of(w * pad, pad), pad)
                for t in range(quads):
                    q4 = qkv_ref[g2, line, 128 * t : 128 * (t + 1)]
                    k4 = qkv_ref[g2, line, width + 128 * t : width + 128 * (t + 1)]
                    v4 = qkv_ref[g2, line, 2 * width + 128 * t : 2 * width + 128 * (t + 1)]
                    scores = dot_nt(k4, stacked(q4))[0:key_rows] + bias_ref[t]
                    top = jnp.max(scores, axis=0, keepdims=True)
                    weight = jnp.exp(scores - top)
                    total = jnp.sum(weight, axis=0, keepdims=True)
                    lse_ref[g2, w, t : t + 1, :] = top + jnp.log(total)
                    probs = grow(weight * (1.0 / total)).astype(bf16)
                    mixed_w_ref[line, 128 * t : 128 * (t + 1)] = diagonal(dot_tn(probs, v4)).astype(
                        bf16
                    )

            wide_ref[:, sub * s : sub * (s + 1), :] = dot_nn(back_ref[...], mixed_w_ref[...]).reshape(
                tokens, sub, width
            )

        mixed_ref[:, pl.ds(win0, group), :] = wide_ref[...].astype(bf16)
        mixed = mixed_ref[:, pl.ds(win0, group), :].reshape(rows, width)
        for n in range(width // chunk):
            cols = slice(n * chunk, (n + 1) * chunk)
            out = dot_nn(mixed, wproj_ref[:, cols]) + proj_bias_ref[:, cols]
            dx_ref[:, pl.ds(win0, group), cols] = (
                x_ref[:, pl.ds(win0, group), cols].astype(f32) + out.reshape(tokens, group, chunk)
            )

    @pl.loop(0, groups)
    def _(g):
        win0 = pl.multiple_of(g * group, group)

        @pl.loop(0, tokens // step)
        def _(n):
            part = dx_ref[pl.ds(n * step, step), pl.ds(win0, group), :].reshape(step * group, width)
            normal, _ = norm_parts(part)
            lines = pl.ds(pl.multiple_of(n * step * group, step * group), step * group)
            sa_ref[lines, :] = (normal * gain2_ref[...] + shift2_ref[...]).astype(bf16)

        dy = dy_ref[:, pl.ds(win0, group), :].reshape(rows, width)
        sat_ref[...] = sa_ref[...].T
        dyt_ref[...] = dy.T

        @pl.loop(0, hidden // chunk)
        def _(n):
            start = pl.multiple_of(n * chunk, chunk)
            cols = pl.ds(start, chunk)
            u_ref[...] = dot_nn(sa_ref[...], w1_ref[:, cols])
            da_ref[...] = dot_nt(
                dy_ref[:, pl.ds(win0, group), :].reshape(rows, width), w2_ref[cols, :]
            )

            @pl.loop(0, tokens // step)
            def _(m):
                lines = pl.ds(pl.multiple_of(m * step * group, step * group), step * group)
                value, slope = gelu_pair(u_ref[lines, :] + hidden_bias_ref[:, cols])
                act_ref[lines, cols] = value.astype(bf16)
                dup = (da_ref[lines, :] * slope).astype(bf16)
                dup_ref[lines, cols] = dup
                add_small("hb", fold_rows(dup.astype(f32)), start)

            part1 = dot_nn(sat_ref[...], dup_ref[:, cols])
            part2 = dot_nn(dyt_ref[...], act_ref[:, cols])

            @pl.when(g == 0)
            def _():
                dw1_ref[:, cols] = part1
                dw2t_ref[:, cols] = part2

            @pl.when(g != 0)
            def _():
                dw1_ref[:, cols] += part1
                dw2t_ref[:, cols] += part2

        for n in range(width // chunk):
            cols = slice(n * chunk, (n + 1) * chunk)
            out = dot_nn(act_ref[...], w2_ref[:, cols]) + output_bias_ref[:, cols]
            y_ref[:, pl.ds(win0, group), cols] = (
                dx_ref[:, pl.ds(win0, group), cols] + out.reshape(tokens, group, chunk)
            ).astype(bf16)
            acc_ref[:, cols] = dot_nt(dup_ref[...], w1_ref[cols, :])

        @pl.loop(0, tokens // step)
        def _(n):
            lines = pl.ds(pl.multiple_of(n * step * group, step * group), step * group)
            normal, inverse = norm_parts(
                dx_ref[pl.ds(n * step, step), pl.ds(win0, group), :].reshape(step * group, width)
            )
            grad = acc_ref[lines, :]
            scaled = grad * gain2_ref[...]
            back = inverse * (
                scaled
                - jnp.mean(scaled, axis=-1, keepdims=True)
                - normal * jnp.mean(scaled * normal, axis=-1, keepdims=True)
            )
            cot = dy_ref[pl.ds(n * step, step), pl.ds(win0, group), :].astype(f32)
            cot = cot.reshape(step * group, width)
            total = cot + back
            dx_ref[pl.ds(n * step, step), pl.ds(win0, group), :] = total.reshape(step, group, width)
            sa_ref[lines, :] = total.astype(bf16)
            add_small("ob", fold_rows(cot))
            add_small("pb", fold_rows(total))
            add_small("g2", fold_rows(grad * normal))
            add_small("s2", fold_rows(grad))

        mixed = mixed_ref[:, pl.ds(win0, group), :].reshape(rows, width)
        part3 = dot_tn(mixed, sa_ref[...])

        @pl.when(g == 0)
        def _():
            dwproj_ref[...] = part3

        @pl.when(g != 0)
        def _():
            dwproj_ref[...] += part3

    @pl.loop(0, groups)
    def _(g):
        win0 = pl.multiple_of(g * group, group)
        wide_ref[...] = dx_ref[:, pl.ds(win0, group), :]
        for s in range(2):
            g2 = g * 2 + s
            half8 = wide_ref[:, sub * s : sub * (s + 1), :].reshape(rows8, width).astype(bf16)
            half_w = dot_nn(perm_ref[...], half8).astype(bf16)
            mixed_w_ref[...] = dot_nt(half_w, wproj_ref[...]).astype(bf16)

            @pl.loop(0, sub)
            def _(w):
                line = pl.ds(pl.multiple_of(w * pad, pad), pad)
                for t in range(quads):
                    cols_q = slice(128 * t, 128 * (t + 1))
                    cols_k = slice(width + 128 * t, width + 128 * (t + 1))
                    cols_v = slice(2 * width + 128 * t, 2 * width + 128 * (t + 1))
                    q4 = qkv_ref[g2, line, cols_q]
                    k4 = qkv_ref[g2, line, cols_k]
                    v4 = qkv_ref[g2, line, cols_v]
                    go4 = mixed_w_ref[line, cols_q]
                    queries = stacked(q4)
                    grads = stacked(go4)
                    scores = dot_nt(k4, queries)[0:key_rows] + bias_ref[t]
                    probs = jnp.exp(scores - lse_ref[g2, w, t : t + 1, :])
                    prob_grad = dot_nt(v4, grads)[0:key_rows]
                    delta = jnp.sum(probs * prob_grad, axis=0, keepdims=True)
                    score_grad = probs * (prob_grad - delta)
                    dbias_ref[t] += score_grad
                    prob_half = grow(probs).astype(bf16)
                    score_half = grow(score_grad).astype(bf16)
                    value_grad = dot_nn(prob_half, grads)
                    key_grad = dot_nn(score_half, queries)
                    query_grad = diagonal(dot_tn(score_half, k4)) * scale
                    add_small("qb", fold_rows(query_grad), 128 * t)
                    add_small("vb", fold_rows(value_grad), 128 * t)
                    qkv_ref[g2, line, cols_q] = query_grad.astype(bf16)
                    qkv_ref[g2, line, cols_k] = key_grad.astype(bf16)
                    qkv_ref[g2, line, cols_v] = value_grad.astype(bf16)

            @pl.loop(0, 3 * width // chunk)
            def _(n):
                cols = pl.ds(pl.multiple_of(n * chunk, chunk), chunk)
                part = dot_tn(act_w_ref[g2], qkv_ref[g2, :, cols])

                @pl.when(g2 == 0)
                def _():
                    dwqkv_ref[:, cols] = part

                @pl.when(g2 != 0)
                def _():
                    dwqkv_ref[:, cols] += part

            for n in range(width // chunk):
                cols = slice(n * chunk, (n + 1) * chunk)
                mixed_w_ref[:, cols] = dot_nt(qkv_ref[g2], wqkv_ref[cols, :]).astype(bf16)
            wide_ref[:, sub * s : sub * (s + 1), :] = dot_nn(back_ref[...], mixed_w_ref[...]).reshape(
                tokens, sub, width
            )

        @pl.loop(0, tokens // step)
        def _(n):
            part = x_ref[pl.ds(n * step, step), pl.ds(win0, group), :].astype(f32)
            normal, inverse = norm_parts(part.reshape(step * group, width))
            grad = wide_ref[pl.ds(n * step, step)].reshape(step * group, width)
            scaled = grad * gain1_ref[...]
            back = inverse * (
                scaled
                - jnp.mean(scaled, axis=-1, keepdims=True)
                - normal * jnp.mean(scaled * normal, axis=-1, keepdims=True)
            )
            dx_ref[pl.ds(n * step, step), pl.ds(win0, group), :] += back.reshape(step, group, width)
            add_small("g1", fold_rows(grad * normal))
            add_small("s1", fold_rows(grad))


def local_pass(x, dy, wqkv, wproj, w1, w2, vectors, bias, heads):
    tokens, windows, width = x.shape
    hidden = w1.shape[1]
    dims = (tokens, windows, width, heads, hidden)
    sub = 8
    pad = 64
    rows = tokens * 2 * sub
    small_size = 8 * width + hidden
    subs = windows // sub
    shapes = (
        jax.ShapeDtypeStruct(x.shape, bf16),
        jax.ShapeDtypeStruct(x.shape, f32),
        jax.ShapeDtypeStruct(wqkv.shape, f32),
        jax.ShapeDtypeStruct(wproj.shape, f32),
        jax.ShapeDtypeStruct(w1.shape, f32),
        jax.ShapeDtypeStruct((width, hidden), f32),
        jax.ShapeDtypeStruct((8, small_size), f32),
        jax.ShapeDtypeStruct(bias.shape, f32),
    )
    vmem = pl.BlockSpec(memory_space=pltpu.VMEM)
    return pl.pallas_call(
        functools.partial(compute_kernel, dims),
        out_shape=shapes,
        in_specs=[vmem] * 16,
        out_specs=[vmem] * len(shapes),
        scratch_shapes=[
            pltpu.VMEM((sub * pad, tokens * sub), bf16),
            pltpu.VMEM((tokens * sub, sub * pad), bf16),
            pltpu.VMEM((subs, sub * pad, width), bf16),
            pltpu.VMEM((subs, sub * pad, 3 * width), bf16),
            pltpu.VMEM((sub * pad, width), bf16),
            pltpu.VMEM(x.shape, bf16),
            pltpu.VMEM((subs, sub, heads // 4, 256), f32),
            pltpu.VMEM((tokens, 2 * sub, width), f32),
            pltpu.VMEM((rows, width), bf16),
            pltpu.VMEM((width, rows), bf16),
            pltpu.VMEM((width, rows), bf16),
            pltpu.VMEM((rows, 256), f32),
            pltpu.VMEM((rows, 256), f32),
            pltpu.VMEM((rows, hidden), bf16),
            pltpu.VMEM((rows, hidden), bf16),
            pltpu.VMEM((rows, width), f32),
        ],
        compiler_params=pltpu.CompilerParams(vmem_limit_bytes=67043328),
    )(x, dy, wqkv, wproj, w1, w2, *vectors, bias)


def on_device(
    block_input,
    out_grad,
    qkv_weight,
    query_bias,
    value_bias,
    proj_weight,
    proj_bias,
    hidden_weight,
    hidden_bias,
    output_weight,
    output_bias,
    first_gain,
    first_shift,
    second_gain,
    second_shift,
    bias_table,
    table_index,
):
    windows, tokens, width = block_input.shape
    table_rows, heads = bias_table.shape
    hidden = hidden_bias.shape[0]
    scale = (width // heads) ** (-0.5)
    pairs = tokens * tokens
    one_hot = (
        table_index.T.reshape(pairs, 1) == lax.broadcasted_iota(jnp.int32, (pairs, table_rows), 1)
    ).astype(f32)
    by_pair = jnp.dot(one_hot, bias_table, precision=lax.Precision.HIGHEST)
    by_key = by_pair.reshape(tokens, tokens, heads).transpose(0, 2, 1)
    by_key = jnp.pad(by_key, ((0, 0), (0, 0), (0, 64 - tokens)))
    by_key = jnp.pad(by_key, ((0, 56 - tokens), (0, 0), (0, 0)), constant_values=-1e30)
    quads = heads // 4
    bias = by_key.reshape(56, quads, 256).transpose(1, 0, 2)
    wqkv, wproj, w1, w2 = (
        lax.all_gather(w, "shard", axis=0, tiled=True)
        for w in (qkv_weight, proj_weight, hidden_weight, output_weight)
    )
    zeros = jnp.zeros((width,), f32)
    ones = jnp.ones((2 * width,), f32)
    vectors = [
        v.reshape(1, -1)
        for v in (
            jnp.concatenate([query_bias, zeros, value_bias]),
            jnp.concatenate([jnp.full((width,), scale, f32), ones]),
            proj_bias,
            hidden_bias,
            output_bias,
            first_gain,
            first_shift,
            second_gain,
            second_shift,
        )
    ]
    y, dx, dwqkv, dwproj, dw1, dw2t, small, dbias = local_pass(
        jnp.transpose(block_input, (1, 0, 2)),
        jnp.transpose(out_grad, (1, 0, 2)),
        wqkv,
        wproj,
        w1,
        w2,
        vectors,
        bias,
        heads,
    )
    dbias = dbias.transpose(1, 0, 2).reshape(56, heads, 64)[:tokens, :, :tokens]
    dbias = dbias.transpose(1, 0, 2).reshape(heads, pairs)
    bias_table_grad = jnp.dot(dbias, one_hot, precision=lax.Precision.HIGHEST).T
    shares = [
        lax.psum_scatter(g.astype(bf16), "shard", scatter_dimension=0, tiled=True)
        for g in (dwqkv, dwproj, dw1, dw2t.T)
    ]
    shares = [lax.psum(s, "rep").astype(f32) for s in shares]
    small, bias_table_grad = lax.psum(
        (jnp.sum(small, axis=0), bias_table_grad), ("shard", "rep")
    )
    cuts = [width, width, width, hidden, width, width, width, width, width]
    parts = []
    at = 0
    for size in cuts:
        parts.append(small[at : at + size])
        at += size
    qb, vb, pb, hb, ob, g1, s1, g2, s2 = parts
    return (
        jnp.transpose(y, (1, 0, 2)),
        jnp.transpose(dx, (1, 0, 2)),
        shares[0],
        qb,
        vb,
        shares[1],
        pb,
        shares[2],
        hb,
        shares[3],
        ob,
        g1,
        s1,
        g2,
        s2,
        bias_table_grad,
    )


def solution(mesh):
    rows = P(("shard", "rep"), None, None)
    cut = P("shard", None)
    full = P()
    return jax.shard_map(
        on_device,
        mesh=mesh,
        in_specs=(
            rows,
            rows,
            cut,
            full,
            full,
            cut,
            full,
            cut,
            full,
            cut,
            full,
            full,
            full,
            full,
            full,
            full,
            full,
        ),
        out_specs=(
            rows,
            rows,
            cut,
            full,
            full,
            cut,
            full,
            cut,
            full,
            cut,
            full,
            full,
            full,
            full,
            full,
            full,
        ),
        check_vma=False,
    )
```

time: 633 us -> 547 us (0.86); the launches traced: 625 us -> 546 us
  Pallas kernels: 0 us -> 235 us
  local copies, waits for them, and re-layouts: 210 us -> 6.82 us
  matrix products: 206 us -> 2.87 us
  waiting for transfers between devices: 65.2 us -> 217 us
  other arithmetic: 76.1 us -> 18.7 us
    pallas_call x0 -> x1, Pallas kernels: none -> 235 us  [local_pass(): pl.pallas_call(functools.partial(compute_kernel, dims), out_shape=shapes,...]
    dot_general x20 -> x2, matrix products: 206 us -> 2.87 us  [the longest x1 1.96 us: on_device(): by_pair = jnp.dot(one_hot, bias_table, precision=lax.Precision.HIGHEST)]
    reshape x16 -> x6, local copies, waits for them, and re-layouts: 135 us -> 2.08 us  [the longest x2 0.92 us: on_device(): bias = by_key.reshape(56, quads, 256).transpose(1, 0, 2)]
    reduce_scatter x4, waiting for transfers between devices: 39.3 us -> 108 us  [on_device(): lax.psum_scatter(g.astype(bf16), 'shard', scatter_dimension=0, tiled=True)]
    all_gather x3, waiting for transfers between devices: 0.02 us -> 56.9 us  [on_device(): lax.all_gather(w, 'shard', axis=0, tiled=True)]
    reduce_sum x9 -> x1, other arithmetic: 54.7 us -> 0.05 us  [on_device(): jnp.sum(small, axis=0)]
    psum x1, waiting for transfers between devices: 23.8 us -> 49.6 us  [on_device(): shares = [lax.psum(s, 'rep').astype(f32) for s in shares]]
    unnamed x123 -> x14, local copies, waits for them, and re-layouts: 24.9 us -> 2.33 us
  transfers between devices with their start and end apart: 8 -> 8, of which waited for: 3 -> 8; matrix products, arithmetic and copies ran while one was open for 52% -> 4% of each run, Pallas kernels for 0% -> 0%
where the time goes in v1:
time: 547 us; the launch traced here: 546 us
  Pallas kernels  235 us (43%)
  waiting for transfers between devices  217 us (40%)
  blocking collectives  52 us (10%)
  other arithmetic  18.7 us (3%)
  between operations  14.3 us (3%)
  local copies, waits for them, and re-layouts  6.82 us (1%)
    pallas_call x1, Pallas kernels, local_pass(): pl.pallas_call(functools.partial(compute_kernel, dims), out_shape=shapes,...  235 us
    reduce_scatter x4, waiting for transfers between devices, on_device(): lax.psum_scatter(g.astype(bf16), 'shard', scatter_dimension=0, tiled=True)  108 us
    all_gather x3, waiting for transfers between devices, on_device(): lax.all_gather(w, 'shard', axis=0, tiled=True)  56.9 us
    psum x1, waiting for transfers between devices, on_device(): shares = [lax.psum(s, 'rep').astype(f32) for s in shares]  49.6 us
    psum x1, blocking collectives, on_device(): lax.psum((jnp.sum(small, axis=0), bias_table_grad), ('shard', 'rep'))  42 us
    convert_element_type x4, other arithmetic, on_device(): g.astype(bf16)  13.2 us
  transfers between devices with their start and end apart: 8, of which 8 were waited for; matrix products, arithmetic and copies ran while one was open for 4% of the time, Pallas kernels for 0%

profile of v1, /device:TPU:0, one launch (start us, length us, event | category | flops | bytes accessed | tf_op | source)
XLA Modules:
  0.0 546.4 jit_solution(13366522487170430471)
XLA Ops:
  7.2 0.0 all-gather.4.cloned.1.call-start
  7.2 0.7 all-gather.4.cloned.1.call-update
  7.9 0.0 all-gather.6.cloned.1.call-start
  8.0 0.7 all-gather.6.cloned.1.call-update
  8.7 0.0 copy-start.3
  8.7 0.0 all-gather.8.cloned.1.call-start
  8.7 0.7 all-gather.8.cloned.1.call-update
  9.4 0.0 reduce-scatter.7.cloned.1.call-start
  9.5 0.7 pad_maximum_fusion
  10.2 0.6 reshape.70.qkv_bias_ref
  10.8 0.8 copy.34
  11.6 0.1 eq.10
  11.7 0.0 copy-start.4
  11.7 2.0 fusion.1
  13.7 0.2 reshape.78
  13.9 0.1 copy.41
  14.0 0.0 copy-done.4
  14.1 0.2 reshape.79
  14.3 0.7 copy.43
  15.0 0.0 copy-done.3
  15.0 10.0 %all_gather.13.wproj_ref = bf16[512,512]{1,0:T(8,128)(2,1)} all-gather(bf16[128,512]{1,0:T(8,128)(2,1)S(1)} %copy-done.3), channel_id=1, replica_groups=mesh['shard'=4,'rep'=8] {'shard'}, dimensions={0}, use_global_device_ids=true | all-gather | bytes 655360 | tf_op jit(solution)/shard_map/all_gather | solution.py:465
  25.0 7.7 %all-gather.4.cloned.1.call-done.wqkv_ref = bf16[512,1536]{1,0:T(8,128)(2,1)} async-done(((bf16[128,1536]{1,0:T(8,128)(2,1)}), bf16[512,1536]{1,0:T(8,128)(2,1)}) %all-gather.4.cloned.1.call-update) | async-done | bytes 1572880 | tf_op jit(solution)/shard_map/all_gather | solution.py:465
  32.7 25.0 %all-gather.6.cloned.1.call-done.w1_ref = bf16[512,2048]{1,0:T(8,128)(2,1)} async-done(((bf16[128,2048]{1,0:T(8,128)(2,1)}), bf16[512,2048]{1,0:T(8,128)(2,1)}) %all-gather.6.cloned.1.call-update) | async-done | bytes 2097168 | tf_op jit(solution)/shard_map/all_gather | solution.py:465
  57.7 24.2 %all-gather.8.cloned.1.call-done.w2_ref = bf16[2048,512]{1,0:T(8,128)(2,1)} async-done(((bf16[512,512]{1,0:T(8,128)(2,1)}), bf16[2048,512]{1,0:T(8,128)(2,1)}) %all-gather.8.cloned.1.call-update) | async-done | bytes 2097168 | tf_op jit(solution)/shard_map/all_gather | solution.py:465
  81.8 234.7 %shard_map.288 = (bf16[49,48,512]{2,1,0:T(8,128)(2,1)}, f32[49,48,512]{2,1,0:T(8,128)}, f32[512,1536]{1,0:T(8,128)}, f32[512,512]{1,0:T(8,128)}, f32[512,2048]{1...) custom-call(bf16[49,48,512]{2,1,0:T(8,128)(2,1)} %bitcast.25, ...), custom_call_target="tpu_custom_call" | custom-call | tf_op jit(solution)/shard_map/pallas_call | solution.py:404
  316.5 2.1 convert_element_type.32
  318.6 0.0 reduce-scatter.7.cloned.1.call-update
  318.6 0.0 reduce-scatter.5.cloned.1.call-start
  318.7 3.3 convert_element_type.30
  322.0 0.0 reduce-scatter.5.cloned.1.call-update
  322.0 0.0 reduce-scatter.9.cloned.1.call-start
  322.1 3.9 convert_element_type.34
  326.0 0.0 reduce-scatter.9.cloned.1.call-update
  326.0 0.0 reduce-scatter.11.cloned.1.call-start
  326.1 3.9 convert_bitcast_fusion
  330.0 0.0 copy-start.2
  330.0 0.0 copy-start.1
  330.0 0.0 reduce-scatter.11.cloned.1.call-update
  330.0 0.0 all-reduce.6.cloned.1.call-start
  330.0 10.4 %reduce-scatter.7.cloned.1.call-done = bf16[128,512]{1,0:T(8,128)(2,1)} async-done(((bf16[512,512]{1,0:T(8,128)(2,1)}), bf16[128,512]{1,0:T(8,128)(2,1)}) %reduce-scatter.7.cloned.1.call-update) | async-done | bytes 131088 | tf_op jit(solution)/shard_map/reduce_scatter | solution.py:499
  340.4 30.4 %reduce-scatter.5.cloned.1.call-done = bf16[128,1536]{1,0:T(8,128)(2,1)} async-done(((bf16[512,1536]{1,0:T(8,128)(2,1)}), bf16[128,1536]{1,0:T(8,128)(2,1)}) %reduce-scatter.5.cloned.1.call-update) | async-done | bytes 393232 | tf_op jit(solution)/shard_map/reduce_scatter | solution.py:499
  370.8 33.6 %reduce-scatter.9.cloned.1.call-done = bf16[128,2048]{1,0:T(8,128)(2,1)} async-done(((bf16[512,2048]{1,0:T(8,128)(2,1)}), bf16[128,2048]{1,0:T(8,128)(2,1)}) %reduce-scatter.9.cloned.1.call-update) | async-done | bytes 524304 | tf_op jit(solution)/shard_map/reduce_scatter | solution.py:499
  404.4 33.7 %reduce-scatter.11.cloned.1.call-done = bf16[512,512]{0,1:T(8,128)(2,1)} async-done(((bf16[2048,512]{0,1:T(8,128)(2,1)}), bf16[512,512]{0,1:T(8,128)(2,1)}) %reduce-scatter.11.cloned.1.call-update) | async-done | bytes 524304 | tf_op jit(solution)/shard_map/reduce_scatter | solution.py:499
  438.2 0.0 copy-start.5
  438.2 0.0 all-reduce.6.cloned.1.call-update
  438.2 0.0 copy-done.2
  438.2 0.1 reduce_sum.9
  438.3 0.0 copy-done.1
  438.3 0.1 copy.37
  438.4 0.2 reshape.80
  438.6 0.1 copy.38
  438.7 0.2 reshape.81
  438.9 0.0 copy-done.5
  438.9 0.9 fusion
  439.8 42.0 %all-reduce.2 = (f32[6144]{0:T(1024)S(1)}, f32[169,16]{0,1:T(8,128)}) all-reduce(f32[6144]{0:T(1024)S(1)} %reduce_sum.9, f32[169,16]{0,1:T(8,128)S(1)} %fusion), channel_id=1, replica_groups=mesh['shard'=4,'rep'=8] {'shard','rep'}, use_global_device_ids=true, to_apply=%region_3.4 | all-reduce | flops 8848 | bytes 70784 | tf_op jit(solution)/shard_map/psum | solution.py:503
  481.8 0.6 slice.43
  482.4 0.6 fusion.4
  483.0 49.6 %all-reduce.6.cloned.1.call-done = (bf16[512,512]{0,1:T(8,128)(2,1)}, bf16[128,1536]{1,0:T(8,128)(2,1)}, bf16[128,512]{1,0:T(8,128)(2,1)}, bf16[128,2048]{1,0:T(8,128)(2,1)}) async-done(((bf16[512,512]{0,1:T(8,128)(2,1)}, bf16[128,1536]{1,0:T(8,128)(2,1)}, bf16[128,512]{1,0:T(8,128)(2,1)}, bf16[128,2048]{1,0:T(8,128)(2,1)}), (bf16[512,512]{0,1:T(8,128)(2,1)}, bf16[128,1536]{1,0:T(8,128)(2,1)}, ...) | async-done | bytes 1572880 | tf_op jit(solution)/shard_map/psum | solution.py:502
  532.6 0.0 copy-start
  532.6 1.7 convert_element_type.33
  534.3 2.2 copy.39
  536.6 2.0 convert_element_type.31
  538.5 0.0 copy-done
  538.5 1.1 convert_element_type.35
  (3 shorter events, 0.1 us)
Async XLA Ops:
  7.2 25.5 %all-gather.4.cloned.1.call-start = ((), (), s32[]{:S(2)}) async-start(), calls=%async_computation.4 | async-start | bytes 1966080 | tf_op jit(solution)/shard_map/all_gather | solution.py:465
  7.9 49.8 %all-gather.6.cloned.1.call-start = ((), (), s32[]{:S(2)}) async-start(), calls=%async_computation.5 | async-start | bytes 2621440 | tf_op jit(solution)/shard_map/all_gather | solution.py:465
  8.7 6.3 %copy-start.3 = (bf16[128,512]{1,0:T(8,128)(2,1)S(1)}, bf16[128,512]{1,0:T(8,128)(2,1)}, u32[]{:S(2)}) copy-start(bf16[128,512]{1,0:T(8,128)(2,1)} %param.22) | copy-start | bytes 393220
  8.7 73.2 %all-gather.8.cloned.1.call-start = ((), (), s32[]{:S(2)}) async-start(), calls=%async_computation.6 | async-start | bytes 2621440 | tf_op jit(solution)/shard_map/all_gather | solution.py:465
  9.4 331.0 %reduce-scatter.7.cloned.1.call-start = ((), (), s32[]{:S(2)}) async-start(), calls=%async_computation.8 | async-start | bytes 655360 | tf_op jit(solution)/shard_map/reduce_scatter | solution.py:499
  11.7 2.3 copy-start.4
  318.6 52.2 %reduce-scatter.5.cloned.1.call-start = ((), (), s32[]{:S(2)}) async-start(), calls=%async_computation.7 | async-start | bytes 1966080 | tf_op jit(solution)/shard_map/reduce_scatter | solution.py:499
  322.0 82.4 %reduce-scatter.9.cloned.1.call-start = ((), (), s32[]{:S(2)}) async-start(), calls=%async_computation.9 | async-start | bytes 2621440 | tf_op jit(solution)/shard_map/reduce_scatter | solution.py:499
  326.0 112.2 %reduce-scatter.11.cloned.1.call-start = ((), (), s32[]{:S(2)}) async-start(), calls=%async_computation.10 | async-start | bytes 2621440 | tf_op jit(solution)/shard_map/reduce_scatter | solution.py:499
  330.0 108.2 %copy-start.2 = (f32[8,6144]{1,0:T(8,128)S(1)}, f32[8,6144]{1,0:T(8,128)}, u32[]{:S(2)}) copy-start(f32[8,6144]{1,0:T(8,128)} %get-tuple-element.27) | copy-start | bytes 589828
  330.0 108.3 %copy-start.1 = (f32[4,56,256]{2,1,0:T(8,128)S(1)}, f32[4,56,256]{2,1,0:T(8,128)}, u32[]{:S(2)}) copy-start(f32[4,56,256]{2,1,0:T(8,128)} %get-tuple-element.31) | copy-start | bytes 688132
  330.0 202.7 %all-reduce.6.cloned.1.call-start = ((), (), s32[]{:S(2)}) async-start(), calls=%async_computation.11 | async-start | bytes 3145728 | tf_op jit(solution)/shard_map/psum | solution.py:502
  438.2 0.7 copy-start.5
  532.6 5.9 %copy-start = (bf16[128,2048]{1,0:T(8,128)(2,1)S(1)}, bf16[128,2048]{1,0:T(8,128)(2,1)}, u32[]{:S(2)}) copy-start(bf16[128,2048]{1,0:T(8,128)(2,1)} %get-tuple-element.69) | copy-start | bytes 1572868
Sparse Core Ops, SparseCore 0:
  9.5 23.0 all-gather.3
  34.2 23.3 all-gather.5
  59.3 22.5 all-gather.7
  318.7 21.6 reduce-scatter.6
  342.8 27.9 reduce-scatter.4
  373.2 31.1 reduce-scatter.8
  407.0 31.1 reduce-scatter.10
  442.0 90.6 all-reduce.5

commit v2 on v1

--- a/solution.py
+++ b/solution.py
@@ -51,10 +51,10 @@
     dims,
     x_ref,
     dy_ref,
-    wqkv_ref,
-    wproj_ref,
-    w1_ref,
-    w2_ref,
+    wqkv_shard,
+    wproj_shard,
+    w1_shard,
+    w2_shard,
     qkv_bias_ref,
     qkv_scale_ref,
     proj_bias_ref,
@@ -89,8 +89,95 @@
     act_ref,
     dup_ref,
     acc_ref,
+    wqkv_ref,
+    wproj_ref,
+    w1_ref,
+    w2_ref,
+    own_sem,
+    pair_send,
+    pair_recv,
+    chip_send,
+    chip_recv,
 ):
-    tokens, windows, width, heads, hidden = dims
+    tokens, windows, width, heads, hidden, shards = dims
+    me = lax.axis_index("shard")
+    chips = shards // 2
+    core = lax.rem(me, 2)
+    chip = me // 2
+    pair = chip * 2 + 1 - core
+
+    def block(ref, index):
+        size = ref.shape[0] // shards
+        return ref.at[pl.ds(pl.multiple_of(index * size, size), size), :]
+
+    def peer(k):
+        return lax.rem(chip + k, chips) * 2 + core
+
+    def owner(k, side):
+        return lax.rem(chip + chips - k, chips) * 2 + side
+
+    gathers = (
+        (wqkv_shard, wqkv_ref),
+        (wproj_shard, wproj_ref),
+        (w1_shard, w1_ref),
+        (w2_shard, w2_ref),
+    )
+
+    def own_copy(i):
+        shard, full = gathers[i]
+        return pltpu.make_async_copy(shard, block(full, me), own_sem.at[i])
+
+    def chip_copy(i, k):
+        shard, full = gathers[i]
+        return pltpu.make_async_remote_copy(
+            src_ref=shard,
+            dst_ref=block(full, me),
+            send_sem=chip_send.at[i, k - 1],
+            recv_sem=chip_recv.at[i, k - 1],
+            device_id={"shard": peer(k)},
+            device_id_type=pl.DeviceIdType.MESH,
+        )
+
+    def pair_copy(i, k):
+        shard, full = gathers[i]
+        return pltpu.make_async_remote_copy(
+            src_ref=shard if k == 0 else block(full, owner(k, core)),
+            dst_ref=block(full, owner(k, core)),
+            send_sem=pair_send.at[i, k],
+            recv_sem=pair_recv.at[i, k],
+            device_id={"shard": pair},
+            device_id_type=pl.DeviceIdType.MESH,
+        )
+
+    def gather_start(i):
+        own_copy(i).start()
+        for k in range(1, chips):
+            chip_copy(i, k).start()
+        pair_copy(i, 0).start()
+
+    def gather_finish(i):
+        for k in range(1, chips):
+            chip_copy(i, k).wait_recv()
+            pair_copy(i, k).start()
+        own_copy(i).wait()
+        for k in range(chips):
+            pair_copy(i, k).wait_recv()
+
+    def gather_drain(i):
+        for k in range(1, chips):
+            chip_copy(i, k).wait_send()
+        for k in range(chips):
+            pair_copy(i, k).wait_send()
+
+    barrier = pltpu.get_barrier_semaphore()
+    for target in [pair] + [peer(k) for k in range(1, chips)]:
+        pl.semaphore_signal(
+            barrier, inc=1, device_id={"shard": target}, device_id_type=pl.DeviceIdType.MESH
+        )
+    pl.semaphore_wait(barrier, chips)
+    gather_start(0)
+    gather_start(1)
+
     head_size = width // heads
     scale = head_size ** (-0.5)
     pad = 64
@@ -178,6 +265,14 @@
             g2 = g * 2 + s
             act8 = wide_ref[:, sub * s : sub * (s + 1), :].reshape(rows8, width).astype(bf16)
             act_w_ref[g2] = dot_nn(perm_ref[...], act8).astype(bf16)
+            if s == 0:
+
+                @pl.when(g == 0)
+                def _():
+                    gather_finish(0)
+                    gather_finish(1)
+                    gather_start(2)
+                    gather_start(3)
 
             @pl.loop(0, 3 * width // chunk)
             def _(n):
@@ -216,6 +311,11 @@
             dx_ref[:, pl.ds(win0, group), cols] = (
                 x_ref[:, pl.ds(win0, group), cols].astype(f32) + out.reshape(tokens, group, chunk)
             )
+
+    gather_finish(2)
+    gather_finish(3)
+    for i in range(4):
+        gather_drain(i)
 
     @pl.loop(0, groups)
     def _(g):
@@ -381,10 +481,11 @@
             add_small("s1", fold_rows(grad))
 
 
-def local_pass(x, dy, wqkv, wproj, w1, w2, vectors, bias, heads):
+def local_pass(x, dy, wqkv, wproj, w1, w2, vectors, bias, heads, shards):
     tokens, windows, width = x.shape
     hidden = w1.shape[1]
-    dims = (tokens, windows, width, heads, hidden)
+    dims = (tokens, windows, width, heads, hidden, shards)
+    chips = shards // 2
     sub = 8
     pad = 64
     rows = tokens * 2 * sub
@@ -393,9 +494,9 @@
     shapes = (
         jax.ShapeDtypeStruct(x.shape, bf16),
         jax.ShapeDtypeStruct(x.shape, f32),
-        jax.ShapeDtypeStruct(wqkv.shape, f32),
-        jax.ShapeDtypeStruct(wproj.shape, f32),
-        jax.ShapeDtypeStruct(w1.shape, f32),
+        jax.ShapeDtypeStruct((width, 3 * width), f32),
+        jax.ShapeDtypeStruct((width, width), f32),
+        jax.ShapeDtypeStruct((width, hidden), f32),
         jax.ShapeDtypeStruct((width, hidden), f32),
         jax.ShapeDtypeStruct((8, small_size), f32),
         jax.ShapeDtypeStruct(bias.shape, f32),
@@ -404,7 +505,7 @@
     return pl.pallas_call(
         functools.partial(compute_kernel, dims),
         out_shape=shapes,
-        in_specs=[vmem] * 16,
+        in_specs=[vmem] * 2 + [pl.BlockSpec(memory_space=pl.ANY)] * 4 + [vmem] * 10,
         out_specs=[vmem] * len(shapes),
         scratch_shapes=[
             pltpu.VMEM((sub * pad, tokens * sub), bf16),
@@ -423,12 +524,24 @@
             pltpu.VMEM((rows, hidden), bf16),
             pltpu.VMEM((rows, hidden), bf16),
             pltpu.VMEM((rows, width), f32),
+            pltpu.VMEM((width, 3 * width), bf16),
+            pltpu.VMEM((width, width), bf16),
+            pltpu.VMEM((width, hidden), bf16),
+            pltpu.VMEM((hidden, width), bf16),
+            pltpu.SemaphoreType.DMA((4,)),
+            pltpu.SemaphoreType.DMA((4, chips)),
+            pltpu.SemaphoreType.DMA((4, chips)),
+            pltpu.SemaphoreType.DMA((4, chips - 1)),
+            pltpu.SemaphoreType.DMA((4, chips - 1)),
         ],
-        compiler_params=pltpu.CompilerParams(vmem_limit_bytes=67043328),
+        compiler_params=pltpu.CompilerParams(
+            vmem_limit_bytes=67043328, collective_id=0, has_side_effects=True
+        ),
     )(x, dy, wqkv, wproj, w1, w2, *vectors, bias)
 
 
 def on_device(
+    shards,
     block_input,
     out_grad,
     qkv_weight,
@@ -461,10 +574,6 @@
     by_key = jnp.pad(by_key, ((0, 56 - tokens), (0, 0), (0, 0)), constant_values=-1e30)
     quads = heads // 4
     bias = by_key.reshape(56, quads, 256).transpose(1, 0, 2)
-    wqkv, wproj, w1, w2 = (
-        lax.all_gather(w, "shard", axis=0, tiled=True)
-        for w in (qkv_weight, proj_weight, hidden_weight, output_weight)
-    )
     zeros = jnp.zeros((width,), f32)
     ones = jnp.ones((2 * width,), f32)
     vectors = [
@@ -484,13 +593,14 @@
     y, dx, dwqkv, dwproj, dw1, dw2t, small, dbias = local_pass(
         jnp.transpose(block_input, (1, 0, 2)),
         jnp.transpose(out_grad, (1, 0, 2)),
-        wqkv,
-        wproj,
-        w1,
-        w2,
+        qkv_weight,
+        proj_weight,
+        hidden_weight,
+        output_weight,
         vectors,
         bias,
         heads,
+        shards,
     )
     dbias = dbias.transpose(1, 0, 2).reshape(56, heads, 64)[:tokens, :, :tokens]
     dbias = dbias.transpose(1, 0, 2).reshape(heads, pairs)
@@ -535,7 +645,7 @@
     cut = P("shard", None)
     full = P()
     return jax.shard_map(
-        on_device,
+        functools.partial(on_device, mesh.shape["shard"]),
         mesh=mesh,
         in_specs=(
             rows,

time: 547 us -> 501 us (0.916)
  waiting for transfers between devices: 217 us -> 160 us
  Pallas kernels: 235 us -> 251 us
  blocking collectives: 52 us -> 41.8 us
  local copies, waits for them, and re-layouts: 6.82 us -> 14.6 us
    all_gather x3 -> x0, waiting for transfers between devices: 56.9 us -> none  [on_device(): lax.all_gather(w, 'shard', axis=0, tiled=True)]
    pallas_call x1, Pallas kernels: 235 us -> 251 us  [local_pass(): pl.pallas_call(functools.partial(compute_kernel, dims), out_shape=shapes,...]
    all_gather x1 -> x0, blocking collectives: 9.99 us -> none  [on_device(): lax.all_gather(w, 'shard', axis=0, tiled=True)]
    unnamed x14 -> x22, local copies, waits for them, and re-layouts: 2.33 us -> 10.1 us
  transfers between devices with their start and end apart: 8 -> 5, of which waited for: 8 -> 5; matrix products, arithmetic and copies ran while one was open for 4% -> 3% of each run, Pallas kernels for 0% -> 0%
where the time goes in v2:
time: 501 us
  Pallas kernels  251 us (50%)
  waiting for transfers between devices  160 us (32%)
  blocking collectives  41.8 us (8%)
  other arithmetic  17 us (3%)
  local copies, waits for them, and re-layouts  14.6 us (3%)
  between operations  13.9 us (3%)
    pallas_call x1, Pallas kernels, local_pass(): pl.pallas_call(functools.partial(compute_kernel, dims), out_shape=shapes,...  251 us
    reduce_scatter x4, waiting for transfers between devices, on_device(): lax.psum_scatter(g.astype(bf16), 'shard', scatter_dimension=0, tiled=True)  111 us
    psum x1, waiting for transfers between devices, on_device(): shares = [lax.psum(s, 'rep').astype(f32) for s in shares]  49.1 us
    psum x1, blocking collectives, on_device(): lax.psum((jnp.sum(small, axis=0), bias_table_grad), ('shard', 'rep'))  41.8 us
    convert_element_type x4, other arithmetic, on_device(): g.astype(bf16)  13.1 us
    unnamed x22, local copies, waits for them, and re-layouts  10.1 us
  transfers between devices with their start and end apart: 5, of which 5 were waited for; matrix products, arithmetic and copies ran while one was open for 3% of the time, Pallas kernels for 0%

profile of v2, /device:TPU:0, one launch (start us, length us, event | category | flops | bytes accessed | tf_op | source)
XLA Modules:
  0.0 500.9 jit_solution(15928262186060519419)
XLA Ops:
  7.2 0.0 copy-start.8
  7.2 0.0 copy-start.7
  7.2 0.0 reduce-scatter.7.cloned.1.call-start
  7.2 0.8 copy.34
  8.1 0.1 eq.10
  8.2 0.0 copy-start.5
  8.2 0.6 copy-done.5
  8.8 2.0 fusion.1
  10.8 0.2 reshape.78
  11.0 0.1 copy.41
  11.1 0.2 reshape.79
  11.3 0.7 copy.43
  12.0 0.0 copy-done.8
  12.0 0.0 copy-done.7
  12.1 0.6 reshape.70.qkv_bias_ref
  12.7 250.7 %shard_map.288 = (bf16[49,48,512]{2,1,0:T(8,128)(2,1)}, f32[49,48,512]{2,1,0:T(8,128)}, f32[512,1536]{1,0:T(8,128)}, f32[512,512]{1,0:T(8,128)}, f32[512,2048]{1...) custom-call(bf16[49,48,512]{2,1,0:T(8,128)(2,1)} %bitcast.26, ...), custom_call_target="tpu_custom_call" | custom-call | tf_op jit(solution)/shard_map/pallas_call | solution.py:505
  263.3 2.1 convert_element_type.32
  265.4 0.0 reduce-scatter.7.cloned.1.call-update
  265.4 0.0 reduce-scatter.5.cloned.1.call-start
  265.5 3.2 convert_element_type.30
  268.7 0.0 reduce-scatter.5.cloned.1.call-update
  268.7 0.0 reduce-scatter.11.cloned.1.call-start
  268.8 3.8 convert_bitcast_fusion
  272.6 0.0 reduce-scatter.11.cloned.1.call-update
  272.6 0.0 reduce-scatter.9.cloned.1.call-start
  272.7 4.0 convert_element_type.34
  276.6 0.0 copy-start.2
  276.6 0.0 reduce-scatter.9.cloned.1.call-update
  276.7 0.0 all-reduce.6.cloned.1.call-start
  276.7 11.4 %reduce-scatter.7.cloned.1.call-done = bf16[128,512]{1,0:T(8,128)(2,1)} async-done(((bf16[512,512]{1,0:T(8,128)(2,1)}), bf16[128,512]{1,0:T(8,128)(2,1)}) %reduce-scatter.7.cloned.1.call-update) | async-done | bytes 131088 | tf_op jit(solution)/shard_map/reduce_scatter | solution.py:609
  288.1 30.6 %reduce-scatter.5.cloned.1.call-done = bf16[128,1536]{1,0:T(8,128)(2,1)} async-done(((bf16[512,1536]{1,0:T(8,128)(2,1)}), bf16[128,1536]{1,0:T(8,128)(2,1)}) %reduce-scatter.5.cloned.1.call-update) | async-done | bytes 393232 | tf_op jit(solution)/shard_map/reduce_scatter | solution.py:609
  318.7 34.3 %reduce-scatter.11.cloned.1.call-done = bf16[512,512]{0,1:T(8,128)(2,1)} async-done(((bf16[2048,512]{0,1:T(8,128)(2,1)}), bf16[512,512]{0,1:T(8,128)(2,1)}) %reduce-scatter.11.cloned.1.call-update) | async-done | bytes 524304 | tf_op jit(solution)/shard_map/reduce_scatter | solution.py:609
  353.1 34.2 %reduce-scatter.9.cloned.1.call-done = bf16[128,2048]{1,0:T(8,128)(2,1)} async-done(((bf16[512,2048]{1,0:T(8,128)(2,1)}), bf16[128,2048]{1,0:T(8,128)(2,1)}) %reduce-scatter.9.cloned.1.call-update) | async-done | bytes 524304 | tf_op jit(solution)/shard_map/reduce_scatter | solution.py:609
  387.3 0.0 copy-start.3
  387.3 0.0 copy-start.6
  387.3 0.0 all-reduce.6.cloned.1.call-update
  387.3 0.0 copy-done.2
  387.3 0.1 copy.37
  387.4 0.2 reshape.80
  387.6 0.1 copy.38
  387.8 0.2 reshape.81
  387.9 0.3 copy-done.3
  388.2 0.1 reduce_sum.9
  388.2 0.0 copy-done.6
  388.2 0.9 fusion
  389.2 0.0 copy-start
  389.2 41.8 %all-reduce.2 = (f32[6144]{0:T(1024)S(1)}, f32[169,16]{0,1:T(8,128)}) all-reduce(f32[6144]{0:T(1024)S(1)} %reduce_sum.9, f32[169,16]{0,1:T(8,128)S(1)} %fusion), channel_id=1, replica_groups=mesh['shard'=4,'rep'=8] {'shard','rep'}, use_global_device_ids=true, to_apply=%region_3.4 | all-reduce | flops 8848 | bytes 70784 | tf_op jit(solution)/shard_map/psum | solution.py:613
  431.0 0.6 slice.43
  431.6 0.6 fusion.4
  432.2 49.1 %all-reduce.6.cloned.1.call-done = (bf16[512,512]{0,1:T(8,128)(2,1)}, bf16[128,1536]{1,0:T(8,128)(2,1)}, bf16[128,512]{1,0:T(8,128)(2,1)}, bf16[128,2048]{1,0:T(8,128)(2,1)}) async-done(((bf16[512,512]{0,1:T(8,128)(2,1)}, bf16[128,1536]{1,0:T(8,128)(2,1)}, bf16[128,512]{1,0:T(8,128)(2,1)}, bf16[128,2048]{1,0:T(8,128)(2,1)}), (bf16[512,512]{0,1:T(8,128)(2,1)}, bf16[128,1536]{1,0:T(8,128)(2,1)}, ...) | async-done | bytes 1572880 | tf_op jit(solution)/shard_map/psum | solution.py:612
  481.3 0.0 copy-start.1
  481.3 0.0 copy-start.4
  481.3 2.2 convert_element_type.35
  483.5 2.2 copy.39
  485.7 0.0 copy-done.1
  485.7 1.0 convert_element_type.31
  486.7 0.0 copy-done.4
  486.7 0.7 convert_element_type.33
  487.4 0.0 copy-done
  487.4 1.4 copy.50
  488.8 5.5 %copy.51 = f32[48,49,512]{2,0,1:T(8,128)} copy(f32[48,49,512]{2,0,1:T(8,128)} %bitcast.25) | data formatting | bytes 9633792
  (4 shorter events, 0.1 us)
Async XLA Ops:
  7.2 4.9 copy-start.8
  7.2 4.9 copy-start.7
  7.2 280.9 %reduce-scatter.7.cloned.1.call-start = ((), (), s32[]{:S(2)}) async-start(), calls=%async_computation.5 | async-start | bytes 655360 | tf_op jit(solution)/shard_map/reduce_scatter | solution.py:609
  8.2 0.6 copy-start.5
  265.4 53.3 %reduce-scatter.5.cloned.1.call-start = ((), (), s32[]{:S(2)}) async-start(), calls=%async_computation.4 | async-start | bytes 1966080 | tf_op jit(solution)/shard_map/reduce_scatter | solution.py:609
  268.7 84.4 %reduce-scatter.11.cloned.1.call-start = ((), (), s32[]{:S(2)}) async-start(), calls=%async_computation.7 | async-start | bytes 2621440 | tf_op jit(solution)/shard_map/reduce_scatter | solution.py:609
  272.6 114.6 %reduce-scatter.9.cloned.1.call-start = ((), (), s32[]{:S(2)}) async-start(), calls=%async_computation.6 | async-start | bytes 2621440 | tf_op jit(solution)/shard_map/reduce_scatter | solution.py:609
  276.6 110.6 %copy-start.2 = (f32[4,56,256]{2,1,0:T(8,128)S(1)}, f32[4,56,256]{2,1,0:T(8,128)}, u32[]{:S(2)}) copy-start(f32[4,56,256]{2,1,0:T(8,128)} %get-tuple-element.31) | copy-start | bytes 688132
  276.7 204.6 %all-reduce.6.cloned.1.call-start = ((), (), s32[]{:S(2)}) async-start(), calls=%async_computation.8 | async-start | bytes 3145728 | tf_op jit(solution)/shard_map/psum | solution.py:612
  387.3 0.9 copy-start.3
  387.3 1.0 copy-start.6
  389.2 98.3 %copy-start = (bf16[49,48,512]{2,1,0:T(8,128)(2,1)S(1)}, bf16[49,48,512]{2,1,0:T(8,128)(2,1)}, u32[]{:S(2)}) copy-start(bf16[49,48,512]{2,1,0:T(8,128)(2,1)} %get-tuple-element.24) | copy-start | bytes 7225348
  481.3 4.4 copy-start.1
  481.3 5.4 %copy-start.4 = (bf16[128,512]{1,0:T(8,128)(2,1)S(1)}, bf16[128,512]{1,0:T(8,128)(2,1)}, u32[]{:S(2)}) copy-start(bf16[128,512]{1,0:T(8,128)(2,1)} %get-tuple-element.68) | copy-start | bytes 393220
Sparse Core Ops, SparseCore 0:
  265.6 22.5 reduce-scatter.6
  290.7 28.0 reduce-scatter.4
  321.8 31.1 reduce-scatter.10
  356.0 31.1 reduce-scatter.8
  390.9 90.3 all-reduce.5

commit v3 on v2

--- a/solution.py
+++ b/solution.py
@@ -49,14 +49,14 @@
 
 def compute_kernel(
     dims,
-    x_ref,
-    dy_ref,
+    x_hbm,
+    dy_hbm,
     wqkv_shard,
     wproj_shard,
     w1_shard,
     w2_shard,
-    qkv_bias_ref,
-    qkv_scale_ref,
+    query_bias_ref,
+    value_bias_ref,
     proj_bias_ref,
     hidden_bias_ref,
     output_bias_ref,
@@ -64,7 +64,16 @@
     shift1_ref,
     gain2_ref,
     shift2_ref,
-    bias_ref,
+    table_ref,
+    index_ref,
+    y_hbm,
+    dx_hbm,
+    mixed_hbm,
+    work0_ref,
+    work1_ref,
+    work2_ref,
+    total_ref,
+    in_ref,
     y_ref,
     dx_ref,
     dwqkv_ref,
@@ -73,6 +82,7 @@
     dw2t_ref,
     small_ref,
     dbias_ref,
+    bias_ref,
     perm_ref,
     back_ref,
     act_w_ref,
@@ -84,22 +94,47 @@
     sa_ref,
     sat_ref,
     dyt_ref,
-    u_ref,
+    u0_ref,
+    u1_ref,
     da_ref,
     act_ref,
     dup_ref,
-    acc_ref,
     wqkv_ref,
     wproj_ref,
     w1_ref,
     w2_ref,
+    out0_ref,
+    in0_ref,
+    in1_ref,
+    in2_ref,
+    far0_ref,
+    far1_ref,
+    far2_ref,
+    half0_ref,
+    half1_ref,
+    half2_ref,
+    total_in_ref,
     own_sem,
     pair_send,
     pair_recv,
     chip_send,
     chip_recv,
+    load_sem,
+    y_sem,
+    mixed_sem,
+    dx_sem,
+    core_send,
+    core_recv,
+    far_send,
+    far_recv,
+    half_send,
+    half_recv,
+    join_send,
+    join_recv,
+    total_send,
+    total_recv,
 ):
-    tokens, windows, width, heads, hidden, shards = dims
+    tokens, windows, width, heads, hidden, shards, reps = dims
     me = lax.axis_index("shard")
     chips = shards // 2
     core = lax.rem(me, 2)
@@ -169,12 +204,25 @@
         for k in range(chips):
             pair_copy(i, k).wait_send()
 
+    rep = lax.axis_index("rep")
+    bits = reps.bit_length() - 1
+
+    def rep_bit(b):
+        return lax.rem(rep // (1 << b), 2)
+
+    def rep_peer(b):
+        return rep + (1 - 2 * rep_bit(b)) * (1 << b)
+
     barrier = pltpu.get_barrier_semaphore()
     for target in [pair] + [peer(k) for k in range(1, chips)]:
         pl.semaphore_signal(
             barrier, inc=1, device_id={"shard": target}, device_id_type=pl.DeviceIdType.MESH
         )
-    pl.semaphore_wait(barrier, chips)
+    for b in range(bits):
+        pl.semaphore_signal(
+            barrier, inc=1, device_id={"rep": rep_peer(b)}, device_id_type=pl.DeviceIdType.MESH
+        )
+    pl.semaphore_wait(barrier, chips + bits)
     gather_start(0)
     gather_start(1)
 
@@ -217,6 +265,211 @@
         cols = pl.ds(start, value.shape[1])
         small_ref[:, cols] = small_ref[:, cols] + value
 
+    def load(source, g, slot):
+        return pltpu.make_async_copy(
+            source.at[:, pl.ds(pl.multiple_of(g * group, group), group), :],
+            in_ref.at[slot],
+            load_sem.at[slot],
+        )
+
+    def store(source, target, g, sem):
+        return pltpu.make_async_copy(
+            source, target.at[:, pl.ds(pl.multiple_of(g * group, group), group), :], sem
+        )
+
+    def mixed_load(g):
+        return pltpu.make_async_copy(
+            mixed_hbm.at[:, pl.ds(pl.multiple_of(g * group, group), group), :], mixed_ref, mixed_sem
+        )
+
+    load(x_hbm, 0, 0).start()
+
+    parts = hidden // (shards * chunk)
+    owned = width // shards
+    works = (work0_ref, work1_ref, work2_ref)
+    ins = (in0_ref, in1_ref, in2_ref)
+    fars = (far0_ref, far1_ref, far2_ref)
+    halves = (half0_ref, half1_ref, half2_ref)
+
+    def unit_pieces(u, s):
+        own = pl.ds(pl.multiple_of(s * owned, owned), owned)
+        if u == 2:
+            for i in range(3):
+                cols = slice(width * i, width * (i + 1))
+                yield owned * i, owned, 0, width, (lambda cols=cols: dwqkv_ref[own, cols])
+            return
+        per = width // chunk
+        for i in range(shards):
+            n = i * parts + u
+            cols = slice(n * chunk, (n + 1) * chunk)
+            yield (
+                owned * (i // per),
+                owned,
+                chunk * (i % per),
+                chunk,
+                (lambda cols=cols: dw1_ref[own, cols]),
+            )
+        at_row = owned * (shards // per)
+        lanes = pl.ds(pl.multiple_of((s * parts + u) * chunk, chunk), chunk)
+        yield at_row, chunk, 0, width, (lambda: dw2t_ref[:, lanes].T)
+        if u == 1:
+            yield at_row + chunk, owned, 0, width, (lambda: dwproj_ref[own, :])
+
+    def unit_out(u, j):
+        rows_u = works[u].shape[0]
+        if u == 0:
+            return mixed_w_ref.at[0:rows_u] if j == 0 else out0_ref.at[j - 1]
+        first = 0 if u == 1 else chips * width
+        return act_ref.at[0:rows_u, first + j * width : first + (j + 1) * width]
+
+    def core_copy(u, j):
+        return pltpu.make_async_remote_copy(
+            src_ref=unit_out(u, j),
+            dst_ref=ins[u].at[j],
+            send_sem=core_send.at[u, j],
+            recv_sem=core_recv.at[u, j],
+            device_id={"shard": pair},
+            device_id_type=pl.DeviceIdType.MESH,
+        )
+
+    def far_copy(u, k):
+        return pltpu.make_async_remote_copy(
+            src_ref=ins[u].at[lax.rem(chip + k, chips)],
+            dst_ref=fars[u].at[k - 1],
+            send_sem=far_send.at[u, k - 1],
+            recv_sem=far_recv.at[u, k - 1],
+            device_id={"shard": peer(k)},
+            device_id_type=pl.DeviceIdType.MESH,
+        )
+
+    def halvings(u):
+        rows_u = works[u].shape[0]
+        count = 0
+        while count < bits and rows_u % (16 << (count + 1)) == 0:
+            count += 1
+        return count
+
+    def region(u, b):
+        rows_u = works[u].shape[0]
+        start = 0
+        for i in range(min(b, halvings(u))):
+            rows_u //= 2
+            start = start + rep_bit(i) * rows_u
+        if not isinstance(start, int):
+            start = pl.multiple_of(start, 16)
+        return start, rows_u
+
+    def half_base(u, b):
+        base_row = 0
+        for i in range(b):
+            _, length = region(u, i)
+            base_row += length // 2 if i < halvings(u) else length
+        return base_row
+
+    def half_copy(u, b):
+        start, length = region(u, b)
+        if b < halvings(u):
+            length //= 2
+            start = pl.multiple_of(start + (1 - rep_bit(b)) * length, 16)
+        return pltpu.make_async_remote_copy(
+            src_ref=ins[u].at[chip, pl.ds(start, length), :],
+            dst_ref=halves[u].at[pl.ds(half_base(u, b), length), :],
+            send_sem=half_send.at[u, b],
+            recv_sem=half_recv.at[u, b],
+            device_id={"rep": rep_peer(b)},
+            device_id_type=pl.DeviceIdType.MESH,
+        )
+
+    def half_add(u, b):
+        half_copy(u, b).wait()
+        start, length = region(u, b + 1)
+        got = halves[u][pl.ds(half_base(u, b), length), :].astype(f32)
+        lines = pl.ds(start, length)
+        out = (ins[u][chip, lines, :].astype(f32) + got).astype(bf16)
+        if b < bits - 1:
+            ins[u][chip, lines, :] = out
+        else:
+            works[u][lines, :] = out
+
+    def join_copy(u, b):
+        start, length = region(u, b + 1)
+        lines = pl.ds(start, length)
+        return pltpu.make_async_remote_copy(
+            src_ref=works[u].at[lines, :],
+            dst_ref=works[u].at[lines, :],
+            send_sem=join_send.at[u, b],
+            recv_sem=join_recv.at[u, b],
+            device_id={"rep": rep_peer(b)},
+            device_id_type=pl.DeviceIdType.MESH,
+        )
+
+    def unit_stage(u, stage):
+        if stage == 0:
+            for j in range(chips):
+                target = unit_out(u, j)
+                for r0, nr, c0, nc, value in unit_pieces(u, 2 * j + 1 - core):
+                    target[r0 : r0 + nr, c0 : c0 + nc] = value().astype(bf16)
+                core_copy(u, j).start()
+            return
+        if stage == 1:
+            for j in range(chips):
+                core_copy(u, j).wait()
+            for k in range(1, chips):
+                j = lax.rem(chip + k, chips)
+                for r0, nr, c0, nc, value in unit_pieces(u, 2 * j + core):
+                    got = ins[u][j, r0 : r0 + nr, c0 : c0 + nc].astype(f32)
+                    ins[u][j, r0 : r0 + nr, c0 : c0 + nc] = (value() + got).astype(bf16)
+                far_copy(u, k).start()
+            for r0, nr, c0, nc, value in unit_pieces(u, me):
+                got = ins[u][chip, r0 : r0 + nr, c0 : c0 + nc].astype(f32)
+                ins[u][chip, r0 : r0 + nr, c0 : c0 + nc] = (value() + got).astype(bf16)
+            return
+        if stage == 2:
+            for k in range(1, chips):
+                far_copy(u, k).wait()
+            total = ins[u][chip].astype(f32)
+            for k in range(1, chips):
+                total = total + fars[u][k - 1].astype(f32)
+            ins[u][chip] = total.astype(bf16)
+        if 2 < stage <= 2 + bits:
+            half_add(u, stage - 3)
+        if 2 <= stage < 2 + bits:
+            half_copy(u, stage - 2).start()
+            return
+        joins = [b for b in range(bits) if b < halvings(u)][::-1]
+        at_join = stage - 2 - bits
+        if 0 < at_join <= len(joins):
+            join_copy(u, joins[at_join - 1]).wait()
+        if at_join < len(joins):
+            join_copy(u, joins[at_join]).start()
+
+    stages = 3 + 2 * bits
+
+    def unit_run(u, first, last=None):
+        for stage in range(first, stages if last is None else last + 1):
+            unit_stage(u, stage)
+
+    def total_copy(b):
+        rows_t = total_ref.shape[0]
+        if b == 0:
+            target = {"shard": pair}
+        elif b == 1:
+            target = {"shard": peer(1)}
+        else:
+            target = {"rep": rep_peer(b - 2)}
+        return pltpu.make_async_remote_copy(
+            src_ref=total_ref,
+            dst_ref=total_in_ref.at[b],
+            send_sem=total_send.at[b],
+            recv_sem=total_recv.at[b],
+            device_id=target,
+            device_id_type=pl.DeviceIdType.MESH,
+        )
+
+    def total_add(b):
+        total_copy(b).wait()
+        total_ref[...] = total_ref[...] + total_in_ref[b]
+
     small_ref[...] = jnp.zeros(small_ref.shape, f32)
     dbias_ref[...] = jnp.zeros(dbias_ref.shape, f32)
 
@@ -236,6 +489,43 @@
         hit = (source // pad == to % sub) & (source % pad == to // sub)
         back_ref[pl.ds(start, 56), :] = hit.astype(f32).astype(bf16)
 
+    table_lanes = table_ref.shape[1]
+    row_iota = lax.broadcasted_iota(jnp.int32, (table_lanes, 128), 0)
+    low_lanes = lax.broadcasted_iota(jnp.int32, (key_rows, 128), 1) < pad
+
+    def named(j):
+        return (row_iota == index_ref[pl.ds(j, 1), :]).astype(f32).astype(bf16)
+
+    table = table_ref[...]
+    high = table.astype(bf16)
+    middle = (table - high.astype(f32)).astype(bf16)
+    low = (table - high.astype(f32) - middle.astype(f32)).astype(bf16)
+    upper_heads = heads // 2
+    sides = (u0_ref, u1_ref)
+    for side in sides:
+        side[0 : upper_heads * key_rows, :] = jnp.full((upper_heads * key_rows, 128), -1e30, f32)
+
+    def plane(h):
+        row = (h % upper_heads) * key_rows
+        return sides[h // upper_heads].at[row : row + key_rows, :]
+
+    @pl.loop(0, tokens)
+    def _(j):
+        hit = named(j)
+        line = (dot_nn(high, hit) + dot_nn(middle, hit)) + dot_nn(low, hit)
+        for side in range(2):
+            sides[side][pl.ds(j, upper_heads, stride=key_rows), :] = line[
+                side * upper_heads : (side + 1) * upper_heads
+            ]
+
+    for t in range(quads):
+        for h in range(quad // 2):
+            left = plane(t * quad + 2 * h)[...]
+            right = plane(t * quad + 2 * h + 1)[...]
+            bias_ref[t, :, 128 * h : 128 * (h + 1)] = jnp.where(
+                low_lanes, left, pltpu.roll(right, pad, 1)
+            )
+
     def stacked(tile):
         return jnp.concatenate([tile * m for m in head_masks_half], axis=0)
 
@@ -251,10 +541,20 @@
     @pl.loop(0, groups)
     def _(g):
         win0 = pl.multiple_of(g * group, group)
+        slot = lax.rem(g, 2)
+        load(x_hbm, g, slot).wait()
+
+        @pl.when(g < groups - 1)
+        def _():
+            load(x_hbm, g + 1, 1 - slot).start()
+
+        @pl.when(g == groups - 1)
+        def _():
+            load(dy_hbm, 0, 1 - slot).start()
 
         @pl.loop(0, tokens // step)
         def _(n):
-            part = x_ref[pl.ds(n * step, step), pl.ds(win0, group), :].astype(f32)
+            part = in_ref[slot, pl.ds(n * step, step)].astype(f32)
             flat = part.reshape(step * group, width)
             normal, _ = norm_parts(flat)
             wide_ref[pl.ds(n * step, step)] = (normal * gain1_ref[...] + shift1_ref[...]).reshape(
@@ -274,13 +574,15 @@
                     gather_start(2)
                     gather_start(3)
 
-            @pl.loop(0, 3 * width // chunk)
-            def _(n):
-                cols = pl.ds(pl.multiple_of(n * chunk, chunk), chunk)
+            for n in range(3 * width // chunk):
+                cols = slice(n * chunk, (n + 1) * chunk)
                 out = dot_nn(act_w_ref[g2], wqkv_ref[:, cols])
-                qkv_ref[g2, :, cols] = (
-                    (out + qkv_bias_ref[:, cols]) * qkv_scale_ref[:, cols]
-                ).astype(bf16)
+                if n < width // chunk:
+                    out = (out + query_bias_ref[:, cols]) * scale
+                if n >= 2 * width // chunk:
+                    first = n * chunk - 2 * width
+                    out = out + value_bias_ref[:, first : first + chunk]
+                qkv_ref[g2, :, cols] = out.astype(bf16)
 
             @pl.loop(0, sub)
             def _(w):
@@ -303,23 +605,45 @@
                 tokens, sub, width
             )
 
-        mixed_ref[:, pl.ds(win0, group), :] = wide_ref[...].astype(bf16)
-        mixed = mixed_ref[:, pl.ds(win0, group), :].reshape(rows, width)
+        @pl.when(g != 0)
+        def _():
+            store(mixed_ref, mixed_hbm, g - 1, mixed_sem).wait()
+
+        mixed_ref[...] = wide_ref[...].astype(bf16)
+        store(mixed_ref, mixed_hbm, g, mixed_sem).start()
+        mixed = mixed_ref[...].reshape(rows, width)
         for n in range(width // chunk):
             cols = slice(n * chunk, (n + 1) * chunk)
             out = dot_nn(mixed, wproj_ref[:, cols]) + proj_bias_ref[:, cols]
-            dx_ref[:, pl.ds(win0, group), cols] = (
-                x_ref[:, pl.ds(win0, group), cols].astype(f32) + out.reshape(tokens, group, chunk)
-            )
+            dx_ref[:, pl.ds(win0, group), cols] = in_ref[slot, :, :, cols].astype(
+                f32
+            ) + out.reshape(tokens, group, chunk)
 
     gather_finish(2)
     gather_finish(3)
     for i in range(4):
         gather_drain(i)
+    store(mixed_ref, mixed_hbm, groups - 1, mixed_sem).wait()
 
     @pl.loop(0, groups)
     def _(g):
         win0 = pl.multiple_of(g * group, group)
+        slot = lax.rem(groups + g, 2)
+        load(dy_hbm, g, slot).wait()
+
+        @pl.when(g < groups - 1)
+        def _():
+            load(dy_hbm, g + 1, 1 - slot).start()
+
+        @pl.when(g == groups - 1)
+        def _():
+            load(x_hbm, 0, 1 - slot).start()
+
+        @pl.when(g != 0)
+        def _():
+            store(y_ref, y_hbm, g - 1, y_sem).wait()
+
+        mixed_load(g).start()
 
         @pl.loop(0, tokens // step)
         def _(n):
@@ -328,23 +652,26 @@
             lines = pl.ds(pl.multiple_of(n * step * group, step * group), step * group)
             sa_ref[lines, :] = (normal * gain2_ref[...] + shift2_ref[...]).astype(bf16)
 
-        dy = dy_ref[:, pl.ds(win0, group), :].reshape(rows, width)
         sat_ref[...] = sa_ref[...].T
-        dyt_ref[...] = dy.T
+        dyt_ref[...] = in_ref[slot].reshape(rows, width).T
 
         @pl.loop(0, hidden // chunk)
-        def _(n):
+        def _(i):
+            n = lax.rem(i, shards) * parts + i // shards
             start = pl.multiple_of(n * chunk, chunk)
             cols = pl.ds(start, chunk)
-            u_ref[...] = dot_nn(sa_ref[...], w1_ref[:, cols])
-            da_ref[...] = dot_nt(
-                dy_ref[:, pl.ds(win0, group), :].reshape(rows, width), w2_ref[cols, :]
-            )
+            u = dot_nn(sa_ref[...], w1_ref[:, cols])
+            u0_ref[...] = u[:, 0:128]
+            u1_ref[...] = u[:, 128:256]
+            da_ref[...] = dot_nt(in_ref[slot].reshape(rows, width), w2_ref[cols, :])
 
             @pl.loop(0, tokens // step)
             def _(m):
                 lines = pl.ds(pl.multiple_of(m * step * group, step * group), step * group)
-                value, slope = gelu_pair(u_ref[lines, :] + hidden_bias_ref[:, cols])
+                value, slope = gelu_pair(
+                    jnp.concatenate([u0_ref[lines, :], u1_ref[lines, :]], axis=1)
+                    + hidden_bias_ref[:, cols]
+                )
                 act_ref[lines, cols] = value.astype(bf16)
                 dup = (da_ref[lines, :] * slope).astype(bf16)
                 dup_ref[lines, cols] = dup
@@ -363,13 +690,21 @@
                 dw1_ref[:, cols] += part1
                 dw2t_ref[:, cols] += part2
 
+            @pl.when((g == groups - 1) & (i == shards - 1))
+            def _():
+                unit_stage(0, 0)
+
         for n in range(width // chunk):
             cols = slice(n * chunk, (n + 1) * chunk)
             out = dot_nn(act_ref[...], w2_ref[:, cols]) + output_bias_ref[:, cols]
-            y_ref[:, pl.ds(win0, group), cols] = (
+            y_ref[:, :, cols] = (
                 dx_ref[:, pl.ds(win0, group), cols] + out.reshape(tokens, group, chunk)
             ).astype(bf16)
-            acc_ref[:, cols] = dot_nt(dup_ref[...], w1_ref[cols, :])
+            wide_ref[:, :, cols] = dot_nt(dup_ref[...], w1_ref[cols, :]).reshape(
+                tokens, group, chunk
+            )
+
+        store(y_ref, y_hbm, g, y_sem).start()
 
         @pl.loop(0, tokens // step)
         def _(n):
@@ -377,15 +712,14 @@
             normal, inverse = norm_parts(
                 dx_ref[pl.ds(n * step, step), pl.ds(win0, group), :].reshape(step * group, width)
             )
-            grad = acc_ref[lines, :]
+            grad = wide_ref[pl.ds(n * step, step)].reshape(step * group, width)
             scaled = grad * gain2_ref[...]
             back = inverse * (
                 scaled
                 - jnp.mean(scaled, axis=-1, keepdims=True)
                 - normal * jnp.mean(scaled * normal, axis=-1, keepdims=True)
             )
-            cot = dy_ref[pl.ds(n * step, step), pl.ds(win0, group), :].astype(f32)
-            cot = cot.reshape(step * group, width)
+            cot = in_ref[slot, pl.ds(n * step, step)].astype(f32).reshape(step * group, width)
             total = cot + back
             dx_ref[pl.ds(n * step, step), pl.ds(win0, group), :] = total.reshape(step, group, width)
             sa_ref[lines, :] = total.astype(bf16)
@@ -394,8 +728,8 @@
             add_small("g2", fold_rows(grad * normal))
             add_small("s2", fold_rows(grad))
 
-        mixed = mixed_ref[:, pl.ds(win0, group), :].reshape(rows, width)
-        part3 = dot_tn(mixed, sa_ref[...])
+        mixed_load(g).wait()
+        part3 = dot_tn(mixed_ref[...].reshape(rows, width), sa_ref[...])
 
         @pl.when(g == 0)
         def _():
@@ -404,6 +738,20 @@
         @pl.when(g != 0)
         def _():
             dwproj_ref[...] += part3
+
+    store(y_ref, y_hbm, groups - 1, y_sem).wait()
+    unit_stage(0, 1)
+    unit_stage(1, 0)
+
+    plan = {
+        0: ((1, 1),),
+        1: ((0, 2),),
+        2: ((0, 3),),
+        3: ((0, 4), (1, 2)),
+        4: ((0, 5), (1, 3)),
+        5: ((0, 6), (1, 4)),
+    }
+    plan_last = 5
 
     @pl.loop(0, groups)
     def _(g):
@@ -414,6 +762,14 @@
             half8 = wide_ref[:, sub * s : sub * (s + 1), :].reshape(rows8, width).astype(bf16)
             half_w = dot_nn(perm_ref[...], half8).astype(bf16)
             mixed_w_ref[...] = dot_nt(half_w, wproj_ref[...]).astype(bf16)
+
+            for point, calls in plan.items():
+                if point % 2 == s:
+
+                    @pl.when(g2 == point)
+                    def _():
+                        for u, stage in calls:
+                            unit_stage(u, stage)
 
             @pl.loop(0, sub)
             def _(w):
@@ -458,6 +814,43 @@
                 def _():
                     dwqkv_ref[:, cols] += part
 
+    unit_stage(2, 0)
+    unit_stage(0, 7)
+    unit_stage(1, 5)
+
+    for t in range(quads):
+        for h in range(quad // 2):
+            both = dbias_ref[t, :, 128 * h : 128 * (h + 1)]
+            plane(t * quad + 2 * h)[...] = jnp.where(low_lanes, both, 0.0)
+            plane(t * quad + 2 * h + 1)[...] = jnp.where(
+                low_lanes, pltpu.roll(both, pad, 1), 0.0
+            )
+    total_ref[...] = jnp.zeros(total_ref.shape, f32)
+
+    @pl.loop(0, tokens)
+    def _(j):
+        hit = named(j)
+        line = jnp.concatenate(
+            [side[pl.ds(j, upper_heads, stride=key_rows), :] for side in sides], axis=0
+        )
+        upper_half = line.astype(bf16)
+        lower_half = (line - upper_half.astype(f32)).astype(bf16)
+        total_ref[0:heads, 0:table_lanes] = total_ref[0:heads, 0:table_lanes] + (
+            dot_nt(upper_half, hit) + dot_nt(lower_half, hit)
+        )
+
+    @pl.loop(0, groups)
+    def _(g):
+        win0 = pl.multiple_of(g * group, group)
+        slot = lax.rem(2 * groups + g, 2)
+        load(x_hbm, g, slot).wait()
+
+        @pl.when(g < groups - 1)
+        def _():
+            load(x_hbm, g + 1, 1 - slot).start()
+
+        for s in range(2):
+            g2 = g * 2 + s
             for n in range(width // chunk):
                 cols = slice(n * chunk, (n + 1) * chunk)
                 mixed_w_ref[:, cols] = dot_nt(qkv_ref[g2], wqkv_ref[cols, :]).astype(bf16)
@@ -465,9 +858,20 @@
                 tokens, sub, width
             )
 
+        for point, calls in {
+            0: ((2, 1), (0, 8), (1, 6)),
+            1: ((2, 2), (1, 7)),
+            2: ((2, 3), (1, 8)),
+        }.items():
+
+            @pl.when(g == point)
+            def _():
+                for u, stage in calls:
+                    unit_stage(u, stage)
+
         @pl.loop(0, tokens // step)
         def _(n):
-            part = x_ref[pl.ds(n * step, step), pl.ds(win0, group), :].astype(f32)
+            part = in_ref[slot, pl.ds(n * step, step)].astype(f32)
             normal, inverse = norm_parts(part.reshape(step * group, width))
             grad = wide_ref[pl.ds(n * step, step)].reshape(step * group, width)
             scaled = grad * gain1_ref[...]
@@ -480,68 +884,141 @@
             add_small("g1", fold_rows(grad * normal))
             add_small("s1", fold_rows(grad))
 
-
-def local_pass(x, dy, wqkv, wproj, w1, w2, vectors, bias, heads, shards):
+        store(dx_ref.at[:, pl.ds(win0, group), :], dx_hbm, g, dx_sem.at[g]).start()
+
+    for i in range(small_ref.shape[1] // width):
+        total_ref[heads + i : heads + i + 1, :] = jnp.sum(
+            small_ref[:, i * width : (i + 1) * width], axis=0, keepdims=True
+        )
+    steps = 2 + bits
+    total_copy(0).start()
+    for stage in range(4, stages):
+        unit_stage(2, stage)
+        b = stage - 4
+        if b < steps:
+            total_add(b)
+            if b + 1 < steps:
+                total_copy(b + 1).start()
+    for u in (0, 1):
+        unit_run(u, 9)
+    for b in range(stages - 4, steps):
+        total_add(b)
+        if b + 1 < steps:
+            total_copy(b + 1).start()
+    for g in range(groups):
+        store(dx_ref.at[:, g * group : (g + 1) * group, :], dx_hbm, g, dx_sem.at[g]).wait()
+
+
+def local_pass(x, dy, wqkv, wproj, w1, w2, vectors, table, index, shards, reps):
     tokens, windows, width = x.shape
     hidden = w1.shape[1]
-    dims = (tokens, windows, width, heads, hidden, shards)
+    heads = table.shape[0]
+    dims = (tokens, windows, width, heads, hidden, shards, reps)
     chips = shards // 2
+    bits = reps.bit_length() - 1
     sub = 8
+    group = 2 * sub
     pad = 64
-    rows = tokens * 2 * sub
+    rows = tokens * group
     small_size = 8 * width + hidden
     subs = windows // sub
+    owned = width // shards
+    unit_rows = (
+        (width * hidden) // (shards * width),
+        (width * hidden) // (shards * width) + owned,
+        3 * owned,
+    )
+    total_rows = -(-(heads + small_size // width) // 8) * 8
     shapes = (
-        jax.ShapeDtypeStruct(x.shape, bf16),
-        jax.ShapeDtypeStruct(x.shape, f32),
-        jax.ShapeDtypeStruct((width, 3 * width), f32),
-        jax.ShapeDtypeStruct((width, width), f32),
-        jax.ShapeDtypeStruct((width, hidden), f32),
-        jax.ShapeDtypeStruct((width, hidden), f32),
-        jax.ShapeDtypeStruct((8, small_size), f32),
-        jax.ShapeDtypeStruct(bias.shape, f32),
+        [
+            jax.ShapeDtypeStruct(x.shape, bf16),
+            jax.ShapeDtypeStruct(x.shape, f32),
+            jax.ShapeDtypeStruct(x.shape, bf16),
+        ]
+        + [jax.ShapeDtypeStruct((r, width), bf16) for r in unit_rows]
+        + [jax.ShapeDtypeStruct((total_rows, width), f32)]
     )
     vmem = pl.BlockSpec(memory_space=pltpu.VMEM)
+    hbm = pl.BlockSpec(memory_space=pl.ANY)
+
+    def half_rows(r):
+        total = 0
+        for _ in range(bits):
+            if r % 32 == 0:
+                r //= 2
+            total += r
+        return total
+
     return pl.pallas_call(
         functools.partial(compute_kernel, dims),
         out_shape=shapes,
-        in_specs=[vmem] * 2 + [pl.BlockSpec(memory_space=pl.ANY)] * 4 + [vmem] * 10,
-        out_specs=[vmem] * len(shapes),
+        in_specs=[hbm] * 6 + [vmem] * 11,
+        out_specs=[hbm] * 3 + [vmem] * 4,
         scratch_shapes=[
+            pltpu.VMEM((2, tokens, group, width), bf16),
+            pltpu.VMEM((tokens, group, width), bf16),
+            pltpu.VMEM(x.shape, f32),
+            pltpu.VMEM((width, 3 * width), f32),
+            pltpu.VMEM((width, width), f32),
+            pltpu.VMEM((width, hidden), f32),
+            pltpu.VMEM((width, hidden), f32),
+            pltpu.VMEM((8, small_size), f32),
+            pltpu.VMEM((heads // 4, 56, 256), f32),
+            pltpu.VMEM((heads // 4, 56, 256), f32),
             pltpu.VMEM((sub * pad, tokens * sub), bf16),
             pltpu.VMEM((tokens * sub, sub * pad), bf16),
             pltpu.VMEM((subs, sub * pad, width), bf16),
             pltpu.VMEM((subs, sub * pad, 3 * width), bf16),
             pltpu.VMEM((sub * pad, width), bf16),
-            pltpu.VMEM(x.shape, bf16),
+            pltpu.VMEM((tokens, group, width), bf16),
             pltpu.VMEM((subs, sub, heads // 4, 256), f32),
-            pltpu.VMEM((tokens, 2 * sub, width), f32),
+            pltpu.VMEM((tokens, group, width), f32),
             pltpu.VMEM((rows, width), bf16),
             pltpu.VMEM((width, rows), bf16),
             pltpu.VMEM((width, rows), bf16),
-            pltpu.VMEM((rows, 256), f32),
+            pltpu.VMEM((rows, 128), f32),
+            pltpu.VMEM((rows, 128), f32),
             pltpu.VMEM((rows, 256), f32),
             pltpu.VMEM((rows, hidden), bf16),
             pltpu.VMEM((rows, hidden), bf16),
-            pltpu.VMEM((rows, width), f32),
             pltpu.VMEM((width, 3 * width), bf16),
             pltpu.VMEM((width, width), bf16),
             pltpu.VMEM((width, hidden), bf16),
             pltpu.VMEM((hidden, width), bf16),
+            pltpu.VMEM((chips - 1, unit_rows[0], width), bf16),
+            *[pltpu.VMEM((chips, r, width), bf16) for r in unit_rows],
+            *[pltpu.VMEM((chips - 1, r, width), bf16) for r in unit_rows],
+            *[pltpu.VMEM((half_rows(r), width), bf16) for r in unit_rows],
+            pltpu.VMEM((2 + bits, total_rows, width), f32),
             pltpu.SemaphoreType.DMA((4,)),
             pltpu.SemaphoreType.DMA((4, chips)),
             pltpu.SemaphoreType.DMA((4, chips)),
             pltpu.SemaphoreType.DMA((4, chips - 1)),
             pltpu.SemaphoreType.DMA((4, chips - 1)),
+            pltpu.SemaphoreType.DMA((2,)),
+            pltpu.SemaphoreType.DMA,
+            pltpu.SemaphoreType.DMA,
+            pltpu.SemaphoreType.DMA((windows // group,)),
+            pltpu.SemaphoreType.DMA((3, chips)),
+            pltpu.SemaphoreType.DMA((3, chips)),
+            pltpu.SemaphoreType.DMA((3, chips - 1)),
+            pltpu.SemaphoreType.DMA((3, chips - 1)),
+            pltpu.SemaphoreType.DMA((3, bits)),
+            pltpu.SemaphoreType.DMA((3, bits)),
+            pltpu.SemaphoreType.DMA((3, bits)),
+            pltpu.SemaphoreType.DMA((3, bits)),
+            pltpu.SemaphoreType.DMA((2 + bits,)),
+            pltpu.SemaphoreType.DMA((2 + bits,)),
         ],
         compiler_params=pltpu.CompilerParams(
             vmem_limit_bytes=67043328, collective_id=0, has_side_effects=True
         ),
-    )(x, dy, wqkv, wproj, w1, w2, *vectors, bias)
+    )(x, dy, wqkv, wproj, w1, w2, *vectors, table, index)
 
 
 def on_device(
     shards,
+    reps,
     block_input,
     out_grad,
     qkv_weight,
@@ -563,24 +1040,12 @@
     windows, tokens, width = block_input.shape
     table_rows, heads = bias_table.shape
     hidden = hidden_bias.shape[0]
-    scale = (width // heads) ** (-0.5)
-    pairs = tokens * tokens
-    one_hot = (
-        table_index.T.reshape(pairs, 1) == lax.broadcasted_iota(jnp.int32, (pairs, table_rows), 1)
-    ).astype(f32)
-    by_pair = jnp.dot(one_hot, bias_table, precision=lax.Precision.HIGHEST)
-    by_key = by_pair.reshape(tokens, tokens, heads).transpose(0, 2, 1)
-    by_key = jnp.pad(by_key, ((0, 0), (0, 0), (0, 64 - tokens)))
-    by_key = jnp.pad(by_key, ((0, 56 - tokens), (0, 0), (0, 0)), constant_values=-1e30)
-    quads = heads // 4
-    bias = by_key.reshape(56, quads, 256).transpose(1, 0, 2)
-    zeros = jnp.zeros((width,), f32)
-    ones = jnp.ones((2 * width,), f32)
+    chunk = 256
     vectors = [
         v.reshape(1, -1)
         for v in (
-            jnp.concatenate([query_bias, zeros, value_bias]),
-            jnp.concatenate([jnp.full((width,), scale, f32), ones]),
+            query_bias,
+            value_bias,
             proj_bias,
             hidden_bias,
             output_bias,
@@ -590,7 +1055,11 @@
             second_shift,
         )
     ]
-    y, dx, dwqkv, dwproj, dw1, dw2t, small, dbias = local_pass(
+    table = jnp.pad(bias_table.T, ((0, 0), (0, 256 - table_rows)))
+    index = jnp.pad(
+        table_index.T, ((0, 56 - tokens), (0, 128 - tokens)), constant_values=-1
+    )
+    y, dx, _, work0, work1, work2, total = local_pass(
         jnp.transpose(block_input, (1, 0, 2)),
         jnp.transpose(out_grad, (1, 0, 2)),
         qkv_weight,
@@ -598,45 +1067,48 @@
         hidden_weight,
         output_weight,
         vectors,
-        bias,
-        heads,
+        table,
+        index,
         shards,
+        reps,
     )
-    dbias = dbias.transpose(1, 0, 2).reshape(56, heads, 64)[:tokens, :, :tokens]
-    dbias = dbias.transpose(1, 0, 2).reshape(heads, pairs)
-    bias_table_grad = jnp.dot(dbias, one_hot, precision=lax.Precision.HIGHEST).T
-    shares = [
-        lax.psum_scatter(g.astype(bf16), "shard", scatter_dimension=0, tiled=True)
-        for g in (dwqkv, dwproj, dw1, dw2t.T)
-    ]
-    shares = [lax.psum(s, "rep").astype(f32) for s in shares]
-    small, bias_table_grad = lax.psum(
-        (jnp.sum(small, axis=0), bias_table_grad), ("shard", "rep")
+    owned = width // shards
+    parts = hidden // (shards * chunk)
+    per = width // chunk
+    first_rows = owned * (shards // per)
+    works = (work0, work1)
+    dw1 = jnp.stack(
+        [w[:first_rows].reshape(shards // per, owned, per, chunk) for w in works[:parts]]
     )
+    dw1 = dw1.transpose(2, 1, 3, 0, 4).reshape(owned, hidden)
+    dw2 = jnp.concatenate([w[first_rows : first_rows + chunk] for w in works[:parts]], axis=0)
+    dwproj = work1[first_rows + chunk :]
+    dwqkv = work2.reshape(3, owned, width).transpose(1, 0, 2).reshape(owned, 3 * width)
+    sums = total[heads : heads + (8 * width + hidden) // width].reshape(-1)
     cuts = [width, width, width, hidden, width, width, width, width, width]
-    parts = []
+    split = []
     at = 0
     for size in cuts:
-        parts.append(small[at : at + size])
+        split.append(sums[at : at + size])
         at += size
-    qb, vb, pb, hb, ob, g1, s1, g2, s2 = parts
+    qb, vb, pb, hb, ob, g1, s1, g2, s2 = split
     return (
         jnp.transpose(y, (1, 0, 2)),
         jnp.transpose(dx, (1, 0, 2)),
-        shares[0],
+        dwqkv.astype(f32),
         qb,
         vb,
-        shares[1],
+        dwproj.astype(f32),
         pb,
-        shares[2],
+        dw1.astype(f32),
         hb,
-        shares[3],
+        dw2.astype(f32),
         ob,
         g1,
         s1,
         g2,
         s2,
-        bias_table_grad,
+        total[:heads, :table_rows].T,
     )
 
 
@@ -645,7 +1117,7 @@
     cut = P("shard", None)
     full = P()
     return jax.shard_map(
-        functools.partial(on_device, mesh.shape["shard"]),
+        functools.partial(on_device, mesh.shape["shard"], mesh.shape["rep"]),
         mesh=mesh,
         in_specs=(
             rows,

time: 501 us -> 309 us (0.62)
  waiting for transfers between devices: 160 us -> 0 us
  blocking collectives: 41.8 us -> 0 us
  Pallas kernels: 251 us -> 284 us
  other arithmetic: 17 us -> 3.4 us
  between operations: 13.9 us -> 0.69 us
  local copies, waits for them, and re-layouts: 14.6 us -> 20.2 us
    reduce_scatter x4 -> x0, waiting for transfers between devices: 111 us -> none  [on_device(): lax.psum_scatter(g.astype(bf16), 'shard', scatter_dimension=0, tiled=True)]
    psum x1 -> x0, waiting for transfers between devices: 49.1 us -> none  [on_device(): shares = [lax.psum(s, 'rep').astype(f32) for s in shares]]
    psum x1 -> x0, blocking collectives: 41.8 us -> none  [on_device(): lax.psum((jnp.sum(small, axis=0), bias_table_grad), ('shard', 'rep'))]
    pallas_call x1, Pallas kernels: 251 us -> 284 us  [local_pass(): pl.pallas_call(functools.partial(compute_kernel, dims), out_shape=shapes,...]
    convert_element_type x7 -> x3, other arithmetic: 16.9 us -> 3.4 us  [the longest x1 1.63 us: on_device(): dwproj.astype(f32)]
    unnamed x22 -> x8, local copies, waits for them, and re-layouts: 10.1 us -> 10.2 us
  transfers between devices with their start and end apart: 5 -> 0, of which waited for: 5 -> 0; matrix products, arithmetic and copies ran while one was open for 3% -> 0% of each run, Pallas kernels for 0% -> 0%
where the time goes in v3:
time: 309 us; the launch traced here: 308 us
  Pallas kernels  284 us (92%)
  local copies, waits for them, and re-layouts  20.2 us (7%)
  other arithmetic  3.4 us (1%)
    pallas_call x1, Pallas kernels, local_pass(): pl.pallas_call(functools.partial(compute_kernel, dims), out_shape=shapes,...  284 us
    unnamed x8, local copies, waits for them, and re-layouts  10.2 us

profile of v3, /device:TPU:0, one launch (start us, length us, event | category | flops | bytes accessed | tf_op | source)
XLA Modules:
  0.0 308.3 jit_solution(1121589878598125811)
XLA Ops:
  0.6 1.3 pad.8.table_ref
  2.0 0.8 copy.36
  2.8 0.6 pad.9.index_ref
  3.4 284.0 %shard_map.288 = (bf16[49,48,512]{2,1,0:T(8,128)(2,1)}, f32[49,48,512]{2,1,0:T(8,128)}, bf16[49,48,512]{2,1,0:T(8,128)(2,1)}, bf16[512,512]{1,0:T(8,128)(2,1)}, ...) custom-call(bf16[49,48,512]{2,1,0:T(8,128)(2,1)} %bitcast.38, ...), custom_call_target="tpu_custom_call" | custom-call | tf_op jit(solution)/shard_map/pallas_call | solution.py:952
  287.4 0.7 slice_bitcast_fusion.1
  288.2 0.6 copy.40
  288.8 1.3 slice_bitcast_fusion
  290.1 1.5 fusion.2
  291.6 1.6 slice_convert_fusion
  293.2 1.3 fusion
  294.5 0.1 stack_reshape.7
  294.5 0.1 stack_reshape.6
  294.6 0.7 convert_bitcast_fusion
  295.3 0.8 copy.38
  296.1 1.8 reshape.88
  297.9 0.0 copy-start
  297.9 1.1 maximum_convert_fusion
  299.0 1.2 copy.37
  300.2 1.1 copy.39
  301.3 0.0 copy-done
  301.3 1.4 copy.43
  302.7 5.5 %copy.44 = f32[48,49,512]{2,0,1:T(8,128)} copy(f32[48,49,512]{2,0,1:T(8,128)} %bitcast.35) | data formatting | bytes 9633792
Async XLA Ops:
  297.9 3.4 %copy-start = (bf16[49,48,512]{2,1,0:T(8,128)(2,1)S(1)}, bf16[49,48,512]{2,1,0:T(8,128)(2,1)}, u32[]{:S(2)}) copy-start(bf16[49,48,512]{2,1,0:T(8,128)(2,1)} %get-tuple-element.22) | copy-start | bytes 7225348

commit v4 on v3

v4 whole, which is shorter than its diff:
```python
import functools

import jax
import jax.numpy as jnp
from jax import lax
from jax.experimental import pallas as pl
from jax.experimental.pallas import tpu as pltpu
from jax.sharding import PartitionSpec as P

epsilon = 1e-05
f32 = jnp.float32
bf16 = jnp.bfloat16


def dot_nn(a, b):
    return lax.dot_general(a, b, (((1,), (0,)), ((), ())), preferred_element_type=f32)


def dot_nt(a, b):
    return lax.dot_general(a, b, (((1,), (1,)), ((), ())), preferred_element_type=f32)


def dot_tn(a, b):
    return lax.dot_general(a, b, (((0,), (0,)), ((), ())), preferred_element_type=f32)


def norm_parts(values):
    center = values - jnp.mean(values, axis=-1, keepdims=True)
    inverse = lax.rsqrt(jnp.mean(center * center, axis=-1, keepdims=True) + epsilon)
    return center * inverse, inverse


def fold_rows(values):
    rows, cols = values.shape
    return jnp.sum(values.reshape(rows // 8, 8, cols), axis=0)


def gelu_pair(upper):
    phi = 0.5 + 0.5 * lax.erf(upper * 0.7071067811865476)
    bell = jnp.exp(upper * upper * -0.5) * 0.3989422804014327
    return upper * phi, phi + upper * bell


def compute_kernel(
    dims,
    x_hbm,
    dy_hbm,
    wqkv_shard,
    wproj_shard,
    w1_shard,
    w2_shard,
    query_bias_ref,
    value_bias_ref,
    proj_bias_ref,
    hidden_bias_ref,
    output_bias_ref,
    gain1_ref,
    shift1_ref,
    gain2_ref,
    shift2_ref,
    table_ref,
    index_ref,
    y_hbm,
    dx_hbm,
    mixed_hbm,
    act_w_hbm,
    work0_ref,
    work1_ref,
    work2_ref,
    work3_ref,
    work4_ref,
    work5_ref,
    total_ref,
    in_ref,
    y_ref,
    dx_ref,
    dwqkv_ref,
    dwproj_ref,
    dw1_ref,
    dw2t_ref,
    small_ref,
    dbias_ref,
    bias_ref,
    perm_ref,
    back_ref,
    act_w_ref,
    qkv_ref,
    mixed_w_ref,
    mixed_ref,
    lse_ref,
    wide_ref,
    sa_ref,
    sat_ref,
    dyt_ref,
    u_ref,
    da_ref,
    plane_ref,
    names_ref,
    rows_ref,
    act_ref,
    dup_ref,
    wqkv_ref,
    wproj_ref,
    w1_ref,
    w2_ref,
    out0_ref,
    in0_ref,
    in1_ref,
    in2_ref,
    in3_ref,
    in4_ref,
    in5_ref,
    far0_ref,
    far1_ref,
    far2_ref,
    far3_ref,
    far4_ref,
    far5_ref,
    half0_ref,
    half1_ref,
    half2_ref,
    half3_ref,
    half4_ref,
    half5_ref,
    total_in_ref,
    own_sem,
    pair_send,
    pair_recv,
    chip_send,
    chip_recv,
    load_sem,
    y_sem,
    mixed_sem,
    act_w_sem,
    dx_sem,
    core_send,
    core_recv,
    far_send,
    far_recv,
    half_send,
    half_recv,
    join_send,
    join_recv,
    total_send,
    total_recv,
):
    tokens, windows, width, heads, hidden, shards, reps = dims
    me = lax.axis_index("shard")
    chips = shards // 2
    core = lax.rem(me, 2)
    chip = me // 2
    pair = chip * 2 + 1 - core

    def peer(k):
        return lax.rem(chip + k, chips) * 2 + core

    def owner(k, side):
        return lax.rem(chip + chips - k, chips) * 2 + side

    gathers = (
        (wqkv_shard, wqkv_ref, slice(0, wqkv_ref.shape[1] // 2)),
        (wqkv_shard, wqkv_ref, slice(wqkv_ref.shape[1] // 2, wqkv_ref.shape[1])),
        (wproj_shard, wproj_ref, slice(0, wproj_ref.shape[1])),
        (w1_shard, w1_ref, slice(0, w1_ref.shape[1])),
        (w2_shard, w2_ref, slice(0, w2_ref.shape[1])),
    )

    def block(ref, index, cols):
        size = ref.shape[0] // shards
        return ref.at[pl.ds(pl.multiple_of(index * size, size), size), cols]

    def own_copy(i):
        shard, full, cols = gathers[i]
        return pltpu.make_async_copy(shard.at[:, cols], block(full, me, cols), own_sem.at[i])

    def chip_copy(i, k):
        shard, full, cols = gathers[i]
        return pltpu.make_async_remote_copy(
            src_ref=shard.at[:, cols],
            dst_ref=block(full, me, cols),
            send_sem=chip_send.at[i, k - 1],
            recv_sem=chip_recv.at[i, k - 1],
            device_id={"shard": peer(k)},
            device_id_type=pl.DeviceIdType.MESH,
        )

    def pair_copy(i, k):
        shard, full, cols = gathers[i]
        return pltpu.make_async_remote_copy(
            src_ref=shard.at[:, cols] if k == 0 else block(full, owner(k, core), cols),
            dst_ref=block(full, owner(k, core), cols),
            send_sem=pair_send.at[i, k],
            recv_sem=pair_recv.at[i, k],
            device_id={"shard": pair},
            device_id_type=pl.DeviceIdType.MESH,
        )

    def gather_start(i):
        own_copy(i).start()
        for k in range(1, chips):
            chip_copy(i, k).start()
        pair_copy(i, 0).start()

    def gather_relay(i):
        for k in range(1, chips):
            chip_copy(i, k).wait_recv()
            pair_copy(i, k).start()

    def gather_finish(i):
        own_copy(i).wait()
        for k in range(chips):
            pair_copy(i, k).wait_recv()

    def gather_drain(i):
        for k in range(1, chips):
            chip_copy(i, k).wait_send()
        for k in range(chips):
            pair_copy(i, k).wait_send()

    rep = lax.axis_index("rep")
    bits = reps.bit_length() - 1

    near = min(bits, 3)
    near_size = 1 << near
    far_bits = list(range(near, bits))

    def flipped(index, distance, span):
        for b in range(span):
            if distance >> b & 1:
                index = index + (1 - 2 * lax.rem(index // (1 << b), 2)) * (1 << b)
        return index

    shard_span = shards.bit_length() - 1
    barrier = pltpu.get_barrier_semaphore()
    greeted = [{"shard": flipped(me, d, shard_span)} for d in range(1, shards)]
    greeted += [{"rep": flipped(rep, d, near)} for d in range(1, near_size)]
    greeted += [{"rep": flipped(rep, 1 << b, bits)} for b in far_bits]
    for target in greeted:
        pl.semaphore_signal(
            barrier, inc=1, device_id=target, device_id_type=pl.DeviceIdType.MESH
        )
    pl.semaphore_wait(barrier, len(greeted))
    gather_start(0)
    gather_start(1)

    head_size = width // heads
    scale = head_size ** (-0.5)
    pad = 64
    key_rows = 56
    sub = 8
    group = 2 * sub
    groups = windows // group
    quad = 128 // head_size
    quads = heads // quad
    rows8 = tokens * sub
    rows = tokens * group
    rows_w = sub * pad
    chunk = width
    step = 7
    lane_head = lax.broadcasted_iota(jnp.int32, (pad, 128), 1) // head_size
    head_masks = [lane_head == h for h in range(quad)]
    head_masks_half = [m.astype(f32).astype(bf16) for m in head_masks]

    base = {}
    at = 0
    for name, size in (
        ("qb", width),
        ("vb", width),
        ("pb", width),
        ("hb", hidden),
        ("ob", width),
        ("g1", width),
        ("s1", width),
        ("g2", width),
        ("s2", width),
    ):
        base[name] = (at, size)
        at += size

    def add_small(name, value, offset=0):
        start = base[name][0] + offset
        cols = pl.ds(start, value.shape[1])
        small_ref[:, cols] = small_ref[:, cols] + value

    def load(source, g, slot):
        return pltpu.make_async_copy(
            source.at[:, pl.ds(pl.multiple_of(g * group, group), group), :],
            in_ref.at[slot],
            load_sem.at[slot],
        )

    def store(source, target, g, sem):
        return pltpu.make_async_copy(
            source, target.at[:, pl.ds(pl.multiple_of(g * group, group), group), :], sem
        )

    def mixed_load(g):
        return pltpu.make_async_copy(
            mixed_hbm.at[:, pl.ds(pl.multiple_of(g * group, group), group), :], mixed_ref, mixed_sem
        )

    def act_w_store(g2, slot):
        return pltpu.make_async_copy(act_w_ref.at[slot], act_w_hbm.at[g2], act_w_sem.at[slot])

    def act_w_load(g2, slot):
        return pltpu.make_async_copy(act_w_hbm.at[g2], act_w_ref.at[slot], act_w_sem.at[slot])

    load(x_hbm, 0, 0).start()

    owned = width // shards
    works = (work0_ref, work1_ref, work2_ref, work3_ref, work4_ref, work5_ref)
    ins = (in0_ref, in1_ref, in2_ref, in3_ref, in4_ref, in5_ref)
    fars = (far0_ref, far1_ref, far2_ref, far3_ref, far4_ref, far5_ref)
    halves = (half0_ref, half1_ref, half2_ref, half3_ref, half4_ref, half5_ref)

    def unit_pieces(u, s):
        own = pl.ds(pl.multiple_of(s * owned, owned), owned)
        if u == 0:
            for i in range(hidden // width):
                cols = slice(width * i, width * (i + 1))
                yield owned * i, owned, (lambda cols=cols: dw1_ref[own, cols])
        elif u == 1:
            size = hidden // shards
            for i in range(size // 256):
                lanes = pl.ds(pl.multiple_of(s * size + i * 256, 256), 256)
                yield i * 256, 256, (lambda lanes=lanes: dw2t_ref[:, lanes].T)
        elif u == 2:
            yield 0, owned, (lambda: dwproj_ref[own, :])
        else:
            cols = slice(width * (u - 3), width * (u - 2))
            yield 0, owned, (lambda: dwqkv_ref[own, cols])

    def unit_out(u, j):
        rows_u = works[u].shape[0]
        if u == 0:
            return mixed_w_ref.at[0:rows_u] if j == 0 else out0_ref.at[j - 1]
        if u == 1:
            return act_ref.at[0:rows_u, j * width : (j + 1) * width]
        first = (u - 2) * owned
        return act_ref.at[
            first : first + owned, (chips + j) * width : (chips + j + 1) * width
        ]

    def core_copy(u, j):
        return pltpu.make_async_remote_copy(
            src_ref=unit_out(u, j),
            dst_ref=ins[u].at[j],
            send_sem=core_send.at[u, j],
            recv_sem=core_recv.at[u, j],
            device_id={"shard": pair},
            device_id_type=pl.DeviceIdType.MESH,
        )

    def levels(u):
        if u < 2 and near == 3:
            return [(0, 1), (1, 2)]
        return [(0, near)]

    def level_index(u, at_level):
        low, count = levels(u)[at_level]
        return lax.rem(rep // (1 << low), 1 << count)

    def held(u, at_level):
        size = works[u].shape[0]
        start = 0
        for k in range(at_level):
            size >>= levels(u)[k][1]
            start = start + level_index(u, k) * size
        return start, size

    def lines_of(start, size):
        return pl.ds(start if isinstance(start, int) else pl.multiple_of(start, 16), size)

    def own_piece(u):
        return lines_of(*held(u, len(levels(u))))

    def peers_of(u, at_level):
        slot = 0
        row = 0
        for k in range(at_level):
            others = (1 << levels(u)[k][1]) - 1
            slot += others
            row += others * held(u, k + 1)[1]
        low, count = levels(u)[at_level]
        size = held(u, at_level + 1)[1]
        return [
            (d, slot + d - 1, row + (d - 1) * size, {"rep": flipped(rep, d << low, bits)})
            for d in range(1, 1 << count)
        ]

    def far_copy(u, k):
        return pltpu.make_async_remote_copy(
            src_ref=ins[u].at[lax.rem(chip + k, chips)],
            dst_ref=fars[u].at[k - 1],
            send_sem=far_send.at[u, k - 1],
            recv_sem=far_recv.at[u, k - 1],
            device_id={"shard": peer(k)},
            device_id_type=pl.DeviceIdType.MESH,
        )

    def spread_copy(u, at_level, link):
        d, slot, row, partner = link
        start, _ = held(u, at_level)
        size = held(u, at_level + 1)[1]
        index = flipped(level_index(u, at_level), d, levels(u)[at_level][1])
        return pltpu.make_async_remote_copy(
            src_ref=ins[u].at[chip, lines_of(start + index * size, size), :],
            dst_ref=halves[u].at[pl.ds(row, size), :],
            send_sem=half_send.at[u, slot],
            recv_sem=half_recv.at[u, slot],
            device_id=partner,
            device_id_type=pl.DeviceIdType.MESH,
        )

    def double_copy(u, b):
        slot = near_size - 1 + b - near
        size = works[u].shape[0] // near_size
        return pltpu.make_async_remote_copy(
            src_ref=ins[u].at[chip, own_piece(u), :],
            dst_ref=halves[u].at[pl.ds(slot * size, size), :],
            send_sem=half_send.at[u, slot],
            recv_sem=half_recv.at[u, slot],
            device_id={"rep": flipped(rep, 1 << b, bits)},
            device_id_type=pl.DeviceIdType.MESH,
        )

    def join_copy(u, at_level, link):
        d, slot, row, partner = link
        lines = lines_of(*held(u, at_level + 1))
        return pltpu.make_async_remote_copy(
            src_ref=works[u].at[lines, :],
            dst_ref=works[u].at[lines, :],
            send_sem=join_send.at[u, slot],
            recv_sem=join_recv.at[u, slot],
            device_id=partner,
            device_id_type=pl.DeviceIdType.MESH,
        )

    def level_start(u, at_level):
        for link in peers_of(u, at_level):
            spread_copy(u, at_level, link).start()

    def join_start(u, at_level):
        for link in peers_of(u, at_level):
            join_copy(u, at_level, link).start()

    def unit_stage(u, stage):
        if stage == 0:
            for j in range(chips):
                target = unit_out(u, j)
                for r0, nr, value in unit_pieces(u, 2 * j + 1 - core):
                    target[r0 : r0 + nr, :] = value().astype(bf16)
                core_copy(u, j).start()
            return
        if stage == 1:
            for j in range(chips):
                core_copy(u, j).wait()
            for k in range(1, chips + 1):
                j = lax.rem(chip + k, chips)
                for r0, nr, value in unit_pieces(u, 2 * j + core):
                    got = ins[u][j, r0 : r0 + nr, :].astype(f32)
                    ins[u][j, r0 : r0 + nr, :] = (value() + got).astype(bf16)
                if k == chips - 1:
                    for n in range(1, chips):
                        far_copy(u, n).start()
            return
        if stage == 2:
            for k in range(1, chips):
                far_copy(u, k).wait()
            total = ins[u][chip].astype(f32)
            for k in range(1, chips):
                total = total + fars[u][k - 1].astype(f32)
            ins[u][chip] = total.astype(bf16)
            level_start(u, 0)
            return
        count = len(levels(u))
        at_level = stage - 3
        if at_level < count:
            lines = lines_of(*held(u, at_level + 1))
            size = held(u, at_level + 1)[1]
            total = ins[u][chip, lines, :].astype(f32)
            for link in peers_of(u, at_level):
                spread_copy(u, at_level, link).wait()
                total = total + halves[u][link[2] : link[2] + size, :].astype(f32)
            if at_level + 1 < count:
                ins[u][chip, lines, :] = total.astype(bf16)
                level_start(u, at_level + 1)
            elif far_bits:
                ins[u][chip, lines, :] = total.astype(bf16)
                double_copy(u, far_bits[0]).start()
            else:
                works[u][lines, :] = total.astype(bf16)
                join_start(u, count - 1)
            return
        at_double = at_level - count
        if at_double < len(far_bits):
            b = far_bits[at_double]
            double_copy(u, b).wait()
            size = works[u].shape[0] // near_size
            row = (near_size - 1 + b - near) * size
            total = ins[u][chip, own_piece(u), :].astype(f32) + halves[u][
                row : row + size, :
            ].astype(f32)
            if b != far_bits[-1]:
                ins[u][chip, own_piece(u), :] = total.astype(bf16)
                double_copy(u, b + 1).start()
            else:
                works[u][own_piece(u), :] = total.astype(bf16)
                join_start(u, count - 1)
            return
        at_join = count - 1 - (at_double - len(far_bits))
        if at_join >= 0:
            for link in peers_of(u, at_join):
                join_copy(u, at_join, link).wait()
            if at_join > 0:
                join_start(u, at_join - 1)

    stages = 7 + len(far_bits)

    total_steps = 2 + len(far_bits)

    def total_copies(part, step):
        first, last = part
        if step == 0:
            links = [(d - 1, {"shard": flipped(me, d, shard_span)}) for d in range(1, shards)]
        elif step == 1:
            links = [
                (shards + d - 2, {"rep": flipped(rep, d, near)}) for d in range(1, near_size)
            ]
        else:
            b = far_bits[step - 2]
            links = [(shards + near_size + step - 4, {"rep": flipped(rep, 1 << b, bits)})]
        which = 0 if first == 0 else 1
        return [
            (
                at_slot,
                pltpu.make_async_remote_copy(
                    src_ref=total_ref.at[first:last],
                    dst_ref=total_in_ref.at[at_slot, first:last],
                    send_sem=total_send.at[which, at_slot],
                    recv_sem=total_recv.at[which, at_slot],
                    device_id=target,
                    device_id_type=pl.DeviceIdType.MESH,
                ),
            )
            for at_slot, target in links
        ]

    def total_start(part, step):
        for _, copy in total_copies(part, step):
            copy.start()

    def total_finish(part, step):
        first, last = part
        values = [total_ref[first:last]]
        for at_slot, copy in total_copies(part, step):
            copy.wait()
            values.append(total_in_ref[at_slot, first:last])
        while len(values) > 1:
            values = [values[i] + values[i + 1] for i in range(0, len(values), 2)]
        total_ref[first:last] = values[0]
        if step + 1 < total_steps:
            total_start(part, step + 1)

    small_ref[...] = jnp.zeros(small_ref.shape, f32)
    dbias_ref[...] = jnp.zeros(dbias_ref.shape, f32)
    sat_ref[width:, :] = (
        lax.broadcasted_iota(jnp.int32, (16, rows), 0) == 0
    ).astype(f32).astype(bf16)

    @pl.loop(0, width // 32)
    def _(n):
        lines = pl.ds(pl.multiple_of(n * 32, 32), 32)
        dwqkv_ref[lines, :] = jnp.zeros((32, 3 * width), f32)
        dwproj_ref[lines, :] = jnp.zeros((32, width), f32)
        dw1_ref[lines, :] = jnp.zeros((32, hidden), f32)
        dw2t_ref[lines, :] = jnp.zeros((32, hidden), f32)

    @pl.loop(0, rows_w // 64)
    def _(n):
        start = pl.multiple_of(n * 64, 64)
        to = lax.broadcasted_iota(jnp.int32, (64, rows8), 0) + start
        source = lax.broadcasted_iota(jnp.int32, (64, rows8), 1)
        hit = (to // pad == source % sub) & (to % pad == source // sub)
        perm_ref[pl.ds(start, 64), :] = hit.astype(f32).astype(bf16)

    @pl.loop(0, rows8 // 56)
    def _(n):
        start = pl.multiple_of(n * 56, 8)
        to = lax.broadcasted_iota(jnp.int32, (56, rows_w), 0) + start
        source = lax.broadcasted_iota(jnp.int32, (56, rows_w), 1)
        hit = (source // pad == to % sub) & (source % pad == to // sub)
        back_ref[pl.ds(start, 56), :] = hit.astype(f32).astype(bf16)

    table_tall = heads // 2
    table_rows = table_ref.shape[1]
    table_lanes = -(-table_rows // 128) * 128
    row_iota = lax.broadcasted_iota(jnp.int32, (table_lanes, 128), 0).astype(f32)
    low_lanes = lax.broadcasted_iota(jnp.int32, (key_rows, 128), 1) < pad
    rows_ref[...] = jnp.zeros(rows_ref.shape, f32)
    rows_ref[:, 0:table_rows] = table_ref[...]
    names_ref[...] = jnp.full(names_ref.shape, -1.0, f32)
    names_ref[0:tokens, 0:tokens] = index_ref[...].astype(f32)
    names_ref[...] = names_ref[...].T

    def named(j):
        return (row_iota == names_ref[pl.ds(j, 1), :]).astype(f32).astype(bf16)

    table = rows_ref[...]
    high = table.astype(bf16)
    middle = (table - high.astype(f32)).astype(bf16)
    low = (table - high.astype(f32) - middle.astype(f32)).astype(bf16)
    plane_ref[...] = jnp.full(plane_ref.shape, -1e30, f32)

    def plane(h):
        return plane_ref.at[h * key_rows : (h + 1) * key_rows, :]

    @pl.loop(0, tokens)
    def _(j):
        hit = named(j)
        line = (dot_nn(high, hit) + dot_nn(middle, hit)) + dot_nn(low, hit)
        plane_ref[pl.ds(j, heads, stride=key_rows), :] = line

    for t in range(quads):
        for h in range(quad // 2):
            left = plane(t * quad + 2 * h)[...]
            right = plane(t * quad + 2 * h + 1)[...]
            bias_ref[t, :, 128 * h : 128 * (h + 1)] = jnp.where(
                low_lanes, left, pltpu.roll(right, pad, 1)
            )

    def stacked(tile):
        return jnp.concatenate([tile * m for m in head_masks_half], axis=0)

    def diagonal(tall):
        total = tall[0:pad]
        for h in range(1, quad):
            total = jnp.where(head_masks[h], tall[h * pad : (h + 1) * pad], total)
        return total

    def grow(values):
        return jnp.concatenate([values, jnp.zeros((pad - key_rows, values.shape[1]), f32)], axis=0)

    @pl.loop(0, groups)
    def _(g):
        slot = lax.rem(g, 2)
        load(x_hbm, g, slot).wait()
        load(x_hbm, lax.rem(g + 1, groups), 1 - slot).start()

        @pl.when(g == groups - 1)
        def _():
            gather_relay(0)

        @pl.loop(0, tokens // step)
        def _(n):
            part = in_ref[slot, pl.ds(n * step, step)].astype(f32)
            flat = part.reshape(step * group, width)
            normal, _ = norm_parts(flat)
            wide_ref[pl.ds(n * step, step)] = (normal * gain1_ref[...] + shift1_ref[...]).reshape(
                step, group, width
            )

        for s in range(2):
            act8 = wide_ref[:, sub * s : sub * (s + 1), :].reshape(rows8, width).astype(bf16)

            @pl.when(g != 0)
            def _():
                act_w_store(2 * g - 2 + s, s).wait()

            act_w_ref[s] = dot_nn(perm_ref[...], act8).astype(bf16)
            act_w_store(2 * g + s, s).start()

    for s in range(2):
        act_w_store(2 * groups - 2 + s, s).wait()
    act_w_load(0, 0).start()
    gather_relay(1)
    for i in range(2, 5):
        gather_start(i)
    for i in range(2):
        gather_finish(i)

    @pl.loop(0, groups)
    def _(g):
        win0 = pl.multiple_of(g * group, group)
        slot = lax.rem(groups + g, 2)
        load(x_hbm, g, slot).wait()

        @pl.when(g < groups - 1)
        def _():
            load(x_hbm, g + 1, 1 - slot).start()

        @pl.when(g == groups - 1)
        def _():
            load(dy_hbm, 0, 1 - slot).start()
            gather_relay(3)

        @pl.loop(0, 2)
        def _(s):
            g2 = g * 2 + s
            act_w_load(g2, s).wait()

            @pl.when(g2 < 2 * groups - 1)
            def _():
                act_w_load(g2 + 1, 1 - s).start()

            for n in range(3):
                cols = slice(n * width, (n + 1) * width)
                out = dot_nn(act_w_ref[s], wqkv_ref[:, cols])
                if n == 0:
                    out = (out + query_bias_ref[...]) * scale
                if n == 2:
                    out = out + value_bias_ref[...]
                qkv_ref[g2, :, cols] = out.astype(bf16)

            @pl.loop(0, sub // 4)
            def _(wi):
                items = []
                for e in range(4):
                    w = wi * 4 + e
                    line = pl.ds(pl.multiple_of(w * pad, pad), pad)
                    items += [(w, line, t) for t in range(quads)]
                for first in range(0, len(items), 8):
                    batch = items[first : first + 8]
                    scores = [
                        dot_nt(
                            qkv_ref[g2, line, width + 128 * t : width + 128 * (t + 1)],
                            stacked(qkv_ref[g2, line, 128 * t : 128 * (t + 1)]),
                        )[0:key_rows]
                        + bias_ref[t]
                        for w, line, t in batch
                    ]
                    tops = [jnp.max(x, axis=0, keepdims=True) for x in scores]
                    weights = [jnp.exp(x - top) for x, top in zip(scores, tops)]
                    totals = [jnp.sum(x, axis=0, keepdims=True) for x in weights]
                    for (w, line, t), top, total in zip(batch, tops, totals):
                        lse_ref[g2, w, t : t + 1, :] = top + jnp.log(total)
                    probs = [
                        grow(x * (1.0 / total)).astype(bf16) for x, total in zip(weights, totals)
                    ]
                    mixes = [
                        dot_tn(
                            x, qkv_ref[g2, line, 2 * width + 128 * t : 2 * width + 128 * (t + 1)]
                        )
                        for x, (w, line, t) in zip(probs, batch)
                    ]
                    for x, (w, line, t) in zip(mixes, batch):
                        mixed_w_ref[line, 128 * t : 128 * (t + 1)] = diagonal(x).astype(bf16)

            wide_ref[:, pl.ds(pl.multiple_of(sub * s, sub), sub), :] = dot_nn(
                back_ref[...], mixed_w_ref[...]
            ).reshape(tokens, sub, width)

        @pl.when(g != 0)
        def _():
            store(mixed_ref, mixed_hbm, g - 1, mixed_sem).wait()

        @pl.when(g == 0)
        def _():
            gather_relay(2)
            gather_finish(2)

        @pl.when(g == groups - 1)
        def _():
            gather_relay(4)

        mixed_ref[...] = wide_ref[...].astype(bf16)
        store(mixed_ref, mixed_hbm, g, mixed_sem).start()
        out = dot_nn(mixed_ref[...].reshape(rows, width), wproj_ref[...]) + proj_bias_ref[...]
        dx_ref[:, pl.ds(win0, group), :] = in_ref[slot].astype(f32) + out.reshape(
            tokens, group, width
        )

    gather_finish(3)
    gather_finish(4)
    for i in range(5):
        gather_drain(i)
    store(mixed_ref, mixed_hbm, groups - 1, mixed_sem).wait()

    @pl.loop(0, groups)
    def _(g):
        win0 = pl.multiple_of(g * group, group)
        slot = lax.rem(2 * groups + g, 2)
        load(dy_hbm, g, slot).wait()

        @pl.when(g < groups - 1)
        def _():
            load(dy_hbm, g + 1, 1 - slot).start()

        @pl.when(g == groups - 1)
        def _():
            load(x_hbm, 0, 1 - slot).start()

        @pl.when(g != 0)
        def _():
            store(y_ref, y_hbm, g - 1, y_sem).wait()

        mixed_load(g).start()

        @pl.loop(0, tokens // step)
        def _(n):
            part = dx_ref[pl.ds(n * step, step), pl.ds(win0, group), :].reshape(step * group, width)
            normal, _ = norm_parts(part)
            lines = pl.ds(pl.multiple_of(n * step * group, step * group), step * group)
            sa_ref[lines, :] = (normal * gain2_ref[...] + shift2_ref[...]).astype(bf16)

        sat_ref[0:width, :] = sa_ref[...].T
        dyt_ref[...] = in_ref[slot].reshape(rows, width).T

        count = hidden // chunk
        columns = [slice(i * chunk, (i + 1) * chunk) for i in range(count)]

        def rise(i):
            u_ref[...] = dot_nn(sa_ref[...], w1_ref[:, columns[i]])
            da_ref[...] = dot_nt(in_ref[slot].reshape(rows, width), w2_ref[columns[i], :])

        def bend(i):
            for m in range(tokens // step):
                lines = slice(m * step * group, (m + 1) * step * group)
                value, slope = gelu_pair(u_ref[lines, :] + hidden_bias_ref[:, columns[i]])
                act_ref[lines, columns[i]] = value.astype(bf16)
                dup_ref[lines, columns[i]] = (da_ref[lines, :] * slope).astype(bf16)

        def gather_grads(i):
            cols = columns[i]
            part1 = dot_nn(sat_ref[...], dup_ref[:, cols])
            dw1_ref[:, cols] += part1[0:width]
            add_small("hb", part1[width : width + 8], cols.start)
            dw2t_ref[:, cols] += dot_nn(dyt_ref[...], act_ref[:, cols])

        rise(0)
        for i in range(count):
            bend(i)
            if i > 0:
                gather_grads(i - 1)
            if i + 1 < count:
                rise(i + 1)
        gather_grads(count - 1)

        @pl.when(g == groups - 1)
        def _():
            unit_stage(0, 0)

        out = dot_nn(act_ref[...], w2_ref[...]) + output_bias_ref[...]
        y_ref[...] = (
            dx_ref[:, pl.ds(win0, group), :] + out.reshape(tokens, group, width)
        ).astype(bf16)
        wide_ref[...] = dot_nt(dup_ref[...], w1_ref[...]).reshape(tokens, group, width)

        @pl.when(g == groups - 1)
        def _():
            unit_stage(1, 0)

        store(y_ref, y_hbm, g, y_sem).start()

        @pl.loop(0, tokens // step)
        def _(n):
            lines = pl.ds(pl.multiple_of(n * step * group, step * group), step * group)
            normal, inverse = norm_parts(
                dx_ref[pl.ds(n * step, step), pl.ds(win0, group), :].reshape(step * group, width)
            )
            grad = wide_ref[pl.ds(n * step, step)].reshape(step * group, width)
            scaled = grad * gain2_ref[...]
            back = inverse * (
                scaled
                - jnp.mean(scaled, axis=-1, keepdims=True)
                - normal * jnp.mean(scaled * normal, axis=-1, keepdims=True)
            )
            cot = in_ref[slot, pl.ds(n * step, step)].astype(f32).reshape(step * group, width)
            total = cot + back
            dx_ref[pl.ds(n * step, step), pl.ds(win0, group), :] = total.reshape(step, group, width)
            sa_ref[lines, :] = total.astype(bf16)
            add_small("ob", fold_rows(cot))
            add_small("pb", fold_rows(total))
            add_small("g2", fold_rows(grad * normal))
            add_small("s2", fold_rows(grad))

        @pl.when(g == groups - 1)
        def _():
            unit_stage(0, 1)

        mixed_load(g).wait()
        dwproj_ref[...] += dot_tn(mixed_ref[...].reshape(rows, width), sa_ref[...])

    store(y_ref, y_hbm, groups - 1, y_sem).wait()
    unit_stage(1, 1)
    unit_stage(2, 0)
    act_w_load(0, 0).start()

    plan = {
        0: ((2, 1),),
        3: ((0, 2),),
        4: ((1, 2),),
        5: ((2, 2),),
        6: ((0, 3),),
        7: ((1, 3),),
        8: ((2, 3),),
        9: ((0, 4),),
        11: ((1, 4), (2, 4)),
    }

    def progress(g2, half):
        for point, calls in plan.items():
            if point % 2 == half:

                @pl.when(g2 == point // 2)
                def _():
                    for u, stage in calls:
                        unit_stage(u, stage)

    subs = 2 * groups

    @pl.loop(0, subs)
    def _(g2):
        s = lax.rem(g2, 2)
        half8 = dx_ref[:, pl.ds(pl.multiple_of(g2 * sub, sub), sub), :]
        half_w = dot_nn(perm_ref[...], half8.reshape(rows8, width).astype(bf16)).astype(bf16)
        mixed_w_ref[...] = dot_nt(half_w, wproj_ref[...]).astype(bf16)
        progress(g2, 0)

        @pl.loop(0, sub // 2)
        def _(wi):
            items = []
            for e in range(2):
                w = wi * 2 + e
                line = pl.ds(pl.multiple_of(w * pad, pad), pad)
                for t in range(quads):
                    cols = [
                        slice(i * width + 128 * t, i * width + 128 * (t + 1)) for i in range(3)
                    ]
                    items.append((w, line, t, cols))
            for first in range(0, len(items), 8):
                batch = items[first : first + 8]
                queries = [stacked(qkv_ref[g2, line, c[0]]) for w, line, t, c in batch]
                scores = [
                    dot_nt(qkv_ref[g2, line, c[1]], x)[0:key_rows] + bias_ref[t]
                    for x, (w, line, t, c) in zip(queries, batch)
                ]
                grads = [stacked(mixed_w_ref[line, c[0]]) for w, line, t, c in batch]
                prob_grads = [
                    dot_nt(qkv_ref[g2, line, c[2]], x)[0:key_rows]
                    for x, (w, line, t, c) in zip(grads, batch)
                ]
                probs = [
                    jnp.exp(x - lse_ref[g2, w, t : t + 1, :])
                    for x, (w, line, t, c) in zip(scores, batch)
                ]
                prob_halves = [grow(x).astype(bf16) for x in probs]
                value_grads = [dot_nn(x, y) for x, y in zip(prob_halves, grads)]
                deltas = [
                    jnp.sum(x * y, axis=0, keepdims=True) for x, y in zip(probs, prob_grads)
                ]
                score_grads = [
                    x * (y - delta) for x, y, delta in zip(probs, prob_grads, deltas)
                ]
                for x, (w, line, t, c) in zip(score_grads, batch):
                    dbias_ref[t] += x
                halves_ = [grow(x).astype(bf16) for x in score_grads]
                key_grads = [dot_nn(x, y) for x, y in zip(halves_, queries)]
                query_grads = [
                    dot_tn(x, qkv_ref[g2, line, c[1]])
                    for x, (w, line, t, c) in zip(halves_, batch)
                ]
                for k, (w, line, t, c) in enumerate(batch):
                    qkv_ref[g2, line, c[0]] = (diagonal(query_grads[k]) * scale).astype(bf16)
                    qkv_ref[g2, line, c[1]] = key_grads[k].astype(bf16)
                    qkv_ref[g2, line, c[2]] = value_grads[k].astype(bf16)

        progress(g2, 1)
        act_w_load(g2, s).wait()

        @pl.when(g2 < subs - 1)
        def _():
            act_w_load(g2 + 1, 1 - s).start()

        sat_ref[0:width, 0:rows_w] = act_w_ref[s].T
        for n in range(3):
            cols = slice(n * width, (n + 1) * width)
            part = dot_nn(sat_ref[:, 0:rows_w], qkv_ref[g2, :, cols])
            dwqkv_ref[:, cols] += part[0:width]
            if n == 0:
                add_small("qb", part[width : width + 8])
            if n == 2:
                add_small("vb", part[width : width + 8])

            @pl.when(g2 == subs - 1)
            def _():
                unit_stage(3 + n, 0)
                if n == 2:
                    unit_stage(3, 1)

    for t in range(quads):
        for h in range(quad // 2):
            both = dbias_ref[t, :, 128 * h : 128 * (h + 1)]
            plane(t * quad + 2 * h)[...] = jnp.where(low_lanes, both, 0.0)
            plane(t * quad + 2 * h + 1)[...] = jnp.where(
                low_lanes, pltpu.roll(both, pad, 1), 0.0
            )
    total_ref[...] = jnp.zeros(total_ref.shape, f32)

    @pl.loop(0, tokens)
    def _(j):
        hit = named(j)
        line = plane_ref[pl.ds(j, heads, stride=key_rows), :]
        upper_half = line.astype(bf16)
        lower_half = (line - upper_half.astype(f32)).astype(bf16)
        found = dot_nt(upper_half, hit) + dot_nt(lower_half, hit)
        for side in range(2):
            lanes = slice(side * table_lanes, (side + 1) * table_lanes)
            total_ref[0:table_tall, lanes] = (
                total_ref[0:table_tall, lanes] + found[side * table_tall : (side + 1) * table_tall]
            )

    for u in range(4, 6):
        unit_stage(u, 1)
    early = (0, table_tall + (small_ref.shape[1] - 4 * width) // width)
    late = (early[1], early[1] + 8)

    def put_sums(first, last):
        for i in range(first, last):
            total_ref[table_tall + i : table_tall + i + 1, :] = jnp.sum(
                small_ref[:, i * width : (i + 1) * width], axis=0, keepdims=True
            )

    put_sums(0, early[1] - table_tall)
    total_start(early, 0)
    plan2 = {
        0: ((0, 5),),
        1: ((3, 2),),
        2: ((1, 5), (4, 2), (-1, 0)),
        3: ((5, 2),),
        4: ((0, 6),),
        5: ((3, 3),),
    }

    @pl.loop(0, groups)
    def _(g):
        win0 = pl.multiple_of(g * group, group)
        slot = lax.rem(3 * groups + g, 2)
        load(x_hbm, g, slot).wait()

        @pl.when(g < groups - 1)
        def _():
            load(x_hbm, g + 1, 1 - slot).start()

        for s in range(2):
            g2 = g * 2 + s
            mixed_w_ref[...] = dot_nt(qkv_ref[g2], wqkv_ref[...]).astype(bf16)
            wide_ref[:, sub * s : sub * (s + 1), :] = dot_nn(back_ref[...], mixed_w_ref[...]).reshape(
                tokens, sub, width
            )
            for point, calls in plan2.items():
                if point % 2 == s:

                    @pl.when(g == point // 2)
                    def _():
                        for u, stage in calls:
                            if u < 0:
                                total_finish(early, stage)
                            else:
                                unit_stage(u, stage)

        @pl.loop(0, tokens // step)
        def _(n):
            part = in_ref[slot, pl.ds(n * step, step)].astype(f32)
            normal, inverse = norm_parts(part.reshape(step * group, width))
            grad = wide_ref[pl.ds(n * step, step)].reshape(step * group, width)
            scaled = grad * gain1_ref[...]
            back = inverse * (
                scaled
                - jnp.mean(scaled, axis=-1, keepdims=True)
                - normal * jnp.mean(scaled * normal, axis=-1, keepdims=True)
            )
            dx_ref[pl.ds(n * step, step), pl.ds(win0, group), :] += back.reshape(step, group, width)
            add_small("g1", fold_rows(grad * normal))
            add_small("s1", fold_rows(grad))

        @pl.when(g != 0)
        def _():
            store(y_ref, dx_hbm, g - 1, dx_sem).wait()

        y_ref[...] = dx_ref[:, pl.ds(win0, group), :].astype(bf16)
        store(y_ref, dx_hbm, g, dx_sem).start()

    put_sums(early[1] - table_tall, small_ref.shape[1] // width)
    total_start(late, 0)
    done = {0: 6, 1: 5, 2: 4, 3: 3, 4: 2, 5: 2}
    for stage in range(2, stages):
        for u in range(6):
            if stage > done[u]:
                unit_stage(u, stage)
        if stage == 3:
            total_finish(late, 0)
            total_finish(early, 1)
    for step_at in range(1, total_steps):
        total_finish(late, step_at)
        if step_at > 1:
            total_finish(early, step_at)
    store(y_ref, dx_hbm, groups - 1, dx_sem).wait()


def local_pass(x, dy, wqkv, wproj, w1, w2, vectors, table, index, shards, reps):
    tokens, windows, width = x.shape
    hidden = w1.shape[1]
    heads = table.shape[0]
    dims = (tokens, windows, width, heads, hidden, shards, reps)
    chips = shards // 2
    bits = reps.bit_length() - 1
    sub = 8
    group = 2 * sub
    pad = 64
    rows = tokens * group
    small_size = 8 * width + hidden
    subs = windows // sub
    owned = width // shards
    unit_rows = (hidden // shards, hidden // shards, owned, owned, owned, owned)
    near_size = 1 << min(bits, 3)
    slots = near_size - 1 + bits - min(bits, 3)
    total_rows = heads // 2 + small_size // width + 4
    shapes = (
        [
            jax.ShapeDtypeStruct(x.shape, bf16),
            jax.ShapeDtypeStruct(x.shape, bf16),
            jax.ShapeDtypeStruct(x.shape, bf16),
            jax.ShapeDtypeStruct((subs, sub * pad, width), bf16),
        ]
        + [jax.ShapeDtypeStruct((r, width), bf16) for r in unit_rows]
        + [jax.ShapeDtypeStruct((total_rows, width), f32)]
    )
    vmem = pl.BlockSpec(memory_space=pltpu.VMEM)
    hbm = pl.BlockSpec(memory_space=pl.ANY)

    return pl.pallas_call(
        functools.partial(compute_kernel, dims),
        out_shape=shapes,
        in_specs=[hbm] * 6 + [vmem] * 11,
        out_specs=[hbm] * 4 + [vmem] * 7,
        scratch_shapes=[
            pltpu.VMEM((2, tokens, group, width), bf16),
            pltpu.VMEM((tokens, group, width), bf16),
            pltpu.VMEM(x.shape, f32),
            pltpu.VMEM((width, 3 * width), f32),
            pltpu.VMEM((width, width), f32),
            pltpu.VMEM((width, hidden), f32),
            pltpu.VMEM((width, hidden), f32),
            pltpu.VMEM((8, small_size), f32),
            pltpu.VMEM((heads // 4, 56, 256), f32),
            pltpu.VMEM((heads // 4, 56, 256), f32),
            pltpu.VMEM((sub * pad, tokens * sub), bf16),
            pltpu.VMEM((tokens * sub, sub * pad), bf16),
            pltpu.VMEM((2, sub * pad, width), bf16),
            pltpu.VMEM((subs, sub * pad, 3 * width), bf16),
            pltpu.VMEM((sub * pad, width), bf16),
            pltpu.VMEM((tokens, group, width), bf16),
            pltpu.VMEM((subs, sub, heads // 4, 256), f32),
            pltpu.VMEM((tokens, group, width), f32),
            pltpu.VMEM((rows, width), bf16),
            pltpu.VMEM((width + 16, rows), bf16),
            pltpu.VMEM((width, rows), bf16),
            pltpu.VMEM((rows, width), f32),
            pltpu.VMEM((rows, width), f32),
            pltpu.VMEM((heads * 56, 128), f32),
            pltpu.VMEM((128, 128), f32),
            pltpu.VMEM((heads, -(-table.shape[1] // 128) * 128), f32),
            pltpu.VMEM((rows, hidden), bf16),
            pltpu.VMEM((rows, hidden), bf16),
            pltpu.VMEM((width, 3 * width), bf16),
            pltpu.VMEM((width, width), bf16),
            pltpu.VMEM((width, hidden), bf16),
            pltpu.VMEM((hidden, width), bf16),
            pltpu.VMEM((chips - 1, unit_rows[0], width), bf16),
            *[pltpu.VMEM((chips, r, width), bf16) for r in unit_rows],
            *[pltpu.VMEM((chips - 1, r, width), bf16) for r in unit_rows],
            *[pltpu.VMEM((slots * r // near_size, width), bf16) for r in unit_rows],
            pltpu.VMEM((shards - 1 + slots, total_rows, width), f32),
            pltpu.SemaphoreType.DMA((5,)),
            pltpu.SemaphoreType.DMA((5, chips)),
            pltpu.SemaphoreType.DMA((5, chips)),
            pltpu.SemaphoreType.DMA((5, chips - 1)),
            pltpu.SemaphoreType.DMA((5, chips - 1)),
            pltpu.SemaphoreType.DMA((2,)),
            pltpu.SemaphoreType.DMA,
            pltpu.SemaphoreType.DMA,
            pltpu.SemaphoreType.DMA((2,)),
            pltpu.SemaphoreType.DMA,
            pltpu.SemaphoreType.DMA((6, chips)),
            pltpu.SemaphoreType.DMA((6, chips)),
            pltpu.SemaphoreType.DMA((6, chips - 1)),
            pltpu.SemaphoreType.DMA((6, chips - 1)),
            pltpu.SemaphoreType.DMA((6, slots)),
            pltpu.SemaphoreType.DMA((6, slots)),
            pltpu.SemaphoreType.DMA((6, slots)),
            pltpu.SemaphoreType.DMA((6, slots)),
            pltpu.SemaphoreType.DMA((2, shards - 1 + slots)),
            pltpu.SemaphoreType.DMA((2, shards - 1 + slots)),
        ],
        compiler_params=pltpu.CompilerParams(
            vmem_limit_bytes=67043328, collective_id=0, has_side_effects=True
        ),
    )(x, dy, wqkv, wproj, w1, w2, *vectors, table, index)


def spread_kernel(heads, sizes, *refs):
    works = refs[:6]
    total_ref = refs[6]
    dwqkv_ref, dwproj_ref, dw1_ref, dw2_ref, table_ref = refs[7:12]
    width = dwproj_ref.shape[1]
    owned = dwproj_ref.shape[0]
    for i in range(dw1_ref.shape[1] // width):
        dw1_ref[:, i * width : (i + 1) * width] = works[0][i * owned : (i + 1) * owned, :].astype(f32)
    dw2_ref[...] = works[1][...].astype(f32)
    dwproj_ref[...] = works[2][...].astype(f32)
    for i in range(3):
        dwqkv_ref[:, i * width : (i + 1) * width] = works[3 + i][...].astype(f32)
    tall = heads // 2
    rows_t = table_ref.shape[1]
    lanes = total_ref.shape[1] // 2
    table_ref[0:tall, :] = total_ref[0:tall, 0:rows_t]
    table_ref[tall:heads, :] = total_ref[0:tall, lanes : lanes + rows_t]
    row = tall
    for ref, size in zip(refs[12:], sizes):
        for i in range(size // width):
            ref[:, i * width : (i + 1) * width] = total_ref[row : row + 1, :]
            row += 1


def spread(works, total, width, hidden, heads, table_rows):
    owned = works[2].shape[0]
    sizes = (width, width, width, hidden, width, width, width, width, width)
    shapes = [
        (owned, 3 * width),
        (owned, width),
        (owned, hidden),
        works[1].shape,
        (heads, table_rows),
    ] + [(1, size) for size in sizes]
    vmem = pl.BlockSpec(memory_space=pltpu.VMEM)
    return pl.pallas_call(
        functools.partial(spread_kernel, heads, sizes),
        out_shape=[jax.ShapeDtypeStruct(shape, f32) for shape in shapes],
        in_specs=[vmem] * 7,
        out_specs=[vmem] * len(shapes),
    )(*works, total)


def on_device(
    shards,
    reps,
    block_input,
    out_grad,
    qkv_weight,
    query_bias,
    value_bias,
    proj_weight,
    proj_bias,
    hidden_weight,
    hidden_bias,
    output_weight,
    output_bias,
    first_gain,
    first_shift,
    second_gain,
    second_shift,
    bias_table,
    table_index,
):
    windows, tokens, width = block_input.shape
    table_rows, heads = bias_table.shape
    hidden = hidden_bias.shape[0]
    vectors = [
        v.reshape(1, -1)
        for v in (
            query_bias,
            value_bias,
            proj_bias,
            hidden_bias,
            output_bias,
            first_gain,
            first_shift,
            second_gain,
            second_shift,
        )
    ]
    y, dx, _, _, *works, total = local_pass(
        jnp.transpose(block_input, (1, 0, 2)),
        jnp.transpose(out_grad, (1, 0, 2)),
        qkv_weight,
        proj_weight,
        hidden_weight,
        output_weight,
        vectors,
        bias_table.T,
        table_index,
        shards,
        reps,
    )
    (dwqkv, dwproj, dw1, dw2, table_grad, qb, vb, pb, hb, ob, g1, s1, g2, s2) = spread(
        works, total, width, hidden, heads, table_rows
    )
    return (
        jnp.transpose(y, (1, 0, 2)),
        jnp.transpose(dx, (1, 0, 2)).astype(f32),
        dwqkv,
        qb.reshape(-1),
        vb.reshape(-1),
        dwproj,
        pb.reshape(-1),
        dw1,
        hb.reshape(-1),
        dw2,
        ob.reshape(-1),
        g1.reshape(-1),
        s1.reshape(-1),
        g2.reshape(-1),
        s2.reshape(-1),
        table_grad.T,
    )


def solution(mesh):
    rows = P(("shard", "rep"), None, None)
    cut = P("shard", None)
    full = P()
    return jax.shard_map(
        functools.partial(on_device, mesh.shape["shard"], mesh.shape["rep"]),
        mesh=mesh,
        in_specs=(
            rows,
            rows,
            cut,
            full,
            full,
            cut,
            full,
            cut,
            full,
            cut,
            full,
            full,
            full,
            full,
            full,
            full,
            full,
        ),
        out_specs=(
            rows,
            rows,
            cut,
            full,
            full,
            cut,
            full,
            cut,
            full,
            cut,
            full,
            full,
            full,
            full,
            full,
            full,
        ),
        check_vma=False,
    )
```

time: 309 us -> 212 us (0.69)
  Pallas kernels: 284 us -> 205 us
  local copies, waits for them, and re-layouts: 20.2 us -> 1.43 us
    pallas_call x1, Pallas kernels: 284 us -> 202 us  [local_pass(): pl.pallas_call(functools.partial(compute_kernel, dims), out_shape=shapes,...]
    unnamed x8 -> x3, local copies, waits for them, and re-layouts: 10.2 us -> 1.43 us
    convert_element_type x3 -> x0, local copies, waits for them, and re-layouts: 3.78 us -> none  [the longest x2 2.62 us: on_device(): dw1.astype(f32)]
    pallas_call x0 -> x1, Pallas kernels: none -> 3.13 us  [spread(): pl.pallas_call(functools.partial(spread_kernel, heads, sizes), out_shape=...]
where the time goes in v4:
time: 212 us
  Pallas kernels  205 us (97%)
  other arithmetic  4.73 us (2%)
    pallas_call x1, Pallas kernels, local_pass(): pl.pallas_call(functools.partial(compute_kernel, dims), out_shape=shapes,...  202 us
    convert_element_type x1, other arithmetic, on_device(): jnp.transpose(dx, (1, 0, 2)).astype(f32)  4.73 us

profile of v4, /device:TPU:0, one launch (start us, length us, event | category | flops | bytes accessed | tf_op | source)
XLA Modules:
  0.0 211.9 jit_solution(2071695355959602647)
XLA Ops:
  0.7 201.9 %shard_map.288 = (bf16[49,48,512]{2,1,0:T(8,128)(2,1)}, bf16[49,48,512]{2,1,0:T(8,128)(2,1)}, bf16[49,48,512]{2,1,0:T(8,128)(2,1)}, bf16[6,512,512]{2,1,0:T(8,12...) custom-call(bf16[49,48,512]{2,1,0:T(8,128)(2,1)} %bitcast.26, ...), custom_call_target="tpu_custom_call" | custom-call | tf_op jit(solution)/shard_map/pallas_call | solution.py:1132
  202.6 0.0 copy-start
  202.6 4.7 %convert_bitcast_fusion = f32[48,49,512]{2,0,1:T(8,128)} fusion(bf16[49,48,512]{2,1,0:T(8,128)(2,1)} %get-tuple-element.40), kind=kLoop, calls=%fused_computation | loop fusion | flops 1204224 | bytes 7225344 | tf_op jit(solution)/shard_map/convert_element_type | solution.py:1301
  207.3 3.1 %shard_map.289 = (f32[128,1536]{1,0:T(8,128)}, f32[128,512]{1,0:T(8,128)}, f32[128,2048]{1,0:T(8,128)}, f32[512,512]{1,0:T(8,128)}, f32[16,169]{1,0:T(8,128)}, /...) custom-call(bf16[512,512]{1,0:T(8,128)(2,1)} %get-tuple-element.41.r, ...), custom_call_target="tpu_custom_call" | custom-call | tf_op jit(solution)/shard_map/pallas_call | solution.py:1237
  210.5 0.0 copy-done
  210.5 1.4 copy.34
Async XLA Ops:
  202.6 7.9 %copy-start = (bf16[49,48,512]{2,1,0:T(8,128)(2,1)S(1)}, bf16[49,48,512]{2,1,0:T(8,128)(2,1)}, u32[]{:S(2)}) copy-start(bf16[49,48,512]{2,1,0:T(8,128)(2,1)} %get-tuple-element.39) | copy-start | bytes 7225348

commit v5 on v4

--- a/solution.py
+++ b/solution.py
@@ -64,6 +64,7 @@
     dx_hbm,
     mixed_hbm,
     act_w_hbm,
+    normal_w_hbm,
     work0_ref,
     work1_ref,
     work2_ref,
@@ -84,6 +85,7 @@
     perm_ref,
     back_ref,
     act_w_ref,
+    column_ref,
     qkv_ref,
     mixed_w_ref,
     mixed_ref,
@@ -132,6 +134,7 @@
     y_sem,
     mixed_sem,
     act_w_sem,
+    normal_w_sem,
     dx_sem,
     core_send,
     core_recv,
@@ -305,6 +308,19 @@
     def act_w_load(g2, slot):
         return pltpu.make_async_copy(act_w_hbm.at[g2], act_w_ref.at[slot], act_w_sem.at[slot])
 
+    def normal_stage(slot):
+        return mixed_w_ref if slot == 0 else out0_ref.at[0]
+
+    def normal_w_store(g2, slot):
+        return pltpu.make_async_copy(
+            normal_stage(slot), normal_w_hbm.at[g2], normal_w_sem.at[slot]
+        )
+
+    def normal_w_load(g2, slot):
+        return pltpu.make_async_copy(
+            normal_w_hbm.at[g2], act_w_ref.at[slot], normal_w_sem.at[slot]
+        )
+
     load(x_hbm, 0, 0).start()
 
     owned = width // shards
@@ -328,7 +344,12 @@
             yield 0, owned, (lambda: dwproj_ref[own, :])
         else:
             cols = slice(width * (u - 3), width * (u - 2))
-            yield 0, owned, (lambda: dwqkv_ref[own, cols])
+            name = ("qb", "s1", "vb")[u - 3]
+            sums = small_ref[0:1, base[name][0] : base[name][0] + width]
+            yield 0, owned, (
+                lambda: dwqkv_ref[own, cols] * column_ref[0, own, 0:1]
+                + column_ref[1, own, 0:1] * sums
+            )
 
     def unit_out(u, j):
         rows_u = works[u].shape[0]
@@ -517,53 +538,65 @@
 
     stages = 7 + len(far_bits)
 
-    total_steps = 2 + len(far_bits)
-
-    def total_copies(part, step):
-        first, last = part
-        if step == 0:
-            links = [(d - 1, {"shard": flipped(me, d, shard_span)}) for d in range(1, shards)]
+    total_steps = 3 + len(far_bits)
+    share = total_ref.shape[0] // shards
+
+    def total_share(index):
+        return total_ref.at[pl.ds(pl.multiple_of(index * share, share), share), :]
+
+    def total_copies(step):
+        if step == 0 or step == total_steps - 1:
+            first = 0 if step == 0 else shards - 2 + near_size + len(far_bits)
+            links = [
+                (first + d - 1, flipped(me, d, shard_span), {"shard": flipped(me, d, shard_span)})
+                for d in range(1, shards)
+            ]
         elif step == 1:
             links = [
-                (shards + d - 2, {"rep": flipped(rep, d, near)}) for d in range(1, near_size)
+                (shards + d - 2, me, {"rep": flipped(rep, d, near)}) for d in range(1, near_size)
             ]
         else:
             b = far_bits[step - 2]
-            links = [(shards + near_size + step - 4, {"rep": flipped(rep, 1 << b, bits)})]
-        which = 0 if first == 0 else 1
+            links = [(shards + near_size + step - 4, me, {"rep": flipped(rep, 1 << b, bits)})]
         return [
             (
                 at_slot,
+                other,
                 pltpu.make_async_remote_copy(
-                    src_ref=total_ref.at[first:last],
-                    dst_ref=total_in_ref.at[at_slot, first:last],
-                    send_sem=total_send.at[which, at_slot],
-                    recv_sem=total_recv.at[which, at_slot],
+                    src_ref=total_share(other if step == 0 else me),
+                    dst_ref=total_in_ref.at[at_slot],
+                    send_sem=total_send.at[at_slot],
+                    recv_sem=total_recv.at[at_slot],
                     device_id=target,
                     device_id_type=pl.DeviceIdType.MESH,
                 ),
             )
-            for at_slot, target in links
+            for at_slot, other, target in links
         ]
 
-    def total_start(part, step):
-        for _, copy in total_copies(part, step):
+    def total_start(step):
+        for _, _, copy in total_copies(step):
             copy.start()
 
-    def total_finish(part, step):
-        first, last = part
-        values = [total_ref[first:last]]
-        for at_slot, copy in total_copies(part, step):
+    def total_finish(step):
+        if step == total_steps - 1:
+            for at_slot, other, copy in total_copies(step):
+                copy.wait()
+                total_share(other)[...] = total_in_ref[at_slot]
+            return
+        values = [total_share(me)[...]]
+        for at_slot, _, copy in total_copies(step):
             copy.wait()
-            values.append(total_in_ref[at_slot, first:last])
+            values.append(total_in_ref[at_slot])
         while len(values) > 1:
             values = [values[i] + values[i + 1] for i in range(0, len(values), 2)]
-        total_ref[first:last] = values[0]
-        if step + 1 < total_steps:
-            total_start(part, step + 1)
+        total_share(me)[...] = values[0]
+        total_start(step + 1)
 
     small_ref[...] = jnp.zeros(small_ref.shape, f32)
     dbias_ref[...] = jnp.zeros(dbias_ref.shape, f32)
+    for i, ref in enumerate((gain1_ref, shift1_ref)):
+        column_ref[i] = jnp.broadcast_to(ref[...], (128, width)).T
     sat_ref[width:, :] = (
         lax.broadcasted_iota(jnp.int32, (16, rows), 0) == 0
     ).astype(f32).astype(bf16)
@@ -659,6 +692,8 @@
             wide_ref[pl.ds(n * step, step)] = (normal * gain1_ref[...] + shift1_ref[...]).reshape(
                 step, group, width
             )
+            lines = pl.ds(pl.multiple_of(n * step * group, step * group), step * group)
+            u_ref[lines, :] = normal
 
         for s in range(2):
             act8 = wide_ref[:, sub * s : sub * (s + 1), :].reshape(rows8, width).astype(bf16)
@@ -666,12 +701,19 @@
             @pl.when(g != 0)
             def _():
                 act_w_store(2 * g - 2 + s, s).wait()
+                normal_w_store(2 * g - 2 + s, s).wait()
 
             act_w_ref[s] = dot_nn(perm_ref[...], act8).astype(bf16)
             act_w_store(2 * g + s, s).start()
+            normal8 = u_ref[...].reshape(tokens, group, width)[:, sub * s : sub * (s + 1), :]
+            normal_stage(s)[...] = dot_nn(
+                perm_ref[...], normal8.reshape(rows8, width).astype(bf16)
+            ).astype(bf16)
+            normal_w_store(2 * g + s, s).start()
 
     for s in range(2):
         act_w_store(2 * groups - 2 + s, s).wait()
+        normal_w_store(2 * groups - 2 + s, s).wait()
     act_w_load(0, 0).start()
     gather_relay(1)
     for i in range(2, 5):
@@ -884,19 +926,9 @@
     store(y_ref, y_hbm, groups - 1, y_sem).wait()
     unit_stage(1, 1)
     unit_stage(2, 0)
-    act_w_load(0, 0).start()
-
-    plan = {
-        0: ((2, 1),),
-        3: ((0, 2),),
-        4: ((1, 2),),
-        5: ((2, 2),),
-        6: ((0, 3),),
-        7: ((1, 3),),
-        8: ((2, 3),),
-        9: ((0, 4),),
-        11: ((1, 4), (2, 4)),
-    }
+    normal_w_load(0, 0).start()
+
+    plan = {0: ((2, 1),), 5: ((0, 2),), 6: ((1, 2),), 7: ((2, 2),), 8: ((0, 3),), 9: ((1, 3),), 10: ((2, 3),), 11: ((0, 4),)}
 
     def progress(g2, half):
         for point, calls in plan.items():
@@ -966,21 +998,18 @@
                     qkv_ref[g2, line, c[2]] = value_grads[k].astype(bf16)
 
         progress(g2, 1)
-        act_w_load(g2, s).wait()
+        normal_w_load(g2, s).wait()
 
         @pl.when(g2 < subs - 1)
         def _():
-            act_w_load(g2 + 1, 1 - s).start()
+            normal_w_load(g2 + 1, 1 - s).start()
 
         sat_ref[0:width, 0:rows_w] = act_w_ref[s].T
         for n in range(3):
             cols = slice(n * width, (n + 1) * width)
             part = dot_nn(sat_ref[:, 0:rows_w], qkv_ref[g2, :, cols])
             dwqkv_ref[:, cols] += part[0:width]
-            if n == 0:
-                add_small("qb", part[width : width + 8])
-            if n == 2:
-                add_small("vb", part[width : width + 8])
+            add_small(("qb", "s1", "vb")[n], part[width : width + 8])
 
             @pl.when(g2 == subs - 1)
             def _():
@@ -1012,8 +1041,19 @@
 
     for u in range(4, 6):
         unit_stage(u, 1)
-    early = (0, table_tall + (small_ref.shape[1] - 4 * width) // width)
-    late = (early[1], early[1] + 8)
+    weighted = jnp.zeros((width, 128), f32)
+    for n in range(3 * width // 128):
+        lanes = slice(n * 128, (n + 1) * 128)
+        weighted = weighted + dwqkv_ref[:, lanes] * wqkv_ref[:, lanes].astype(f32)
+    add_small("g1", fold_rows(weighted.T))
+    merged_sums = jnp.concatenate(
+        [small_ref[:, base[n][0] : base[n][0] + width] for n in ("qb", "s1", "vb")], axis=1
+    )
+    sums_high = merged_sums.astype(bf16)
+    sums_low = (merged_sums - sums_high.astype(f32)).astype(bf16)
+    small_ref[:, base["s1"][0] : base["s1"][0] + width] = dot_nt(
+        sums_high, wqkv_ref[...]
+    ) + dot_nt(sums_low, wqkv_ref[...])
 
     def put_sums(first, last):
         for i in range(first, last):
@@ -1021,16 +1061,9 @@
                 small_ref[:, i * width : (i + 1) * width], axis=0, keepdims=True
             )
 
-    put_sums(0, early[1] - table_tall)
-    total_start(early, 0)
-    plan2 = {
-        0: ((0, 5),),
-        1: ((3, 2),),
-        2: ((1, 5), (4, 2), (-1, 0)),
-        3: ((5, 2),),
-        4: ((0, 6),),
-        5: ((3, 3),),
-    }
+    put_sums(0, small_ref.shape[1] // width)
+    total_start(0)
+    plan2 = {0: ((1, 4),), 1: ((3, 2), (2, 4), (-1, 0)), 2: ((0, 5), (4, 2)), 3: ((5, 2),), 4: ((1, 5), (-1, 1)), 5: ((3, 3),)}
 
     @pl.loop(0, groups)
     def _(g):
@@ -1055,7 +1088,7 @@
                     def _():
                         for u, stage in calls:
                             if u < 0:
-                                total_finish(early, stage)
+                                total_finish(stage)
                             else:
                                 unit_stage(u, stage)
 
@@ -1071,8 +1104,6 @@
                 - normal * jnp.mean(scaled * normal, axis=-1, keepdims=True)
             )
             dx_ref[pl.ds(n * step, step), pl.ds(win0, group), :] += back.reshape(step, group, width)
-            add_small("g1", fold_rows(grad * normal))
-            add_small("s1", fold_rows(grad))
 
         @pl.when(g != 0)
         def _():
@@ -1081,20 +1112,13 @@
         y_ref[...] = dx_ref[:, pl.ds(win0, group), :].astype(bf16)
         store(y_ref, dx_hbm, g, dx_sem).start()
 
-    put_sums(early[1] - table_tall, small_ref.shape[1] // width)
-    total_start(late, 0)
-    done = {0: 6, 1: 5, 2: 4, 3: 3, 4: 2, 5: 2}
+    done = {0: 5, 1: 5, 2: 4, 3: 3, 4: 2, 5: 2}
     for stage in range(2, stages):
-        for u in range(6):
+        for u in (3, 4, 5, 2, 0, 1):
             if stage > done[u]:
                 unit_stage(u, stage)
-        if stage == 3:
-            total_finish(late, 0)
-            total_finish(early, 1)
-    for step_at in range(1, total_steps):
-        total_finish(late, step_at)
-        if step_at > 1:
-            total_finish(early, step_at)
+    for step_at in range(2, total_steps):
+        total_finish(step_at)
     store(y_ref, dx_hbm, groups - 1, dx_sem).wait()
 
 
@@ -1115,12 +1139,13 @@
     unit_rows = (hidden // shards, hidden // shards, owned, owned, owned, owned)
     near_size = 1 << min(bits, 3)
     slots = near_size - 1 + bits - min(bits, 3)
-    total_rows = heads // 2 + small_size // width + 4
+    total_rows = -(-(heads // 2 + small_size // width) // (8 * shards)) * 8 * shards
     shapes = (
         [
             jax.ShapeDtypeStruct(x.shape, bf16),
             jax.ShapeDtypeStruct(x.shape, bf16),
             jax.ShapeDtypeStruct(x.shape, bf16),
+            jax.ShapeDtypeStruct((subs, sub * pad, width), bf16),
             jax.ShapeDtypeStruct((subs, sub * pad, width), bf16),
         ]
         + [jax.ShapeDtypeStruct((r, width), bf16) for r in unit_rows]
@@ -1133,7 +1158,7 @@
         functools.partial(compute_kernel, dims),
         out_shape=shapes,
         in_specs=[hbm] * 6 + [vmem] * 11,
-        out_specs=[hbm] * 4 + [vmem] * 7,
+        out_specs=[hbm] * 5 + [vmem] * 7,
         scratch_shapes=[
             pltpu.VMEM((2, tokens, group, width), bf16),
             pltpu.VMEM((tokens, group, width), bf16),
@@ -1148,6 +1173,7 @@
             pltpu.VMEM((sub * pad, tokens * sub), bf16),
             pltpu.VMEM((tokens * sub, sub * pad), bf16),
             pltpu.VMEM((2, sub * pad, width), bf16),
+            pltpu.VMEM((2, width, 128), f32),
             pltpu.VMEM((subs, sub * pad, 3 * width), bf16),
             pltpu.VMEM((sub * pad, width), bf16),
             pltpu.VMEM((tokens, group, width), bf16),
@@ -1171,7 +1197,7 @@
             *[pltpu.VMEM((chips, r, width), bf16) for r in unit_rows],
             *[pltpu.VMEM((chips - 1, r, width), bf16) for r in unit_rows],
             *[pltpu.VMEM((slots * r // near_size, width), bf16) for r in unit_rows],
-            pltpu.VMEM((shards - 1 + slots, total_rows, width), f32),
+            pltpu.VMEM((2 * shards - 2 + slots, total_rows // shards, width), f32),
             pltpu.SemaphoreType.DMA((5,)),
             pltpu.SemaphoreType.DMA((5, chips)),
             pltpu.SemaphoreType.DMA((5, chips)),
@@ -1180,6 +1206,7 @@
             pltpu.SemaphoreType.DMA((2,)),
             pltpu.SemaphoreType.DMA,
             pltpu.SemaphoreType.DMA,
+            pltpu.SemaphoreType.DMA((2,)),
             pltpu.SemaphoreType.DMA((2,)),
             pltpu.SemaphoreType.DMA,
             pltpu.SemaphoreType.DMA((6, chips)),
@@ -1190,8 +1217,8 @@
             pltpu.SemaphoreType.DMA((6, slots)),
             pltpu.SemaphoreType.DMA((6, slots)),
             pltpu.SemaphoreType.DMA((6, slots)),
-            pltpu.SemaphoreType.DMA((2, shards - 1 + slots)),
-            pltpu.SemaphoreType.DMA((2, shards - 1 + slots)),
+            pltpu.SemaphoreType.DMA((2 * shards - 2 + slots,)),
+            pltpu.SemaphoreType.DMA((2 * shards - 2 + slots,)),
         ],
         compiler_params=pltpu.CompilerParams(
             vmem_limit_bytes=67043328, collective_id=0, has_side_effects=True
@@ -1201,29 +1228,39 @@
 
 def spread_kernel(heads, sizes, *refs):
     works = refs[:6]
-    total_ref = refs[6]
-    dwqkv_ref, dwproj_ref, dw1_ref, dw2_ref, table_ref = refs[7:12]
+    total_ref, y_in, dx_in = refs[6:9]
+    dwqkv_ref, dwproj_ref, dw1_ref, dw2_ref, table_ref = refs[9:14]
+    sums = refs[14:-2]
+    y_ref, dx_ref = refs[-2:]
     width = dwproj_ref.shape[1]
     owned = dwproj_ref.shape[0]
-    for i in range(dw1_ref.shape[1] // width):
-        dw1_ref[:, i * width : (i + 1) * width] = works[0][i * owned : (i + 1) * owned, :].astype(f32)
-    dw2_ref[...] = works[1][...].astype(f32)
-    dwproj_ref[...] = works[2][...].astype(f32)
-    for i in range(3):
-        dwqkv_ref[:, i * width : (i + 1) * width] = works[3 + i][...].astype(f32)
-    tall = heads // 2
-    rows_t = table_ref.shape[1]
-    lanes = total_ref.shape[1] // 2
-    table_ref[0:tall, :] = total_ref[0:tall, 0:rows_t]
-    table_ref[tall:heads, :] = total_ref[0:tall, lanes : lanes + rows_t]
-    row = tall
-    for ref, size in zip(refs[12:], sizes):
-        for i in range(size // width):
-            ref[:, i * width : (i + 1) * width] = total_ref[row : row + 1, :]
-            row += 1
-
-
-def spread(works, total, width, hidden, heads, table_rows):
+    y_ref[...] = y_in[...]
+    dx_ref[...] = dx_in[...].astype(f32)
+
+    @pl.when(pl.program_id(0) == 0)
+    def _():
+        for i in range(dw1_ref.shape[1] // width):
+            dw1_ref[:, i * width : (i + 1) * width] = works[0][
+                i * owned : (i + 1) * owned, :
+            ].astype(f32)
+        dw2_ref[...] = works[1][...].astype(f32)
+        dwproj_ref[...] = works[2][...].astype(f32)
+        for i in range(3):
+            dwqkv_ref[:, i * width : (i + 1) * width] = works[3 + i][...].astype(f32)
+        tall = heads // 2
+        rows_t = table_ref.shape[1]
+        lanes = total_ref.shape[1] // 2
+        table_ref[0:tall, :] = total_ref[0:tall, 0:rows_t]
+        table_ref[tall:heads, :] = total_ref[0:tall, lanes : lanes + rows_t]
+        row = tall
+        for ref, size in zip(sums, sizes):
+            for i in range(size // width):
+                ref[:, i * width : (i + 1) * width] = total_ref[row : row + 1, :]
+                row += 1
+
+
+def spread(works, total, y, dx, hidden, heads, table_rows):
+    tokens, windows, width = y.shape
     owned = works[2].shape[0]
     sizes = (width, width, width, hidden, width, width, width, width, width)
     shapes = [
@@ -1233,13 +1270,17 @@
         works[1].shape,
         (heads, table_rows),
     ] + [(1, size) for size in sizes]
-    vmem = pl.BlockSpec(memory_space=pltpu.VMEM)
+    step = 7
+    slab = pl.BlockSpec((step, windows, width), lambda i: (i, 0, 0))
+    whole = lambda shape: pl.BlockSpec(shape, lambda i: (0, 0))
     return pl.pallas_call(
         functools.partial(spread_kernel, heads, sizes),
-        out_shape=[jax.ShapeDtypeStruct(shape, f32) for shape in shapes],
-        in_specs=[vmem] * 7,
-        out_specs=[vmem] * len(shapes),
-    )(*works, total)
+        grid=(tokens // step,),
+        out_shape=[jax.ShapeDtypeStruct(shape, f32) for shape in shapes]
+        + [jax.ShapeDtypeStruct(y.shape, bf16), jax.ShapeDtypeStruct(y.shape, f32)],
+        in_specs=[whole(w.shape) for w in works] + [whole(total.shape), slab, slab],
+        out_specs=[whole(shape) for shape in shapes] + [slab, slab],
+    )(*works, total, y, dx)
 
 
 def on_device(
@@ -1280,7 +1321,7 @@
             second_shift,
         )
     ]
-    y, dx, _, _, *works, total = local_pass(
+    y, dx, _, _, _, *works, total = local_pass(
         jnp.transpose(block_input, (1, 0, 2)),
         jnp.transpose(out_grad, (1, 0, 2)),
         qkv_weight,
@@ -1293,12 +1334,12 @@
         shards,
         reps,
     )
-    (dwqkv, dwproj, dw1, dw2, table_grad, qb, vb, pb, hb, ob, g1, s1, g2, s2) = spread(
-        works, total, width, hidden, heads, table_rows
+    (dwqkv, dwproj, dw1, dw2, table_grad, qb, vb, pb, hb, ob, g1, s1, g2, s2, y, dx) = spread(
+        works, total, y, dx, hidden, heads, table_rows
     )
     return (
         jnp.transpose(y, (1, 0, 2)),
-        jnp.transpose(dx, (1, 0, 2)).astype(f32),
+        jnp.transpose(dx, (1, 0, 2)),
         dwqkv,
         qb.reshape(-1),
         vb.reshape(-1),

time: 212 us -> 202 us (0.953)
  Pallas kernels: 205 us -> 200 us
  other arithmetic: 4.73 us -> 0 us
    pallas_call x1, Pallas kernels: 202 us -> 191 us  [local_pass(): pl.pallas_call(functools.partial(compute_kernel, dims), out_shape=shapes,...]
    pallas_call x1, Pallas kernels: 3.13 us -> 9.21 us  [spread(): pl.pallas_call(functools.partial(spread_kernel, heads, sizes), grid=(toke...]
    convert_element_type x1 -> x0, other arithmetic: 4.73 us -> none  [on_device(): jnp.transpose(dx, (1, 0, 2)).astype(f32)]
where the time goes in v5:
time: 202 us; the launch traced here: 201 us
  Pallas kernels  200 us (99%)
    pallas_call x1, Pallas kernels, local_pass(): pl.pallas_call(functools.partial(compute_kernel, dims), out_shape=shapes,...  191 us
    pallas_call x1, Pallas kernels, spread(): pl.pallas_call(functools.partial(spread_kernel, heads, sizes), grid=(toke...  9.21 us

profile of v5, /device:TPU:0, one launch (start us, length us, event | category | flops | bytes accessed | tf_op | source)
XLA Modules:
  0.0 201.2 jit_solution(12040022811140173827)
XLA Ops:
  0.7 191.1 %shard_map.288 = (bf16[49,48,512]{2,1,0:T(8,128)(2,1)}, bf16[49,48,512]{2,1,0:T(8,128)(2,1)}, bf16[49,48,512]{2,1,0:T(8,128)(2,1)}, bf16[6,512,512]{2,1,0:T(8,12...) custom-call(bf16[49,48,512]{2,1,0:T(8,128)(2,1)} %bitcast.24, ...), custom_call_target="tpu_custom_call" | custom-call | tf_op jit(solution)/shard_map/pallas_call | solution.py:1157
  191.8 9.2 %shard_map.289 = (f32[128,1536]{1,0:T(8,128)}, f32[128,512]{1,0:T(8,128)}, f32[128,2048]{1,0:T(8,128)}, f32[512,512]{1,0:T(8,128)}, f32[16,169]{1,0:T(8,128)}, /...) custom-call(bf16[512,512]{1,0:T(8,128)(2,1)} %get-tuple-element.41.r, ...), custom_call_target="tpu_custom_call" | custom-call | tf_op jit(solution)/shard_map/pallas_call | solution.py:1276

commit v6 on v5

--- a/solution.py
+++ b/solution.py
@@ -1270,7 +1270,7 @@
         works[1].shape,
         (heads, table_rows),
     ] + [(1, size) for size in sizes]
-    step = 7
+    step = tokens
     slab = pl.BlockSpec((step, windows, width), lambda i: (i, 0, 0))
     whole = lambda shape: pl.BlockSpec(shape, lambda i: (0, 0))
     return pl.pallas_call(

time: 202 us -> 199 us (0.985)
    pallas_call x1, Pallas kernels: 9.21 us -> 7.09 us  [spread(): pl.pallas_call(functools.partial(spread_kernel, heads, sizes), grid=(toke...]
where the time goes in v6:
time: 199 us
  Pallas kernels  198 us (99%)
    pallas_call x1, Pallas kernels, local_pass(): pl.pallas_call(functools.partial(compute_kernel, dims), out_shape=shapes,...  191 us
    pallas_call x1, Pallas kernels, spread(): pl.pallas_call(functools.partial(spread_kernel, heads, sizes), grid=(toke...  7.09 us

profile of v6, /device:TPU:0, one launch (start us, length us, event | category | flops | bytes accessed | tf_op | source)
XLA Modules:
  0.0 199.0 jit_solution(3279663105741587285)
XLA Ops:
  0.7 191.1 %shard_map.288 = (bf16[49,48,512]{2,1,0:T(8,128)(2,1)}, bf16[49,48,512]{2,1,0:T(8,128)(2,1)}, bf16[49,48,512]{2,1,0:T(8,128)(2,1)}, bf16[6,512,512]{2,1,0:T(8,12...) custom-call(bf16[49,48,512]{2,1,0:T(8,128)(2,1)} %bitcast.24, ...), custom_call_target="tpu_custom_call" | custom-call | tf_op jit(solution)/shard_map/pallas_call | solution.py:1157
  191.8 7.1 %shard_map.289 = (f32[128,1536]{1,0:T(8,128)}, f32[128,512]{1,0:T(8,128)}, f32[128,2048]{1,0:T(8,128)}, f32[512,512]{1,0:T(8,128)}, f32[16,169]{1,0:T(8,128)}, /...) custom-call(bf16[512,512]{1,0:T(8,128)(2,1)} %get-tuple-element.41.r, ...), custom_call_target="tpu_custom_call" | custom-call | tf_op jit(solution)/shard_map/pallas_call | solution.py:1276

commit v7 on v6

--- a/solution.py
+++ b/solution.py
@@ -911,10 +911,10 @@
             total = cot + back
             dx_ref[pl.ds(n * step, step), pl.ds(win0, group), :] = total.reshape(step, group, width)
             sa_ref[lines, :] = total.astype(bf16)
-            add_small("ob", fold_rows(cot))
-            add_small("pb", fold_rows(total))
-            add_small("g2", fold_rows(grad * normal))
-            add_small("s2", fold_rows(grad))
+            tip = lax.broadcasted_iota(jnp.int32, (16, step * group), 0) == 0
+            tip = tip.astype(f32).astype(bf16)
+            for name, value in (("ob", cot), ("pb", total), ("g2", grad * normal), ("s2", grad)):
+                add_small(name, dot_nn(tip, value.astype(bf16))[0:8])
 
         @pl.when(g == groups - 1)
         def _():

time: 199 us -> 203 us (1.020)
  Pallas kernels: 198 us -> 201 us
    pallas_call x1, Pallas kernels: 191 us -> 194 us  [local_pass(): pl.pallas_call(functools.partial(compute_kernel, dims), out_shape=shapes,...]
where the time goes in v7:
time: 203 us; the launch traced here: 202 us
  Pallas kernels  201 us (99%)
    pallas_call x1, Pallas kernels, local_pass(): pl.pallas_call(functools.partial(compute_kernel, dims), out_shape=shapes,...  194 us
    pallas_call x1, Pallas kernels, spread(): pl.pallas_call(functools.partial(spread_kernel, heads, sizes), grid=(toke...  7.09 us

profile of v7, /device:TPU:0, one launch (start us, length us, event | category | flops | bytes accessed | tf_op | source)
XLA Modules:
  0.0 202.3 jit_solution(9488976641311062377)
XLA Ops:
  0.7 194.4 %shard_map.288 = (bf16[49,48,512]{2,1,0:T(8,128)(2,1)}, bf16[49,48,512]{2,1,0:T(8,128)(2,1)}, bf16[49,48,512]{2,1,0:T(8,128)(2,1)}, bf16[6,512,512]{2,1,0:T(8,12...) custom-call(bf16[49,48,512]{2,1,0:T(8,128)(2,1)} %bitcast.24, ...), custom_call_target="tpu_custom_call" | custom-call | tf_op jit(solution)/shard_map/pallas_call | solution.py:1157
  195.1 7.1 %shard_map.289 = (f32[128,1536]{1,0:T(8,128)}, f32[128,512]{1,0:T(8,128)}, f32[128,2048]{1,0:T(8,128)}, f32[512,512]{1,0:T(8,128)}, f32[16,169]{1,0:T(8,128)}, /...) custom-call(bf16[512,512]{1,0:T(8,128)(2,1)} %get-tuple-element.41.r, ...), custom_call_target="tpu_custom_call" | custom-call | tf_op jit(solution)/shard_map/pallas_call | solution.py:1276
